TPU v7x, 32 devices: a whole 2x2x4 slice. The times are simulated.
32 devices in a mesh: fsdp: 8 (over z, x), tensor: 4 (over y, core).
Axes of the slice: x: 2, y: 2, z: 4, core: 2. Of those that a mesh axis runs over, the one named last changes fastest.
Arguments:
- layer_input: bfloat16 [8192, 2048], P('fsdp'), may hold values from -6 to 6
- out_grad: bfloat16 [8192, 2048], P('fsdp'), may hold values from -6 to 6
- segment_ids: int32 [8192], P('fsdp'), may hold values from 0 to 8191, as said below
- query_weight: float32 [2048, 2048], P('fsdp', 'tensor'), may hold values from -0.125 to 0.125
- key_weight: float32 [2048, 1024], P('fsdp', 'tensor'), may hold values from -0.125 to 0.125
- value_matrix: float32 [2048, 1024], P('fsdp', 'tensor'), may hold values from -0.125 to 0.125
- output_weight: float32 [2048, 2048], P('fsdp', 'tensor'), may hold values from -0.5 to 0.5
- gate_up_weight: float32 [2, 2048, 6144], P(None, 'fsdp', 'tensor'), may hold values from -0.125 to 0.125
- down_weight: float32 [2048, 6144], P('fsdp', 'tensor'), may hold values from -0.15625 to 0.15625
- norm_gains: float32 [2, 2048], P(None, 'fsdp'), may hold values from 0.5 to 1.5
- headnorm_gains: float32 [2, 128], P(None, 'fsdp'), may hold values from 0.5 to 1.5
- query_weight_mean: float32 [2048, 2048], P('fsdp', 'tensor'), may hold values from -112 to 112
- key_weight_first_moment: float32 [2048, 1024], P('fsdp', 'tensor'), may hold values from -128 to 128
- value_weight_first_moment: float32 [2048, 1024], P('fsdp', 'tensor'), may hold values from -256 to 256
- output_weight_mean: float32 [2048, 2048], P('fsdp', 'tensor'), may hold values from -24 to 24
- gate_up_weight_mean: float32 [2, 2048, 6144], P(None, 'fsdp', 'tensor'), may hold values from -40 to 40
- down_weight_mean: float32 [2048, 6144], P('fsdp', 'tensor'), may hold values from -32 to 32
- norm_gains_mean: float32 [2, 2048], P(None, 'fsdp'), may hold values from -128 to 128
- headnorm_gains_mean: float32 [2, 128], P(None, 'fsdp'), may hold values from -448 to 448
- query_weight_square: float32 [2048, 2048], P('fsdp', 'tensor'), may hold values from 401.408 to 4014.08
- key_weight_second_moment: float32 [2048, 1024], P('fsdp', 'tensor'), may hold values from 704.512 to 7045.12
- value_weight_second_moment: float32 [2048, 1024], P('fsdp', 'tensor'), may hold values from 1966.08 to 19660.8
- output_weight_square: float32 [2048, 2048], P('fsdp', 'tensor'), may hold values from 19.6608 to 196.608
- gate_up_weight_square: float32 [2, 2048, 6144], P(None, 'fsdp', 'tensor'), may hold values from 58.968 to 589.68
- down_weight_square: float32 [2048, 6144], P('fsdp', 'tensor'), may hold values from 44.2368 to 442.368
- norm_gains_square: float32 [2, 2048], P(None, 'fsdp'), may hold values from 491.52 to 4915.2
- headnorm_gains_square: float32 [2, 128], P(None, 'fsdp'), may hold values from 6422.528 to 64225.28
Outputs:
- layer_output: float32 [8192, 2048], P('fsdp')
- input_grad: float32 [8192, 2048], P('fsdp')
- query_weight_grad: float32 [2048, 2048], P('fsdp', 'tensor')
- key_weight_grad: float32 [2048, 1024], P('fsdp', 'tensor')
- value_weight_grad: float32 [2048, 1024], P('fsdp', 'tensor')
- output_weight_grad: float32 [2048, 2048], P('fsdp', 'tensor')
- gate_up_weight_grad: float32 [2, 2048, 6144], P(None, 'fsdp', 'tensor')
- down_weight_grad: float32 [2048, 6144], P('fsdp', 'tensor')
- norm_gains_grad: float32 [2, 2048], P(None, 'fsdp')
- headnorm_gains_grad: float32 [2, 128], P(None, 'fsdp')
- query_weight_step: float32 [2048, 2048], P('fsdp', 'tensor')
- key_weight_step: float32 [2048, 1024], P('fsdp', 'tensor')
- value_weight_step: float32 [2048, 1024], P('fsdp', 'tensor')
- output_weight_step: float32 [2048, 2048], P('fsdp', 'tensor')
- gate_up_weight_step: float32 [2, 2048, 6144], P(None, 'fsdp', 'tensor')
- down_weight_step: float32 [2048, 6144], P('fsdp', 'tensor')
- norm_gains_step: float32 [2, 2048], P(None, 'fsdp')
- headnorm_gains_step: float32 [2, 128], P(None, 'fsdp')
- query_weight_mean_next: float32 [2048, 2048], P('fsdp', 'tensor')
- key_weight_mean_next: float32 [2048, 1024], P('fsdp', 'tensor')
- value_weight_mean_next: float32 [2048, 1024], P('fsdp', 'tensor')
- output_weight_mean_next: float32 [2048, 2048], P('fsdp', 'tensor')
- gate_up_weight_mean_next: float32 [2, 2048, 6144], P(None, 'fsdp', 'tensor')
- down_weight_mean_next: float32 [2048, 6144], P('fsdp', 'tensor')
- norm_gains_mean_next: float32 [2, 2048], P(None, 'fsdp')
- headnorm_gains_mean_next: float32 [2, 128], P(None, 'fsdp')
- query_weight_square_next: float32 [2048, 2048], P('fsdp', 'tensor')
- key_weight_square_next: float32 [2048, 1024], P('fsdp', 'tensor')
- value_weight_square_next: float32 [2048, 1024], P('fsdp', 'tensor')
- output_weight_square_next: float32 [2048, 2048], P('fsdp', 'tensor')
- gate_up_weight_square_next: float32 [2, 2048, 6144], P(None, 'fsdp', 'tensor')
- down_weight_square_next: float32 [2048, 6144], P('fsdp', 'tensor')
- norm_gains_square_next: float32 [2, 2048], P(None, 'fsdp')
- headnorm_gains_square_next: float32 [2, 128], P(None, 'fsdp')
Inputs may be any that keep to these rules, and one draw needn't show every extreme that they name: `segment_ids`: segment ids never fall; the tokens of one segment lie within one aligned block of 1024 tokens; in at least one block a single segment fills all 1024 tokens.
All inputs are finite; a program needn't handle non-finite values.
Results may differ from a plain program's by a relative error of at most 0.015.
The roundings to bfloat16 on the way count: a program that leaves them out, or rounds other values in their place, can miss the bound.
Values may be sent and summed in bfloat16 or wider, within the bound.
A program may use at most 256 MiB of HBM per device.

v0:
```python
import math

import jax
import jax.numpy as jnp
from jax import lax
from jax.sharding import PartitionSpec as P

HEAD_SIZE = 128
ADAM_STEP = 3


EPSILON = 1e-06
ROPE_BASE = 1000000.0
MASKED = -1e30
BETA_ONE = 0.9
BETA_TWO = 0.95
ADAM_EPSILON = 1e-08
MATRIX_RATE = 0.02
GAIN_RATE = 0.1
WEIGHT_DECAY = 0.1


def root_mean_scale(values):
    return values * lax.rsqrt(jnp.mean(values * values, axis=-1, keepdims=True) + EPSILON)


def positions_of(segments):
    earlier = jnp.sum((segments[None, :] < segments[:, None]).astype(jnp.int32), axis=1)
    return jnp.arange(segments.shape[0], dtype=jnp.int32) - earlier


def rotary_embedding(values, token_positions):
    head_width = values.shape[-1]
    half_width = head_width // 2
    frequencies = ROPE_BASE ** (-2.0 * jnp.arange(half_width).astype(values.dtype) / head_width)
    angles = token_positions.astype(values.dtype)[:, None] * frequencies[None, :]
    cosine = jnp.cos(angles)[:, None, :]
    sine_part = jnp.sin(angles)[:, None, :]
    first_half = values[..., :half_width]
    second_half = values[..., half_width:]
    return jnp.concatenate(
        [
            first_half * cosine - second_half * sine_part,
            second_half * cosine + first_half * sine_part,
        ],
        axis=-1,
    )


def contract_rows(left, right):
    return lax.dot_general(
        left, right, (((0,), (0,)), ((), ())), preferred_element_type=jnp.float32
    )


def contract_cols(left, right):
    return lax.dot_general(
        left, right, (((1,), (1,)), ((), ())), preferred_element_type=jnp.float32
    )


def gained_norm(values, gain):
    return root_mean_scale(values) * gain


def swiglu(gate_proj, up_proj):
    return jax.nn.silu(gate_proj) * up_proj


def adam_step(weight, gradient, mean_state, square_state, learn_rate, decay_rate):
    mean_next = BETA_ONE * mean_state + (1.0 - BETA_ONE) * gradient
    square_next = BETA_TWO * square_state + (1.0 - BETA_TWO) * gradient * gradient
    mean_hat = mean_next / (1.0 - BETA_ONE**ADAM_STEP)
    square_hat = square_next / (1.0 - BETA_TWO**ADAM_STEP)
    weight_next = weight - learn_rate * (
        mean_hat / (jnp.sqrt(square_hat) + ADAM_EPSILON) + decay_rate * weight
    )
    return (weight_next - weight, mean_next, square_next)


def per_device(
    layer_input,
    out_grad,
    segment_ids,
    query_weight,
    key_weight,
    value_matrix,
    output_weight,
    gate_up_weight,
    down_weight,
    norm_gains,
    headnorm_gains,
    query_weight_mean,
    key_weight_first_moment,
    value_weight_first_moment,
    output_weight_mean,
    gate_up_weight_mean,
    down_weight_mean,
    norm_gains_mean,
    headnorm_gains_mean,
    query_weight_square,
    key_weight_second_moment,
    value_weight_second_moment,
    output_weight_square,
    gate_up_weight_square,
    down_weight_square,
    norm_gains_square,
    headnorm_gains_square,
):
    params = (
        query_weight,
        key_weight,
        value_matrix,
        output_weight,
        gate_up_weight,
        down_weight,
        norm_gains,
        headnorm_gains,
    )
    means = (
        query_weight_mean,
        key_weight_first_moment,
        value_weight_first_moment,
        output_weight_mean,
        gate_up_weight_mean,
        down_weight_mean,
        norm_gains_mean,
        headnorm_gains_mean,
    )
    squares = (
        query_weight_square,
        key_weight_second_moment,
        value_weight_second_moment,
        output_weight_square,
        gate_up_weight_square,
        down_weight_square,
        norm_gains_square,
        headnorm_gains_square,
    )
    lowered = tuple((weight.astype(jnp.bfloat16) for weight in params))
    gathered = (
        lax.all_gather(lowered[0], "fsdp", axis=0, tiled=True),
        lax.all_gather(lowered[1], "fsdp", axis=0, tiled=True),
        lax.all_gather(lowered[2], "fsdp", axis=0, tiled=True),
        lax.all_gather(lowered[3], "fsdp", axis=0, tiled=True),
        lax.all_gather(lowered[4], "fsdp", axis=1, tiled=True),
        lax.all_gather(lowered[5], "fsdp", axis=0, tiled=True),
        lax.all_gather(lowered[6], "fsdp", axis=1, tiled=True),
        lax.all_gather(lowered[7], "fsdp", axis=1, tiled=True),
    )
    query_full, key_full, value_full, output_full, gate_up_full, down_full, norm_full, head_full = (
        gathered
    )
    norm_gain = norm_full.astype(jnp.float32)
    head_gain = head_full.astype(jnp.float32)
    packed_token_count = layer_input.shape[0]
    local_query = query_full.shape[1] // HEAD_SIZE
    local_groups = key_full.shape[1] // HEAD_SIZE
    query_group_width = local_query // local_groups
    score_scale = 1.0 / math.sqrt(HEAD_SIZE)
    token_positions = positions_of(segment_ids)
    token_index = jnp.arange(packed_token_count, dtype=jnp.int32)
    input_rows = layer_input.astype(jnp.float32)

    def head_map(projected, gain, heads):
        return rotary_embedding(
            root_mean_scale(projected.reshape(packed_token_count, heads, HEAD_SIZE)) * gain,
            token_positions,
        )

    normed_one = gained_norm(input_rows, norm_gain[0]).astype(jnp.bfloat16)
    query_proj = jnp.dot(normed_one, query_full, preferred_element_type=jnp.float32)
    key_projected = jnp.dot(normed_one, key_full, preferred_element_type=jnp.float32)
    value_projected = jnp.dot(normed_one, value_full, preferred_element_type=jnp.float32)
    query_heads = (
        head_map(query_proj, head_gain[0], local_query)
        .astype(jnp.bfloat16)
        .reshape(packed_token_count, local_groups, query_group_width, HEAD_SIZE)
    )
    per_head_keys = head_map(key_projected, head_gain[1], local_groups).astype(jnp.bfloat16)
    per_head_values = value_projected.astype(jnp.bfloat16).reshape(
        packed_token_count, local_groups, HEAD_SIZE
    )
    block_rows = min(512, packed_token_count)
    block_count = packed_token_count // block_rows

    def block_scores(row_start, row_stop):
        raw_scores = (
            jnp.einsum(
                "qhgd,khd->hgqk",
                query_heads[row_start:row_stop],
                per_head_keys[:row_stop],
                preferred_element_type=jnp.float32,
            )
            * score_scale
        )
        allowed = (segment_ids[row_start:row_stop, None] == segment_ids[None, :row_stop]) & (
            token_index[None, :row_stop] <= token_index[row_start:row_stop, None]
        )
        return jnp.where(allowed, raw_scores, MASKED)

    mixed_blocks = []
    log_sums = []
    for block_index in range(block_count):
        row_start = block_index * block_rows
        row_stop = row_start + block_rows
        scores = block_scores(row_start, row_stop)
        row_max = jnp.max(scores, axis=-1, keepdims=True)
        exponent = jnp.exp(scores - row_max)
        row_sum = jnp.sum(exponent, axis=-1, keepdims=True)
        weights_block = (exponent / row_sum).astype(jnp.bfloat16)
        log_sums.append(row_max + jnp.log(row_sum))
        mixed_blocks.append(
            jnp.einsum(
                "hgqk,khd->qhgd",
                weights_block,
                per_head_values[:row_stop],
                preferred_element_type=jnp.float32,
            )
        )
    mixed = (
        jnp.concatenate(mixed_blocks, axis=0)
        .reshape(packed_token_count, local_query * HEAD_SIZE)
        .astype(jnp.bfloat16)
    )
    attention_part = contract_cols(mixed, output_full)
    attention_out = lax.psum(attention_part, "tensor")
    middle = input_rows + attention_out
    normed_two = gained_norm(middle, norm_gain[1]).astype(jnp.bfloat16)
    gate_proj = jnp.dot(normed_two, gate_up_full[0], preferred_element_type=jnp.float32)
    up_proj = jnp.dot(normed_two, gate_up_full[1], preferred_element_type=jnp.float32)
    hidden = swiglu(gate_proj, up_proj).astype(jnp.bfloat16)
    down_part = contract_cols(hidden, down_full)
    feedforward_out = lax.psum(down_part.astype(jnp.bfloat16), "tensor").astype(jnp.float32)
    layer_output = middle + feedforward_out
    query_back, key_back, value_back, output_back, gate_up_back, down_back = (
        query_full,
        key_full,
        value_full,
        output_full,
        gate_up_full,
        down_full,
    )
    grad_rows = out_grad.astype(jnp.float32)
    down_grad = contract_rows(out_grad, hidden)
    hidden_grad = jnp.dot(out_grad, down_back, preferred_element_type=jnp.float32)
    swiglu_out, swiglu_back = jax.vjp(swiglu, gate_proj, up_proj)
    gate_grad, up_grad = swiglu_back(hidden_grad)
    gate_grad_low = gate_grad.astype(jnp.bfloat16)
    up_grad_low = up_grad.astype(jnp.bfloat16)
    gate_up_grad = jnp.stack(
        [contract_rows(normed_two, gate_grad_low), contract_rows(normed_two, up_grad_low)]
    )
    normed_two_part = contract_cols(gate_grad_low, gate_up_back[0]) + contract_cols(
        up_grad_low, gate_up_back[1]
    )
    normed_two_grad = lax.psum(normed_two_part, "tensor")
    norm_two_out, norm_two_back = jax.vjp(gained_norm, middle, norm_gain[1])
    middle_norm_grad, gain_two_grad = norm_two_back(normed_two_grad)
    middle_grad = grad_rows + middle_norm_grad
    middle_grad_low = middle_grad.astype(jnp.bfloat16)
    output_grad_w = contract_rows(middle_grad_low, mixed)
    mixed_grad = jnp.dot(middle_grad_low, output_back, preferred_element_type=jnp.float32).astype(
        jnp.bfloat16
    )
    mixed_grad = mixed_grad.reshape(packed_token_count, local_groups, query_group_width, HEAD_SIZE)
    query_grad_blocks = []
    key_grad_acc = jnp.zeros((packed_token_count, local_groups, HEAD_SIZE), jnp.float32)
    value_grad_acc = jnp.zeros((packed_token_count, local_groups, HEAD_SIZE), jnp.float32)
    for block_index in range(block_count):
        row_start = block_index * block_rows
        row_stop = row_start + block_rows
        scores = block_scores(row_start, row_stop)
        probs = jnp.exp(scores - log_sums[block_index])
        grad_block = mixed_grad[row_start:row_stop]
        prob_grad = jnp.einsum(
            "qhgd,khd->hgqk",
            grad_block,
            per_head_values[:row_stop],
            preferred_element_type=jnp.float32,
        )
        row_inner = jnp.sum(probs * prob_grad, axis=-1, keepdims=True)
        score_grad = (probs * (prob_grad - row_inner)).astype(jnp.bfloat16)
        query_grad_blocks.append(
            jnp.einsum(
                "hgqk,khd->qhgd",
                score_grad,
                per_head_keys[:row_stop],
                preferred_element_type=jnp.float32,
            )
            * score_scale
        )
        key_grad_acc = key_grad_acc.at[:row_stop].add(
            jnp.einsum(
                "hgqk,qhgd->khd",
                score_grad,
                query_heads[row_start:row_stop],
                preferred_element_type=jnp.float32,
            )
            * score_scale
        )
        value_grad_acc = value_grad_acc.at[:row_stop].add(
            jnp.einsum(
                "hgqk,qhgd->khd",
                probs.astype(jnp.bfloat16),
                grad_block,
                preferred_element_type=jnp.float32,
            )
        )
    query_grad_heads = (
        jnp.concatenate(query_grad_blocks, axis=0)
        .reshape(packed_token_count, local_query, HEAD_SIZE)
        .astype(jnp.bfloat16)
        .astype(jnp.float32)
    )
    key_grad_heads = key_grad_acc.astype(jnp.bfloat16).astype(jnp.float32)
    value_grad_low = value_grad_acc.astype(jnp.bfloat16).reshape(
        packed_token_count, local_groups * HEAD_SIZE
    )
    query_map_out, query_map_back = jax.vjp(
        lambda projected, gain: head_map(projected, gain, local_query), query_proj, head_gain[0]
    )
    query_proj_grad, head_query_grad = query_map_back(query_grad_heads)
    key_map_out, key_map_back = jax.vjp(
        lambda projected, gain: head_map(projected, gain, local_groups), key_projected, head_gain[1]
    )
    key_proj_grad, head_key_grad = key_map_back(key_grad_heads)
    query_proj_low = query_proj_grad.astype(jnp.bfloat16)
    key_proj_low = key_proj_grad.astype(jnp.bfloat16)
    query_grad_w = contract_rows(normed_one, query_proj_low)
    key_grad_w = contract_rows(normed_one, key_proj_low)
    value_grad_w = contract_rows(normed_one, value_grad_low)
    normed_one_part = (
        contract_cols(query_proj_low, query_back)
        + contract_cols(key_proj_low, key_back)
        + contract_cols(value_grad_low, value_back)
    )
    normed_one_grad, head_query_total, head_key_total = lax.psum(
        (normed_one_part, head_query_grad, head_key_grad), "tensor"
    )
    norm_one_out, norm_one_back = jax.vjp(gained_norm, input_rows, norm_gain[0])
    input_norm_grad, gain_one_grad = norm_one_back(normed_one_grad)
    input_grad = middle_grad + input_norm_grad
    norm_grads = jnp.stack([gain_one_grad, gain_two_grad])
    head_grads = jnp.stack([head_query_total, head_key_total])
    shard_grads = (
        lax.psum_scatter(query_grad_w, "fsdp", scatter_dimension=0, tiled=True),
        lax.psum_scatter(key_grad_w, "fsdp", scatter_dimension=0, tiled=True),
        lax.psum_scatter(value_grad_w, "fsdp", scatter_dimension=0, tiled=True),
        lax.psum_scatter(output_grad_w, "fsdp", scatter_dimension=0, tiled=True),
        lax.psum_scatter(gate_up_grad, "fsdp", scatter_dimension=1, tiled=True),
        lax.psum_scatter(down_grad, "fsdp", scatter_dimension=0, tiled=True),
        lax.psum_scatter(norm_grads, "fsdp", scatter_dimension=1, tiled=True),
        lax.psum_scatter(head_grads, "fsdp", scatter_dimension=1, tiled=True),
    )
    next_steps = []
    next_means = []
    next_squares = []
    for param_index in range(8):
        learn_rate = MATRIX_RATE if param_index < 6 else GAIN_RATE
        decay_rate = WEIGHT_DECAY if param_index < 6 else 0.0
        weight_step, mean_next, square_next = adam_step(
            params[param_index],
            shard_grads[param_index],
            means[param_index],
            squares[param_index],
            learn_rate,
            decay_rate,
        )
        next_steps.append(weight_step)
        next_means.append(mean_next)
        next_squares.append(square_next)
    results = (
        [layer_output, input_grad] + list(shard_grads) + next_steps + next_means + next_squares
    )
    return tuple(results)


def solution(mesh):
    return jax.shard_map(
        per_device,
        mesh=mesh,
        in_specs=(
            P("fsdp", None),
            P("fsdp", None),
            P("fsdp"),
            P("fsdp", "tensor"),
            P("fsdp", "tensor"),
            P("fsdp", "tensor"),
            P("fsdp", "tensor"),
            P(None, "fsdp", "tensor"),
            P("fsdp", "tensor"),
            P(None, "fsdp"),
            P(None, "fsdp"),
            P("fsdp", "tensor"),
            P("fsdp", "tensor"),
            P("fsdp", "tensor"),
            P("fsdp", "tensor"),
            P(None, "fsdp", "tensor"),
            P("fsdp", "tensor"),
            P(None, "fsdp"),
            P(None, "fsdp"),
            P("fsdp", "tensor"),
            P("fsdp", "tensor"),
            P("fsdp", "tensor"),
            P("fsdp", "tensor"),
            P(None, "fsdp", "tensor"),
            P("fsdp", "tensor"),
            P(None, "fsdp"),
            P(None, "fsdp"),
        ),
        out_specs=(
            P("fsdp", None),
            P("fsdp", None),
            P("fsdp", "tensor"),
            P("fsdp", "tensor"),
            P("fsdp", "tensor"),
            P("fsdp", "tensor"),
            P(None, "fsdp", "tensor"),
            P("fsdp", "tensor"),
            P(None, "fsdp"),
            P(None, "fsdp"),
            P("fsdp", "tensor"),
            P("fsdp", "tensor"),
            P("fsdp", "tensor"),
            P("fsdp", "tensor"),
            P(None, "fsdp", "tensor"),
            P("fsdp", "tensor"),
            P(None, "fsdp"),
            P(None, "fsdp"),
            P("fsdp", "tensor"),
            P("fsdp", "tensor"),
            P("fsdp", "tensor"),
            P("fsdp", "tensor"),
            P(None, "fsdp", "tensor"),
            P("fsdp", "tensor"),
            P(None, "fsdp"),
            P(None, "fsdp"),
            P("fsdp", "tensor"),
            P("fsdp", "tensor"),
            P("fsdp", "tensor"),
            P("fsdp", "tensor"),
            P(None, "fsdp", "tensor"),
            P("fsdp", "tensor"),
            P(None, "fsdp"),
            P(None, "fsdp"),
        ),
        check_vma=False,
    )
```

profile of v0, /device:TPU:0, one launch (start us, length us, event | category | flops | bytes accessed | tf_op | source)
XLA Modules:
  0.0 2206.6 jit_solution(4290701593425707592)
XLA Ops:
  17.2 22.3 %all_gather.24 = bf16[2,2048]{1,0:T(2,128)(2,1)S(1)} all-gather(bf16[2,256]{1,0:T(2,128)(2,1)S(1)} %convert_element_type.143), channel_id=1, replica_groups=mesh['fsdp'=8,'tensor'=4] {'fsdp'}, dimensions={1}, use_global_device_ids=true | all-gather | bytes 9216 | tf_op jit(solution)/shard_map/all_gather | solution.py:148
  42.6 16.3 all-gather
  60.5 5.3 fusion.2
  67.4 4.8 multiply_reduce_fusion.8
  73.8 21.6 all-gather.8.cloned.1.call-done
  95.4 3.8 convolution_convert_fusion.1
  100.8 45.1 %all-gather.12.cloned.1.call-done = bf16[2048,512]{1,0:T(8,128)(2,1)} async-done(((bf16[256,512]{1,0:T(8,128)(2,1)}), bf16[2048,512]{1,0:T(8,128)(2,1)}) %all-gather.12.cloned.1.call-update) | async-done | bytes 2097168 | tf_op jit(solution)/shard_map/all_gather | solution.py:142
  146.0 5.3 multiply_reduce_fusion.5
  162.7 33.5 %all-gather.14.cloned.1.call-done = bf16[2048,512]{1,0:T(8,128)(2,1)} async-done(((bf16[256,512]{1,0:T(8,128)(2,1)}), bf16[2048,512]{1,0:T(8,128)(2,1)}) %all-gather.14.cloned.1.call-update) | async-done | bytes 2097168 | tf_op jit(solution)/shard_map/all_gather | solution.py:145
  196.2 7.4 fusion.106
  209.8 145.4 %all-reduce.12.cloned.1.call-done = f32[1024,2048]{1,0:T(8,128)} async-done(((f32[1024,2048]{1,0:T(8,128)}), f32[1024,2048]{1,0:T(8,128)}) %all-reduce.12.cloned.1.call-update) | async-done | bytes 8388624 | tf_op jit(solution)/shard_map/psum | solution.py:227
  355.1 5.7 multiply_reduce_fusion.2
  360.9 3.4 copy-done.1
  367.1 166.9 %all-gather.16.cloned.1.call-done = bf16[2,2048,1536]{2,1,0:T(8,128)(2,1)} async-done(((bf16[2,256,1536]{2,1,0:T(8,128)(2,1)}), bf16[2,2048,1536]{2,1,0:T(8,128)(2,1)}) %all-gather.16.cloned.1.call-update) | async-done | bytes 12582928 | tf_op jit(solution)/shard_map/all_gather | solution.py:146
  534.0 12.5 fusion.18
  546.6 8.6 fusion.20
  555.2 78.5 %all-gather.18.cloned.1.call-done = bf16[2048,1536]{1,0:T(8,128)(2,1)} async-done(((bf16[256,1536]{1,0:T(8,128)(2,1)}), bf16[2048,1536]{1,0:T(8,128)(2,1)}) %all-gather.18.cloned.1.call-update) | async-done | bytes 6291472 | tf_op jit(solution)/shard_map/all_gather | solution.py:147
  633.7 14.7 multiply_convert_fusion.1
  648.4 11.2 fusion.17
  659.6 10.9 fusion.28
  670.6 11.1 convolution_convert_fusion
  681.7 140.0 %all-reduce.16.cloned.1.call-done = f32[1024,2048]{1,0:T(8,128)} async-done(((f32[1024,2048]{1,0:T(8,128)}), f32[1024,2048]{1,0:T(8,128)}) %all-reduce.16.cloned.1.call-update) | async-done | bytes 8388624 | tf_op jit(solution)/shard_map/psum | solution.py:257
  821.7 7.4 multiply_reduce_fusion
  829.1 80.6 %all-reduce.14.cloned.1.call-done = bf16[1024,2048]{1,0:T(8,128)(2,1)} async-done(((bf16[1024,2048]{1,0:T(8,128)(2,1)}), bf16[1024,2048]{1,0:T(8,128)(2,1)}) %all-reduce.14.cloned.1.call-update) | async-done | bytes 4194320 | tf_op jit(solution)/shard_map/psum | solution.py:234
  909.7 13.5 fusion.4
  947.4 5.1 fusion.55
  956.2 4.6 add_add_fusion.2
  960.9 6.1 all-reduce.6
  967.8 4.8 fusion.110
  972.8 4.9 fusion.111
  977.7 136.3 %all-reduce.18.cloned.1.call-done = f32[1024,2048]{1,0:T(8,128)} async-done(((f32[1024,2048]{1,0:T(8,128)}), f32[1024,2048]{1,0:T(8,128)}) %all-reduce.18.cloned.1.call-update) | async-done | bytes 8388624 | tf_op jit(solution)/shard_map/psum | solution.py:338
  1114.0 6.1 fusion.3
  1121.6 6.6 fusion.109
  1129.4 7.8 fusion.35
  1139.0 11.4 convolution_bitcast_fusion
  1151.0 10.0 convolution_bitcast_fusion.1
  1161.0 7.0 convolution_bitcast_fusion.2
  1167.9 9.1 pad_maximum_fusion
  1185.3 67.2 %reduce-scatter.15.cloned.1.call-done = f32[256,256]{1,0:T(8,128)} async-done(((f32[2048,256]{1,0:T(8,128)}), f32[256,256]{1,0:T(8,128)}) %reduce-scatter.15.cloned.1.call-update) | async-done | bytes 262160 | tf_op jit(solution)/shard_map/reduce_scatter | solution.py:348
  1254.6 69.5 %reduce-scatter.17.cloned.1.call-done = f32[256,256]{1,0:T(8,128)} async-done(((f32[2048,256]{1,0:T(8,128)}), f32[256,256]{1,0:T(8,128)}) %reduce-scatter.17.cloned.1.call-update) | async-done | bytes 262160 | tf_op jit(solution)/shard_map/reduce_scatter | solution.py:349
  1326.2 11.7 fusion.5
  1337.9 53.2 %reduce-scatter.25.cloned.1.call-done = f32[256,2]{1,0:T(8,128)} async-done(((f32[2048,2]{1,0:T(8,128)}), f32[256,2]{1,0:T(8,128)}) %reduce-scatter.25.cloned.1.call-update) | async-done | bytes 2064
  1392.7 89.7 %reduce-scatter.13.cloned.1.call-done = f32[256,512]{1,0:T(8,128)} async-done(((f32[2048,512]{1,0:T(8,128)}), f32[256,512]{1,0:T(8,128)}) %reduce-scatter.13.cloned.1.call-update) | async-done | bytes 524304 | tf_op jit(solution)/shard_map/reduce_scatter | solution.py:347
  1485.3 89.1 %reduce-scatter.19.cloned.1.call-done = f32[256,512]{1,0:T(8,128)} async-done(((f32[2048,512]{1,0:T(8,128)}), f32[256,512]{1,0:T(8,128)}) %reduce-scatter.19.cloned.1.call-update) | async-done | bytes 524304 | tf_op jit(solution)/shard_map/reduce_scatter | solution.py:350
  1577.3 208.1 %reduce-scatter.23.cloned.1.call-done = f32[256,1536]{0,1:T(8,128)} async-done(((f32[2048,1536]{0,1:T(8,128)}), f32[256,1536]{0,1:T(8,128)}) %reduce-scatter.23.cloned.1.call-update) | async-done | bytes 1572880 | tf_op jit(solution)/shard_map/reduce_scatter | solution.py:352
  1785.4 4.8 subtract_subtract_fusion.1
  1802.7 389.9 %reduce-scatter.21.cloned.1.call-done = f32[2,256,1536]{2,1,0:T(8,128)} async-done(((f32[2,2048,1536]{2,1,0:T(8,128)}), f32[2,256,1536]{2,1,0:T(8,128)}) %reduce-scatter.21.cloned.1.call-update) | async-done | bytes 3145744 | tf_op jit(solution)/shard_map/reduce_scatter | solution.py:351
  2192.6 6.9 subtract_subtract_fusion
  (286 shorter events, 105.4 us)
Async XLA Ops:
  7.2 35.3 %copy-start.64 = (f32[2,16]{1,0:T(2,128)S(1)}, f32[2,16]{1,0:T(2,128)}, u32[]{:S(2)}) copy-start(f32[2,16]{1,0:T(2,128)} %param.49) | copy-start | bytes 388
  7.2 60.2 %all-gather.10.cloned.1.call-start = ((), (), s32[]{:S(2)}) async-start(), calls=%async_computation.9 | async-start | bytes 1179648 | tf_op jit(solution)/shard_map/all_gather | solution.py:143
  8.9 86.5 %all-gather.8.cloned.1.call-start = ((), (), s32[]{:S(2)}) async-start(), calls=%async_computation.8 | async-start | bytes 1179648 | tf_op jit(solution)/shard_map/all_gather | solution.py:144
  10.6 135.4 %all-gather.12.cloned.1.call-start = ((), (), s32[]{:S(2)}) async-start(), calls=%async_computation.10 | async-start | bytes 2359296 | tf_op jit(solution)/shard_map/all_gather | solution.py:142
  12.5 183.7 %all-gather.14.cloned.1.call-start = ((), (), s32[]{:S(2)}) async-start(), calls=%async_computation.11 | async-start | bytes 2359296 | tf_op jit(solution)/shard_map/all_gather | solution.py:145
  14.3 340.8 %all-reduce.12.cloned.1.call-start = ((), (), s32[]{:S(2)}) async-start(), calls=%async_computation.12 | async-start | bytes 16777216 | tf_op jit(solution)/shard_map/psum | solution.py:227
  39.4 26.4 %copy-start.44 = (f32[1,2048]{1,0:T(1,128)}, f32[1,2048]{1,0:T(1,128)S(1)}, u32[]{:S(2)}) copy-start(f32[1,2048]{1,0:T(1,128)S(1)} %get-tuple-element.322) | copy-start | bytes 24580
  42.5 17.9 copy-start.51
  42.6 23.3 %copy-start.46 = (f32[1024]{0:T(1024)}, f32[1024]{0:T(1024)S(1)}, u32[]{:S(2)}) copy-start(f32[1024]{0:T(1024)S(1)} %fusion.85) | copy-start | bytes 12292
  59.0 41.0 %copy-start.57 = (f32[128]{0:T(128)}, f32[128]{0:T(128)S(1)}, u32[]{:S(2)}) copy-start(f32[128]{0:T(128)S(1)} %get-tuple-element.327) | copy-start | bytes 1540
  59.0 92.3 %copy-start.59 = (f32[128]{0:T(128)}, f32[128]{0:T(128)S(1)}, u32[]{:S(2)}) copy-start(f32[128]{0:T(128)S(1)} %get-tuple-element.328) | copy-start | bytes 1540
  60.0 93.0 %copy-start.22 = (f32[1024,64]{0,1:T(8,128)}, f32[1024,64]{0,1:T(8,128)S(1)}, u32[]{:S(2)}) copy-start(f32[1024,64]{0,1:T(8,128)S(1)} %get-tuple-element.323) | copy-start | bytes 786436
  60.0 93.0 %copy-start.24 = (f32[1024,64]{0,1:T(8,128)}, f32[1024,64]{0,1:T(8,128)S(1)}, u32[]{:S(2)}) copy-start(f32[1024,64]{0,1:T(8,128)S(1)} %get-tuple-element.324) | copy-start | bytes 786436
  60.2 40.1 %copy-start.18 = (f32[1024,64]{1,0:T(8,128)}, f32[1024,64]{1,0:T(8,128)S(1)}, u32[]{:S(2)}) copy-start(f32[1024,64]{1,0:T(8,128)S(1)} %copy.206) | copy-start | bytes 786436
  60.4 39.9 %copy-start.20 = (f32[1024,64]{1,0:T(8,128)}, f32[1024,64]{1,0:T(8,128)S(1)}, u32[]{:S(2)}) copy-start(f32[1024,64]{1,0:T(8,128)S(1)} %copy.205) | copy-start | bytes 786436
  73.8 26.2 %copy-start.7 = (f32[1024,2,128]{2,0,1:T(8,128)}, f32[1024,2,128]{2,0,1:T(8,128)S(1)}, u32[]{:S(2)}) copy-start(f32[1024,2,128]{2,0,1:T(8,128)S(1)} %copy.203) | copy-start | bytes 3145732
  73.8 26.2 %copy-start.42 = (f32[1024,2]{0,1:T(2,128)}, f32[1024,2]{0,1:T(2,128)S(1)}, u32[]{:S(2)}) copy-start(f32[1024,2]{0,1:T(2,128)S(1)} %fusion.84) | copy-start | bytes 24580
  99.2 60.5 %copy-start.30 = (bf16[1024,256]{0,1:T(8,128)(2,1)}, bf16[1024,256]{0,1:T(8,128)(2,1)S(1)}, u32[]{:S(2)}) copy-start(bf16[1024,256]{0,1:T(8,128)(2,1)S(1)} %convolution_convert_fusion.1) | copy-start | bytes 1572868
  100.8 54.3 %copy-start.11 = (bf16[1024,2,64]{2,0,1:T(8,128)(2,1)}, bf16[1024,2,64]{2,0,1:T(8,128)(2,1)S(1)}, u32[]{:S(2)}) copy-start(bf16[1024,2,64]{2,0,1:T(8,128)(2,1)S(1)} %get-tuple-element.315) | copy-start | bytes 786436
  100.8 54.3 %copy-start.13 = (bf16[1024,2,64]{2,0,1:T(8,128)(2,1)}, bf16[1024,2,64]{2,0,1:T(8,128)(2,1)S(1)}, u32[]{:S(2)}) copy-start(bf16[1024,2,64]{2,0,1:T(8,128)(2,1)S(1)} %get-tuple-element.316) | copy-start | bytes 786436
  162.6 40.9 %copy-start.37 = (bf16[1024,2,2,128]{0,3,2,1:T(8,128)(2,1)}, bf16[1024,2,2,128]{0,3,2,1:T(8,128)(2,1)S(1)}, u32[]{:S(2)}) copy-start(bf16[1024,2,2,128]{0,3,2,1:T(8,128)(2,1)S(1)} %pad_maximum_fusion.1) | copy-start | bytes 3145732
  203.6 330.4 %all-gather.16.cloned.1.call-start = ((), (), s32[]{:S(2)}) async-start(), calls=%async_computation.13 | async-start | bytes 14155776 | tf_op jit(solution)/shard_map/all_gather | solution.py:146
  206.8 426.9 %all-gather.18.cloned.1.call-start = ((), (), s32[]{:S(2)}) async-start(), calls=%async_computation.14 | async-start | bytes 7077888 | tf_op jit(solution)/shard_map/all_gather | solution.py:147
  209.7 612.0 %all-reduce.16.cloned.1.call-start = ((), (), s32[]{:S(2)}) async-start(), calls=%async_computation.16 | async-start | bytes 16777216 | tf_op jit(solution)/shard_map/psum | solution.py:257
  534.0 12.5 copy-start.26
  534.0 12.5 copy-start.68
  648.4 11.2 copy-start.71
  648.4 22.1 %copy-start.74 = (bf16[1024,1536]{1,0:T(8,128)(2,1)}, bf16[1024,1536]{1,0:T(8,128)(2,1)S(1)}, u32[]{:S(2)}) copy-start(bf16[1024,1536]{1,0:T(8,128)(2,1)S(1)} %get-tuple-element.306) | copy-start | bytes 9437188
  670.5 239.2 %all-reduce.14.cloned.1.call-start = ((), (), s32[]{:S(2)}) async-start(), calls=%async_computation.15 | async-start | bytes 8388608 | tf_op jit(solution)/shard_map/psum | solution.py:234
  681.6 432.4 %all-reduce.18.cloned.1.call-start = ((), (), s32[]{:S(2)}) async-start(), calls=%async_computation.17 | async-start | bytes 16777216 | tf_op jit(solution)/shard_map/psum | solution.py:338
  909.7 13.6 copy-start.70
  960.9 223.0 %reduce-scatter.27.cloned.1.call-start = ((), (), s32[]{:S(2)}) async-start(), calls=%async_computation.25 | async-start | bytes 73728
  967.8 284.7 %reduce-scatter.15.cloned.1.call-start = ((), (), s32[]{:S(2)}) async-start(), calls=%async_computation.19 | async-start | bytes 2359296 | tf_op jit(solution)/shard_map/reduce_scatter | solution.py:348
  972.7 141.3 %copy-start.45 = (f32[1,2048]{1,0:T(1,128)S(1)}, f32[1,2048]{1,0:T(1,128)}, u32[]{:S(2)}) copy-start(f32[1,2048]{1,0:T(1,128)} %copy-done.44) | copy-start | bytes 24580
  972.7 141.3 %copy-start.47 = (f32[1024]{0:T(1024)S(1)}, f32[1024]{0:T(1024)}, u32[]{:S(2)}) copy-start(f32[1024]{0:T(1024)} %copy-done.46) | copy-start | bytes 12292
  972.7 351.3 %reduce-scatter.17.cloned.1.call-start = ((), (), s32[]{:S(2)}) async-start(), calls=%async_computation.20 | async-start | bytes 2359296 | tf_op jit(solution)/shard_map/reduce_scatter | solution.py:349
  977.7 413.4 %reduce-scatter.25.cloned.1.call-start = ((), (), s32[]{:S(2)}) async-start(), calls=%async_computation.24 | async-start | bytes 1179648
  1121.5 360.8 %reduce-scatter.13.cloned.1.call-start = ((), (), s32[]{:S(2)}) async-start(), calls=%async_computation.18 | async-start | bytes 4718592 | tf_op jit(solution)/shard_map/reduce_scatter | solution.py:347
  1128.2 446.2 %reduce-scatter.19.cloned.1.call-start = ((), (), s32[]{:S(2)}) async-start(), calls=%async_computation.21 | async-start | bytes 4718592 | tf_op jit(solution)/shard_map/reduce_scatter | solution.py:350
  1137.2 648.2 %reduce-scatter.23.cloned.1.call-start = ((), (), s32[]{:S(2)}) async-start(), calls=%async_computation.23 | async-start | bytes 14155776 | tf_op jit(solution)/shard_map/reduce_scatter | solution.py:352
  1150.5 1042.1 %reduce-scatter.21.cloned.1.call-start = ((), (), s32[]{:S(2)}) async-start(), calls=%async_computation.22 | async-start | bytes 28311552 | tf_op jit(solution)/shard_map/reduce_scatter | solution.py:351
  1178.5 74.0 %copy-start.34 = (f32[256,256]{1,0:T(8,128)S(1)}, f32[256,256]{1,0:T(8,128)}, u32[]{:S(2)}) copy-start(f32[256,256]{1,0:T(8,128)} %param.43) | copy-start | bytes 786436
  1184.6 153.3 %copy-start.61 = (f32[2,16]{1,0:T(2,128)}, f32[2,16]{1,0:T(2,128)S(1)}, u32[]{:S(2)}) copy-start(f32[2,16]{1,0:T(2,128)S(1)} %copy.280) | copy-start | bytes 388
  1326.2 65.8 %copy-start.56 = (f32[2,256]{1,0:T(2,128)S(1)}, f32[2,256]{1,0:T(2,128)}, u32[]{:S(2)}) copy-start(f32[2,256]{1,0:T(2,128)} %param.48) | copy-start | bytes 6148
  1326.2 65.8 %copy-start.62 = (f32[2,256]{1,0:T(2,128)S(1)}, f32[2,256]{1,0:T(2,128)}, u32[]{:S(2)}) copy-start(f32[2,256]{1,0:T(2,128)} %param.56) | copy-start | bytes 6148
  1326.2 65.8 %copy-start.63 = (f32[2,256]{1,0:T(2,128)S(1)}, f32[2,256]{1,0:T(2,128)}, u32[]{:S(2)}) copy-start(f32[2,256]{1,0:T(2,128)} %param.64) | copy-start | bytes 6148
  1392.1 398.1 %copy-start.55 = (f32[2,256]{1,0:T(2,128)}, f32[2,256]{1,0:T(2,128)S(1)}, u32[]{:S(2)}) copy-start(f32[2,256]{1,0:T(2,128)S(1)} %copy.278) | copy-start | bytes 6148
  1793.2 399.4 %copy-start.10 = (f32[2,256,1536]{2,1,0:T(8,128)S(1)}, f32[2,256,1536]{2,1,0:T(8,128)}, u32[]{:S(2)}) copy-start(f32[2,256,1536]{2,1,0:T(8,128)} %param.46) | copy-start | bytes 9437188
  (48 other events, 146.9 us)
Sparse Core Ops, SparseCore 0:
  10.7 42.9 all-gather.9
  56.4 38.9 all-gather.7
  98.1 47.7 all-gather.11
  148.5 47.6 all-gather.13
  203.7 151.3 all-reduce.11
  357.8 176.2 all-gather.15
  536.8 96.8 all-gather.17
  670.6 151.0 all-reduce.15
  824.1 85.6 all-reduce.13
  961.0 152.9 all-reduce.17
  1118.0 62.5 reduce-scatter.26
  1185.1 67.2 reduce-scatter.14
  1256.6 67.4 reduce-scatter.16
  1327.9 63.1 reduce-scatter.24
  1395.1 87.1 reduce-scatter.12
  1486.4 87.9 reduce-scatter.18
  1577.8 207.4 reduce-scatter.22
  1789.7 402.9 reduce-scatter.20
where the time goes:
time: 2220 us; the launch traced here: 2210 us
  waiting for transfers between devices  1810 us (82%)
  matrix products  171 us (8%)
  other arithmetic  116 us (5%)
  blocking collectives  44.6 us (2%)
  local copies, waits for them, and re-layouts  43.2 us (2%)
    reduce_scatter x1, waiting for transfers between devices, per_device(): lax.psum_scatter(gate_up_grad, 'fsdp', scatter_dimension=1, tiled=True)  390 us
    reduce_scatter x1, waiting for transfers between devices, per_device(): lax.psum_scatter(down_grad, 'fsdp', scatter_dimension=0, tiled=True)  208 us
    all_gather x1, waiting for transfers between devices, per_device(): lax.all_gather(lowered[4], 'fsdp', axis=1, tiled=True)  167 us
    psum x1, waiting for transfers between devices, per_device(): attention_out = lax.psum(attention_part, 'tensor')  145 us
    psum x1, waiting for transfers between devices, per_device(): normed_two_grad = lax.psum(normed_two_part, 'tensor')  140 us
    psum x1, waiting for transfers between devices, per_device(): lax.psum((normed_one_part, head_query_grad, head_key_grad), 'tensor')  136 us
    reduce_scatter x1, waiting for transfers between devices, per_device(): lax.psum_scatter(query_grad_w, 'fsdp', scatter_dimension=0, tiled=True)  89.7 us
    reduce_scatter x1, waiting for transfers between devices, per_device(): lax.psum_scatter(output_grad_w, 'fsdp', scatter_dimension=0, tiled=True)  89.1 us
  transfers between devices with their start and end apart: 18, of which 16 were waited for; matrix products, arithmetic and copies ran while one was open for 10% of the time, Pallas kernels for 0%

commit v1 on v0

--- a/solution.py
+++ b/solution.py
@@ -137,20 +137,26 @@
         norm_gains_square,
         headnorm_gains_square,
     )
-    lowered = tuple((weight.astype(jnp.bfloat16) for weight in params))
-    gathered = (
-        lax.all_gather(lowered[0], "fsdp", axis=0, tiled=True),
-        lax.all_gather(lowered[1], "fsdp", axis=0, tiled=True),
-        lax.all_gather(lowered[2], "fsdp", axis=0, tiled=True),
-        lax.all_gather(lowered[3], "fsdp", axis=0, tiled=True),
-        lax.all_gather(lowered[4], "fsdp", axis=1, tiled=True),
-        lax.all_gather(lowered[5], "fsdp", axis=0, tiled=True),
-        lax.all_gather(lowered[6], "fsdp", axis=1, tiled=True),
-        lax.all_gather(lowered[7], "fsdp", axis=1, tiled=True),
-    )
-    query_full, key_full, value_full, output_full, gate_up_full, down_full, norm_full, head_full = (
-        gathered
-    )
+    gain_rows = norm_gains.shape[1]
+    gains_low = lax.all_gather(
+        jnp.concatenate([norm_gains, headnorm_gains], axis=1).astype(jnp.bfloat16),
+        "fsdp",
+        axis=0,
+    )
+    norm_full = jnp.swapaxes(gains_low[:, :, :gain_rows], 0, 1).reshape(2, -1)
+    head_full = jnp.swapaxes(gains_low[:, :, gain_rows:], 0, 1).reshape(2, -1)
+    query_cols = query_weight.shape[1]
+    key_cols = key_weight.shape[1]
+    attn_low = jnp.concatenate(
+        [query_weight, key_weight, value_matrix, output_weight], axis=1
+    ).astype(jnp.bfloat16)
+    attn_full = lax.all_gather(attn_low, "fsdp", axis=0, tiled=True)
+    query_full = attn_full[:, :query_cols]
+    key_full = attn_full[:, query_cols : query_cols + key_cols]
+    value_full = attn_full[:, query_cols + key_cols : query_cols + 2 * key_cols]
+    output_full = attn_full[:, query_cols + 2 * key_cols :]
+    gate_up_full = lax.all_gather(gate_up_weight.astype(jnp.bfloat16), "fsdp", axis=1, tiled=True)
+    down_full = lax.all_gather(down_weight.astype(jnp.bfloat16), "fsdp", axis=0, tiled=True)
     norm_gain = norm_full.astype(jnp.float32)
     head_gain = head_full.astype(jnp.float32)
     packed_token_count = layer_input.shape[0]
@@ -224,7 +230,7 @@
         .astype(jnp.bfloat16)
     )
     attention_part = contract_cols(mixed, output_full)
-    attention_out = lax.psum(attention_part, "tensor")
+    attention_out = lax.psum(attention_part.astype(jnp.bfloat16), "tensor").astype(jnp.float32)
     middle = input_rows + attention_out
     normed_two = gained_norm(middle, norm_gain[1]).astype(jnp.bfloat16)
     gate_proj = jnp.dot(normed_two, gate_up_full[0], preferred_element_type=jnp.float32)
@@ -254,7 +260,7 @@
     normed_two_part = contract_cols(gate_grad_low, gate_up_back[0]) + contract_cols(
         up_grad_low, gate_up_back[1]
     )
-    normed_two_grad = lax.psum(normed_two_part, "tensor")
+    normed_two_grad = lax.psum(normed_two_part.astype(jnp.bfloat16), "tensor").astype(jnp.float32)
     norm_two_out, norm_two_back = jax.vjp(gained_norm, middle, norm_gain[1])
     middle_norm_grad, gain_two_grad = norm_two_back(normed_two_grad)
     middle_grad = grad_rows + middle_norm_grad
@@ -335,23 +341,49 @@
         + contract_cols(key_proj_low, key_back)
         + contract_cols(value_grad_low, value_back)
     )
-    normed_one_grad, head_query_total, head_key_total = lax.psum(
-        (normed_one_part, head_query_grad, head_key_grad), "tensor"
-    )
+    normed_one_grad = lax.psum(normed_one_part.astype(jnp.bfloat16), "tensor").astype(jnp.float32)
+    head_query_total, head_key_total = lax.psum((head_query_grad, head_key_grad), "tensor")
     norm_one_out, norm_one_back = jax.vjp(gained_norm, input_rows, norm_gain[0])
     input_norm_grad, gain_one_grad = norm_one_back(normed_one_grad)
     input_grad = middle_grad + input_norm_grad
     norm_grads = jnp.stack([gain_one_grad, gain_two_grad])
     head_grads = jnp.stack([head_query_total, head_key_total])
+    attn_grads = lax.psum_scatter(
+        jnp.concatenate(
+            [
+                query_grad_w.astype(jnp.bfloat16),
+                key_grad_w.astype(jnp.bfloat16),
+                value_grad_w.astype(jnp.bfloat16),
+                output_grad_w.astype(jnp.bfloat16),
+            ],
+            axis=1,
+        ),
+        "fsdp",
+        scatter_dimension=0,
+        tiled=True,
+    ).astype(jnp.float32)
+    shards = norm_grads.shape[1] // gain_rows
+    gains_grad = lax.psum_scatter(
+        jnp.concatenate(
+            [norm_grads.reshape(2, shards, gain_rows), head_grads.reshape(2, shards, -1)], axis=2
+        ),
+        "fsdp",
+        scatter_dimension=1,
+        tiled=False,
+    )
     shard_grads = (
-        lax.psum_scatter(query_grad_w, "fsdp", scatter_dimension=0, tiled=True),
-        lax.psum_scatter(key_grad_w, "fsdp", scatter_dimension=0, tiled=True),
-        lax.psum_scatter(value_grad_w, "fsdp", scatter_dimension=0, tiled=True),
-        lax.psum_scatter(output_grad_w, "fsdp", scatter_dimension=0, tiled=True),
-        lax.psum_scatter(gate_up_grad, "fsdp", scatter_dimension=1, tiled=True),
-        lax.psum_scatter(down_grad, "fsdp", scatter_dimension=0, tiled=True),
-        lax.psum_scatter(norm_grads, "fsdp", scatter_dimension=1, tiled=True),
-        lax.psum_scatter(head_grads, "fsdp", scatter_dimension=1, tiled=True),
+        attn_grads[:, :query_cols],
+        attn_grads[:, query_cols : query_cols + key_cols],
+        attn_grads[:, query_cols + key_cols : query_cols + 2 * key_cols],
+        attn_grads[:, query_cols + 2 * key_cols :],
+        lax.psum_scatter(
+            gate_up_grad.astype(jnp.bfloat16), "fsdp", scatter_dimension=1, tiled=True
+        ).astype(jnp.float32),
+        lax.psum_scatter(
+            down_grad.astype(jnp.bfloat16), "fsdp", scatter_dimension=0, tiled=True
+        ).astype(jnp.float32),
+        gains_grad[:, :gain_rows],
+        gains_grad[:, gain_rows:],
     )
     next_steps = []
     next_means = []

time: 2220 us -> 1320 us (0.59)
  waiting for transfers between devices: 1810 us -> 868 us
  local copies, waits for them, and re-layouts: 43.2 us -> 79.2 us
  blocking collectives: 44.6 us -> 73.6 us
    reduce_scatter x6 -> x3, waiting for transfers between devices: 913 us -> 342 us  [the longest x1 173 us: per_device(): lax.psum_scatter(gate_up_grad.astype(jnp.bfloat16), 'fsdp', scatter_dimen...]
    psum x3 -> x2, waiting for transfers between devices: 422 us -> 150 us  [the longest x1 77.8 us: per_device(): lax.psum(attention_part.astype(jnp.bfloat16), 'tensor').astype(jnp.float32)]
    unnamed x20 -> x9, waiting for transfers between devices: 53.5 us -> 0.15 us
    unnamed x0 -> x1, blocking collectives: none -> 39.2 us
    all_gather x6 -> x3, waiting for transfers between devices: 346 us -> 310 us  [the longest x1 169 us: per_device(): lax.all_gather(gate_up_weight.astype(jnp.bfloat16), 'fsdp', axis=1, tiled...]
    unnamed x167 -> x244, local copies, waits for them, and re-layouts: 39.3 us -> 70.3 us
  transfers between devices with their start and end apart: 18 -> 9, of which waited for: 16 -> 9; matrix products, arithmetic and copies ran while one was open for 10% -> 16% of each run, Pallas kernels for 0% -> 0%
where the time goes in v1:
time: 1320 us; the launch traced here: 1310 us
  waiting for transfers between devices  868 us (66%)
  matrix products  160 us (12%)
  other arithmetic  117 us (9%)
  local copies, waits for them, and re-layouts  79.2 us (6%)
  blocking collectives  73.6 us (6%)
  between operations  15.9 us (1%)
    reduce_scatter x1, waiting for transfers between devices, per_device(): lax.psum_scatter(gate_up_grad.astype(jnp.bfloat16), 'fsdp', scatter_dimen...  173 us
    all_gather x1, waiting for transfers between devices, per_device(): lax.all_gather(gate_up_weight.astype(jnp.bfloat16), 'fsdp', axis=1, tiled...  169 us
    reduce_scatter x1, waiting for transfers between devices, per_device(): lax.psum_scatter(jnp.concatenate([query_grad_w.astype(jnp.bfloat16), key_...  108 us
    all_gather x1, waiting for transfers between devices, per_device(): lax.all_gather(down_weight.astype(jnp.bfloat16), 'fsdp', axis=0, tiled=True)  78.6 us
    psum x1, waiting for transfers between devices, per_device(): lax.psum(attention_part.astype(jnp.bfloat16), 'tensor').astype(jnp.float32)  77.8 us
    psum x1, waiting for transfers between devices, per_device(): lax.psum(normed_two_part.astype(jnp.bfloat16), 'tensor').astype(jnp.float32)  72.6 us
    unnamed x244, local copies, waits for them, and re-layouts  70.3 us
    psum x1, waiting for transfers between devices, per_device(): lax.psum(down_part.astype(jnp.bfloat16), 'tensor').astype(jnp.float32)  66.3 us
  transfers between devices with their start and end apart: 9, of which 9 were waited for; matrix products, arithmetic and copies ran while one was open for 16% of the time, Pallas kernels for 0%

profile of v1, /device:TPU:0, one launch (start us, length us, event | category | flops | bytes accessed | tf_op | source)
XLA Modules:
  0.0 1314.3 jit_solution(13533860759200355081)
XLA Ops:
  12.5 28.5 %all_gather.13 = bf16[8,2,272]{2,1,0:T(2,128)(2,1)S(1)} all-gather(bf16[1,2,272]{2,1,0:T(2,128)(2,1)S(1)} %pad_maximum_fusion.8), channel_id=1, replica_groups=mesh['fsdp'=8,'tensor'=4] {'fsdp'}, dimensions={0}, use_global_device_ids=true | all-gather | bytes 9792 | tf_op jit(solution)/shard_map/all_gather | solution.py:141
  43.3 3.3 fusion.10
  48.8 3.1 fusion.4
  51.8 62.2 %all-gather.4.cloned.1.call-done = bf16[2048,1536]{1,0:T(8,128)(2,1)} async-done(((bf16[256,1536]{1,0:T(8,128)(2,1)}), bf16[2048,1536]{1,0:T(8,128)(2,1)}) %all-gather.4.cloned.1.call-update) | async-done | bytes 6291472 | tf_op jit(solution)/shard_map/all_gather | solution.py:153
  114.0 5.2 multiply_reduce_fusion.3
  122.3 3.5 multiply_reduce_fusion.6
  128.0 4.2 convolution_convert_fusion.9
  144.5 6.0 convolution_convert_fusion.4
  153.8 2.6 convert_element_type.205
  156.6 77.8 %all-reduce.13.cloned.1.call-done = bf16[1024,2048]{1,0:T(8,128)(2,1)} async-done(((bf16[1024,2048]{1,0:T(8,128)(2,1)}), bf16[1024,2048]{1,0:T(8,128)(2,1)}) %all-reduce.13.cloned.1.call-update) | async-done | bytes 4194320 | tf_op jit(solution)/shard_map/psum | solution.py:233
  234.4 5.0 multiply_reduce_fusion
  240.3 4.4 multiply_convert_fusion
  244.7 168.7 %all-gather.6.cloned.1.call-done = bf16[2,2048,1536]{2,1,0:T(8,128)(2,1)} async-done(((bf16[2,256,1536]{2,1,0:T(8,128)(2,1)}), bf16[2,2048,1536]{2,1,0:T(8,128)(2,1)}) %all-gather.6.cloned.1.call-update) | async-done | bytes 12582928 | tf_op jit(solution)/shard_map/all_gather | solution.py:158
  413.4 12.3 fusion.25
  425.8 8.5 fusion.27
  434.3 78.6 %all-gather.8.cloned.1.call-done = bf16[2048,1536]{1,0:T(8,128)(2,1)} async-done(((bf16[256,1536]{1,0:T(8,128)(2,1)}), bf16[2048,1536]{1,0:T(8,128)(2,1)}) %all-gather.8.cloned.1.call-update) | async-done | bytes 6291472 | tf_op jit(solution)/shard_map/all_gather | solution.py:159
  513.0 15.7 %multiply_convert_fusion.1 = (bf16[1024,1536]{1,0:T(8,128)(2,1)S(1)}, bf16[1024,1536]{1,0:T(8,128)(2,1)S(1)}, bf16[1024,1536]{1,0:T(8,128)(2,1)}) fusion(f32[1024,1536]{1,0:T(8,128)} %fusion.25, f32[1024,1536]{1,0:T(8,128)} %fusion.27, bf16[1024,2048]{1,0:T(8,128)(2,1)} %param.40, bf16[2048,1536]{1,0:T(8,128)(2,1)} %all-gather.8.cloned.1.call-done), kind=kOutput, calls=%fused_computation.53 | convolution fusion | flops 6467616768 | bytes 32505856 | tf_op jit(solution)/shard_map/dot_general | solution.py:252
  528.7 11.1 fusion.24
  539.8 11.3 add_convert_fusion.1
  551.2 11.1 convolution_convert_fusion.3
  562.4 72.6 %all-reduce.15.cloned.1.call-done = bf16[1024,2048]{1,0:T(8,128)(2,1)} async-done(((bf16[1024,2048]{1,0:T(8,128)(2,1)}), bf16[1024,2048]{1,0:T(8,128)(2,1)}) %all-reduce.15.cloned.1.call-update) | async-done | bytes 4194320 | tf_op jit(solution)/shard_map/psum | solution.py:263
  635.0 8.1 fusion.6
  643.3 6.8 fusion.8
  650.1 5.8 fusion.54
  662.9 2.8 fusion.14
  680.5 2.5 fusion.87
  683.1 4.0 fusion.49
  687.2 4.7 add_convert_fusion
  691.9 11.4 fusion.18
  703.5 3.6 convolution_convert_fusion.7
  713.8 12.6 pad_maximum_fusion.1
  728.3 9.8 fusion.16
  738.1 7.4 fusion.17
  745.6 5.4 pad_maximum_fusion
  769.1 3.0 copy.396
  772.9 5.9 all-reduce.7
  778.8 66.3 %all-reduce.17.cloned.1.call-done = (bf16[1024,2048]{1,0:T(8,128)(2,1)}, bf16[1024,2048]{1,0:T(8,128)(2,1)}) async-done(((bf16[1024,2048]{1,0:T(8,128)(2,1)}, bf16[1024,2048]{1,0:T(8,128)(2,1)}), (bf16[1024,2048]{1,0:T(8,128)(2,1)}, bf16[1024,2048]{1,0:T(8,128)(2,1)})) %all-reduce.17.cloned.1.call-update) | async-done | bytes 8388624 | tf_op jit(solution)/shard_map/psum | solution.py:240
  845.2 6.2 fusion.7
  851.4 39.2 %all-reduce.6 = f32[2,8,272]{2,0,1:T(2,128)S(1)} all-reduce(f32[2,8,272]{2,0,1:T(2,128)S(1)} %pad_maximum_fusion.6), channel_id=5, replica_groups=mesh['fsdp'=8,'tensor'=4] {'fsdp'}, use_global_device_ids=true, to_apply=%region_28.29.clone | all-reduce | flops 4352 | bytes 34816
  892.5 14.6 %fusion.9 = (f32[1024,2048]{1,0:T(8,128)}, f32[1024,2048]{1,0:T(8,128)}) fusion(f32[1024,2048]{1,0:T(8,128)} %copy-done.8, bf16[1024,2048]{1,0:T(8,128)(2,1)} %get-tuple-element.281, bf16[1024,2048]{1,0:T(8,128)(2,1)} %param.39, f32[1024]{0:T(1024)S(1)} %multiply_multiply_fusion.10, f32[2048]{0:T(1024)S(1)} %bitcast.235, f32[1024]{0:T(1024)S(1)} %copy-done.74, ...), kind=kLoop, calls=%fused_computation.22 | loop fusion | flops 25165824 | bytes 41959424 | tf_op jit(solution)/shard_map/add | solution.py:348
  907.1 60.8 %reduce-scatter.8.cloned.1.call-done = bf16[256,1536]{0,1:T(8,128)(2,1)} async-done(((bf16[2048,1536]{0,1:T(8,128)(2,1)}), bf16[256,1536]{0,1:T(8,128)(2,1)}) %reduce-scatter.8.cloned.1.call-update) | async-done | bytes 786448 | tf_op jit(solution)/shard_map/reduce_scatter | solution.py:382
  967.9 4.6 subtract_subtract_fusion.1
  972.5 3.2 copy.409
  979.0 2.5 copy.404
  981.5 107.8 %reduce-scatter.4.cloned.1.call-done = bf16[256,1536]{0,1:T(8,128)(2,1)} async-done(((bf16[2048,1536]{0,1:T(8,128)(2,1)}), bf16[256,1536]{0,1:T(8,128)(2,1)}) %reduce-scatter.4.cloned.1.call-update) | async-done | bytes 786448 | tf_op jit(solution)/shard_map/reduce_scatter | solution.py:351
  1090.5 3.5 subtract_subtract_fusion.2
  1126.3 173.2 %reduce-scatter.6.cloned.1.call-done = bf16[2,256,1536]{2,1,0:T(8,128)(2,1)} async-done(((bf16[2,2048,1536]{2,1,0:T(8,128)(2,1)}), bf16[2,256,1536]{2,1,0:T(8,128)(2,1)}) %reduce-scatter.6.cloned.1.call-update) | async-done | bytes 1572880 | tf_op jit(solution)/shard_map/reduce_scatter | solution.py:379
  1299.6 7.7 subtract_subtract_fusion
  (347 shorter events, 118.7 us)
Async XLA Ops:
  7.2 33.9 %copy-start.75 = (s32[1024]{0:T(1024)S(1)}, s32[1024]{0:T(1024)}, u32[]{:S(2)}) copy-start(s32[1024]{0:T(1024)} %param.41) | copy-start | bytes 12292
  7.2 106.8 %all-gather.4.cloned.1.call-start = ((), (), s32[]{:S(2)}) async-start(), calls=%async_computation.3 | async-start | bytes 7077888 | tf_op jit(solution)/shard_map/all_gather | solution.py:153
  12.4 222.1 %all-reduce.13.cloned.1.call-start = ((), (), s32[]{:S(2)}) async-start(), calls=%async_computation.4 | async-start | bytes 8388608 | tf_op jit(solution)/shard_map/psum | solution.py:233
  41.1 78.3 %copy-start.86 = (f32[128]{0:T(128)}, f32[128]{0:T(128)S(1)}, u32[]{:S(2)}) copy-start(f32[128]{0:T(128)S(1)} %mul.723) | copy-start | bytes 1540
  41.2 91.1 %copy-start.84 = (f32[128]{0:T(128)}, f32[128]{0:T(128)S(1)}, u32[]{:S(2)}) copy-start(f32[128]{0:T(128)S(1)} %mul.708) | copy-start | bytes 1540
  42.8 77.1 %copy-start.30 = (f32[1024,64]{0,1:T(8,128)}, f32[1024,64]{0,1:T(8,128)S(1)}, u32[]{:S(2)}) copy-start(f32[1024,64]{0,1:T(8,128)S(1)} %get-tuple-element.338) | copy-start | bytes 786436
  42.8 77.1 %copy-start.32 = (f32[1024,64]{0,1:T(8,128)}, f32[1024,64]{0,1:T(8,128)S(1)}, u32[]{:S(2)}) copy-start(f32[1024,64]{0,1:T(8,128)S(1)} %get-tuple-element.339) | copy-start | bytes 786436
  43.0 89.7 %copy-start.26 = (f32[1024,64]{1,0:T(8,128)}, f32[1024,64]{1,0:T(8,128)S(1)}, u32[]{:S(2)}) copy-start(f32[1024,64]{1,0:T(8,128)S(1)} %copy.349) | copy-start | bytes 786436
  43.2 89.5 %copy-start.28 = (f32[1024,64]{1,0:T(8,128)}, f32[1024,64]{1,0:T(8,128)S(1)}, u32[]{:S(2)}) copy-start(f32[1024,64]{1,0:T(8,128)S(1)} %copy.350) | copy-start | bytes 786436
  132.1 7.5 copy-start.50
  150.6 262.9 %all-gather.6.cloned.1.call-start = ((), (), s32[]{:S(2)}) async-start(), calls=%async_computation.5 | async-start | bytes 14155776 | tf_op jit(solution)/shard_map/all_gather | solution.py:158
  153.8 359.2 %all-gather.8.cloned.1.call-start = ((), (), s32[]{:S(2)}) async-start(), calls=%async_computation.6 | async-start | bytes 7077888 | tf_op jit(solution)/shard_map/all_gather | solution.py:159
  156.5 478.5 %all-reduce.15.cloned.1.call-start = ((), (), s32[]{:S(2)}) async-start(), calls=%async_computation.7 | async-start | bytes 8388608 | tf_op jit(solution)/shard_map/psum | solution.py:263
  413.4 12.3 copy-start.34
  413.4 12.3 copy-start.94
  528.7 11.1 copy-start.96
  528.7 11.1 copy-start.98
  551.1 294.0 %all-reduce.17.cloned.1.call-start = ((), (), s32[]{:S(2)}) async-start(), calls=%async_computation.11 | async-start | bytes 16777216 | tf_op jit(solution)/shard_map/psum | solution.py:240
  635.0 8.1 copy-start.2
  635.0 8.2 copy-start.5
  635.0 8.3 copy-start.13
  691.9 276.0 %reduce-scatter.8.cloned.1.call-start = ((), (), s32[]{:S(2)}) async-start(), calls=%async_computation.10 | async-start | bytes 7077888 | tf_op jit(solution)/shard_map/reduce_scatter | solution.py:382
  703.4 385.8 %reduce-scatter.4.cloned.1.call-start = ((), (), s32[]{:S(2)}) async-start(), calls=%async_computation.8 | async-start | bytes 7077888 | tf_op jit(solution)/shard_map/reduce_scatter | solution.py:351
  726.4 573.2 %reduce-scatter.6.cloned.1.call-start = ((), (), s32[]{:S(2)}) async-start(), calls=%async_computation.9 | async-start | bytes 14155776 | tf_op jit(solution)/shard_map/reduce_scatter | solution.py:379
  728.3 9.8 copy-start.35
  728.3 9.8 copy-start.99
  755.5 8.3 copy-start.65
  755.5 9.1 copy-start.66
  755.5 10.0 copy-start.67
  755.6 10.8 copy-start.68
  763.8 8.3 copy-start.95
  763.8 81.3 %copy-start.70 = (f32[1,8,256]{2,0,1:T(1,128)S(1)}, f32[1,8,256]{2,0,1:T(1,128)}, u32[]{:S(2)}) copy-start(f32[1,8,256]{2,0,1:T(1,128)} %copy-done.69) | copy-start | bytes 24580
  763.8 81.3 %copy-start.74 = (f32[1024]{0:T(1024)S(1)}, f32[1024]{0:T(1024)}, u32[]{:S(2)}) copy-start(f32[1024]{0:T(1024)} %copy-done.73) | copy-start | bytes 12292
  845.1 46.1 %copy-start.91 = (f32[2,16]{1,0:T(2,128)S(1)}, f32[2,16]{1,0:T(2,128)}, u32[]{:S(2)}) copy-start(f32[2,16]{1,0:T(2,128)} %param.49) | copy-start | bytes 388
  845.1 46.1 %copy-start.92 = (f32[2,16]{1,0:T(2,128)S(1)}, f32[2,16]{1,0:T(2,128)}, u32[]{:S(2)}) copy-start(f32[2,16]{1,0:T(2,128)} %param.57) | copy-start | bytes 388
  845.1 46.1 %copy-start.93 = (f32[2,16]{1,0:T(2,128)S(1)}, f32[2,16]{1,0:T(2,128)}, u32[]{:S(2)}) copy-start(f32[2,16]{1,0:T(2,128)} %param.65) | copy-start | bytes 388
  845.2 46.7 %copy-start.79 = (f32[1024]{0:T(1024)S(1)}, f32[1024]{0:T(1024)}, u32[]{:S(2)}) copy-start(f32[1024]{0:T(1024)} %copy-done.78) | copy-start | bytes 12292
  845.2 46.7 %copy-start.83 = (f32[2,256]{1,0:T(2,128)S(1)}, f32[2,256]{1,0:T(2,128)}, u32[]{:S(2)}) copy-start(f32[2,256]{1,0:T(2,128)} %param.48) | copy-start | bytes 6148
  845.2 46.7 %copy-start.88 = (f32[2,256]{1,0:T(2,128)S(1)}, f32[2,256]{1,0:T(2,128)}, u32[]{:S(2)}) copy-start(f32[2,256]{1,0:T(2,128)} %param.56) | copy-start | bytes 6148
  845.2 46.7 %copy-start.89 = (f32[2,256]{1,0:T(2,128)S(1)}, f32[2,256]{1,0:T(2,128)}, u32[]{:S(2)}) copy-start(f32[2,256]{1,0:T(2,128)} %param.64) | copy-start | bytes 6148
  977.3 113.2 %copy-start.40 = (f32[256,512]{0,1:T(8,128)S(1)}, f32[256,512]{0,1:T(8,128)}, u32[]{:S(2)}) copy-start(f32[256,512]{0,1:T(8,128)} %copy.378) | copy-start | bytes 1572868
  977.3 113.2 %copy-start.41 = (f32[256,512]{0,1:T(8,128)S(1)}, f32[256,512]{0,1:T(8,128)}, u32[]{:S(2)}) copy-start(f32[256,512]{0,1:T(8,128)} %copy.393) | copy-start | bytes 1572868
  977.3 113.2 %copy-start.42 = (f32[256,512]{0,1:T(8,128)S(1)}, f32[256,512]{0,1:T(8,128)}, u32[]{:S(2)}) copy-start(f32[256,512]{0,1:T(8,128)} %copy.375) | copy-start | bytes 1572868
  1094.1 8.4 copy-start.44
  1094.1 9.4 copy-start.43
  1094.1 10.4 copy-start.52
  1094.1 10.4 copy-start.53
  1108.6 191.0 %copy-start.15 = (f32[2,256,1536]{2,1,0:T(8,128)S(1)}, f32[2,256,1536]{2,1,0:T(8,128)}, u32[]{:S(2)}) copy-start(f32[2,256,1536]{2,1,0:T(8,128)} %param.46) | copy-start | bytes 9437188
  (65 other events, 213.4 us)
Sparse Core Ops, SparseCore 0:
  12.5 101.5 all-gather.3
  150.7 83.6 all-reduce.12
  237.2 176.2 all-gather.5
  416.1 96.8 all-gather.7
  551.3 83.6 all-reduce.14
  692.0 153.0 all-reduce.16
  848.7 119.1 reduce-scatter.7
  971.5 117.6 reduce-scatter.3
  1092.8 206.6 reduce-scatter.5

commit v2 on v1

--- a/solution.py
+++ b/solution.py
@@ -1,11 +1,15 @@
+import functools
 import math
 
 import jax
 import jax.numpy as jnp
 from jax import lax
+from jax.experimental import pallas as pl
+from jax.experimental.pallas import tpu as pltpu
 from jax.sharding import PartitionSpec as P
 
 HEAD_SIZE = 128
+MODEL_WIDTH = 2048
 ADAM_STEP = 3
 
 
@@ -78,7 +82,7 @@
     return (weight_next - weight, mean_next, square_next)
 
 
-def per_device(
+def plain_device(
     layer_input,
     out_grad,
     segment_ids,
@@ -408,9 +412,1181 @@
     return tuple(results)
 
 
+CORE_PAIRS = [(0, 1), (1, 0), (2, 3), (3, 2)]
+CHIP_PAIRS = [(0, 2), (2, 0), (1, 3), (3, 1)]
+FF_CHUNKS = 3
+ROW_TILE = 256
+FULL_TILE = 256
+
+
+def ring_place(place, shards):
+    place = place % shards
+    column = place // (shards // 2)
+    return 2 * (place + column * (shards - 1 - 2 * place)) + column
+
+
+def place_of(index, shards):
+    row, column = index // 2, index % 2
+    return row + column * (shards - 1 - 2 * row)
+
+
+def ring_pairs(shards, step):
+    return [
+        (ring_place(place, shards), ring_place(place + step + shards, shards))
+        for place in range(shards)
+    ]
+
+
+def spread(pieces, shards):
+    return [pieces[0]] + [
+        lax.ppermute(pieces[shards - step], "fsdp", ring_pairs(shards, step))
+        for step in range(1, shards)
+    ]
+
+
+def row_scale(values):
+    return lax.rsqrt(jnp.mean(values * values, axis=-1, keepdims=True) + EPSILON)
+
+
+def row_call(body, scalars, arrays, gains, outs, sums=0, cost=8):
+    tokens, width = arrays[0].shape
+    tiles = tokens // ROW_TILE
+    row = pl.BlockSpec((ROW_TILE, width), lambda tile, *_: (tile, 0))
+    whole = pl.BlockSpec((1, width), lambda tile, *_: (0, 0))
+    return pl.pallas_call(
+        body,
+        grid_spec=pltpu.PrefetchScalarGridSpec(
+            num_scalar_prefetch=1,
+            grid=(tiles,),
+            in_specs=[row] * len(arrays)
+            + [whole] * len(gains),
+            out_specs=[row] * len(outs) + [whole] * sums,
+        ),
+        out_shape=[jax.ShapeDtypeStruct((tokens, width), kind) for kind in outs]
+        + [jax.ShapeDtypeStruct((1, width), jnp.float32)] * sums,
+        cost_estimate=pl.CostEstimate(
+            flops=cost * tokens * width, bytes_accessed=3 * cost * tokens * width // 2, transcendentals=0
+        ),
+        name=body.__name__,
+    )(scalars, *arrays, *gains)
+
+
+def turned_in(scalars, x_ref, g_ref, gain_ref, xr_ref, gr_ref, n_ref):
+    shards = scalars.shape[0] - 1
+    width = x_ref.shape[1] // shards
+    scale = row_scale(x_ref[...].astype(jnp.float32))
+    for at in range(shards):
+        source = pl.ds(pl.multiple_of(scalars[at] * width, 128), width)
+        target = slice(at * width, (at + 1) * width)
+        values = x_ref[:, source]
+        xr_ref[:, target] = values
+        gr_ref[:, target] = g_ref[:, source]
+        n_ref[:, target] = (values.astype(jnp.float32) * scale * gain_ref[:, target]).astype(
+            n_ref.dtype
+        )
+
+
+def layer_out(scalars, mid_ref, came_ref, out_ref):
+    shards = scalars.shape[0] - 1
+    width = mid_ref.shape[1] // shards
+    value = mid_ref[...] + came_ref[...].astype(jnp.float32)
+    for at in range(shards):
+        out_ref[:, pl.ds(pl.multiple_of(scalars[at] * width, 128), width)] = value[
+            :, at * width : (at + 1) * width
+        ]
+
+
+def norm_grad(values, grad, gain, sum_ref):
+    scale = row_scale(values)
+    unit = values * scale
+    inner = grad * gain
+
+    @pl.when(pl.program_id(0) == 0)
+    def _():
+        sum_ref[...] = jnp.zeros_like(sum_ref)
+
+    sum_ref[...] += jnp.sum(grad * unit, axis=0, keepdims=True)
+    return scale * (inner - unit * jnp.mean(inner * unit, axis=-1, keepdims=True))
+
+
+def second_back(scalars, mid_ref, g_ref, came_ref, gain_ref, dx_ref, low_ref, sum_ref):
+    grad = came_ref[...].astype(jnp.float32)
+    value = g_ref[...].astype(jnp.float32) + norm_grad(mid_ref[...], grad, gain_ref[...], sum_ref)
+    dx_ref[...] = value
+    low_ref[...] = value.astype(low_ref.dtype)
+
+
+def first_back(scalars, dx_ref, x_ref, came_ref, gain_ref, out_ref, sum_ref):
+    shards = scalars.shape[0] - 1
+    width = x_ref.shape[1] // shards
+    grad = came_ref[...].astype(jnp.float32)
+    value = dx_ref[...] + norm_grad(
+        x_ref[...].astype(jnp.float32), grad, gain_ref[...], sum_ref
+    )
+    for at in range(shards):
+        out_ref[:, pl.ds(pl.multiple_of(scalars[at] * width, 128), width)] = value[
+            :, at * width : (at + 1) * width
+        ]
+
+
+def full_call(body, scalars, lefts, matrix, window, outs, halves, name):
+    tokens = lefts[0].shape[0]
+    tiles = tokens // FULL_TILE
+    half = tiles // 2
+    columns, at = window
+
+    def turned(step, scalars):
+        return (lax.rem(step + scalars[scalars.shape[0] - 1] * half, tiles), 0)
+
+    def kernel(scalars, *refs):
+        left_refs, whole = refs[: len(lefts)], refs[len(lefts)]
+        out_refs = refs[len(lefts) + 1 : len(lefts) + 1 + len(outs)]
+        half_refs = refs[len(lefts) + 1 + len(outs) :]
+        step = pl.program_id(0)
+        values = body(left_refs, whole, out_refs)
+        for place, value in enumerate(values):
+            kept, sent = half_refs[2 * place : 2 * place + 2]
+
+            @pl.when(step < half)
+            def _():
+                kept[...] = value.astype(kept.dtype)
+
+            @pl.when(step >= half)
+            def _():
+                sent[...] = value.astype(sent.dtype)
+
+    def row_spec(width):
+        return pl.BlockSpec((FULL_TILE, width), turned)
+
+    half_out = []
+    for width, _ in halves:
+        half_out.append(
+            pl.BlockSpec((FULL_TILE, width), lambda step, _: (jnp.minimum(step, half - 1), 0))
+        )
+        half_out.append(
+            pl.BlockSpec((FULL_TILE, width), lambda step, _: (jnp.maximum(step - half, 0), 0))
+        )
+    work = 2 * tokens * matrix.shape[0] * columns
+    return pl.pallas_call(
+        kernel,
+        grid_spec=pltpu.PrefetchScalarGridSpec(
+            num_scalar_prefetch=1,
+            grid=(tiles,),
+            in_specs=[row_spec(left.shape[1]) for left in lefts]
+            + [pl.BlockSpec((matrix.shape[0], columns), lambda step, _: (0, at))],
+            out_specs=[row_spec(width) for width, _ in outs] + half_out,
+        ),
+        out_shape=[jax.ShapeDtypeStruct((tokens, width), kind) for width, kind in outs]
+        + [
+            jax.ShapeDtypeStruct((tokens // 2, width), kind)
+            for width, kind in halves
+            for _ in range(2)
+        ],
+        cost_estimate=pl.CostEstimate(flops=work, bytes_accessed=work // 250, transcendentals=0),
+        name=name,
+    )(scalars, *lefts, matrix)
+
+
+def rows_times(left, right):
+    return jnp.dot(left, right, preferred_element_type=jnp.float32)
+
+
+def project_body(cuts, lefts, whole, outs):
+    start = 0
+    for out, stop in zip(outs, cuts):
+        out[...] = rows_times(lefts[0][...], whole[:, start:stop]).astype(out.dtype)
+        start = stop
+    return []
+
+
+def back_body(lefts, whole, outs):
+    start, value = 0, None
+    for left in lefts:
+        stop = start + left.shape[1]
+        term = contract_cols(left[...], whole[:, start:stop])
+        value = term if value is None else value + term
+        start = stop
+    return [value]
+
+
+def adam_body(places, grad_ref, *refs):
+    count = len({place[0] for place in places})
+    states, outs = refs[: 3 * count], refs[3 * count :]
+    start = 0
+    for array, plane in places:
+        at = (Ellipsis,) if plane is None else (plane,)
+        weight, mean, square = (states[3 * array + kind][at] for kind in range(3))
+        stop = start + weight.shape[-1]
+        grad = grad_ref[:, start:stop]
+        step, mean_next, square_next = adam_step(
+            weight, grad, mean, square, MATRIX_RATE, WEIGHT_DECAY
+        )
+        for kind, result in enumerate((grad, step, mean_next, square_next)):
+            outs[4 * array + kind][at] = result
+        start = stop
+
+
+def adam_update(grads, places, states, parts=None):
+    rows, columns = grads.shape[-2:]
+    tile = min(64, rows)
+    if parts is None:
+        grads, parts = grads[None], 1
+
+    def window(array):
+        lead = array.shape[:-2]
+        shape = lead + (tile, array.shape[-1] // parts)
+        return pl.BlockSpec(shape, lambda part, at: (0,) * len(lead) + (at, part))
+
+    flat = [array for group in states for array in group]
+    out_like = [group[0] for group in states for _ in range(4)]
+    return pl.pallas_call(
+        functools.partial(adam_body, places),
+        grid=(parts, rows // tile),
+        in_specs=[pl.BlockSpec((None, tile, columns), lambda part, at: (part, at, 0))]
+        + [window(array) for array in flat],
+        out_specs=[window(array) for array in out_like],
+        out_shape=[jax.ShapeDtypeStruct(array.shape, jnp.float32) for array in out_like],
+        cost_estimate=pl.CostEstimate(
+            flops=20 * parts * rows * columns,
+            bytes_accessed=32 * parts * rows * columns,
+            transcendentals=0,
+        ),
+        name="adam_update",
+    )(grads, *flat)
+
+
+class Hops:
+    def __init__(self, shards):
+        self.shards = shards
+        place = place_of(lax.axis_index("fsdp"), shards)
+        self.neighbours = [
+            {"fsdp": ring_place(place + shards + step, shards)} for step in (1, -1)
+        ]
+        tensor = lax.axis_index("tensor")
+        self.core = lax.rem(tensor, 2)
+        chip = tensor // 2
+        self.partner = {"tensor": 2 * chip + 1 - self.core}
+        self.across = {"tensor": 2 * (1 - chip) + self.core}
+
+    def meet(self, others):
+        barrier = pltpu.get_barrier_semaphore()
+        for other in others:
+            pl.semaphore_signal(
+                barrier, inc=1, device_id=other, device_id_type=pl.DeviceIdType.MESH
+            )
+        pl.semaphore_wait(barrier, len(others))
+
+
+def remote(source, target, sent, arrived, device):
+    return pltpu.make_async_remote_copy(
+        src_ref=source,
+        dst_ref=target,
+        send_sem=sent,
+        recv_sem=arrived,
+        device_id=device,
+        device_id_type=pl.DeviceIdType.MESH,
+    )
+
+
+class RingGather:
+    def __init__(self, hops, own, slots, sems, forward):
+        legs = hops.shards // 2
+        self.reach = (legs, legs - 1) if forward else (legs - 1, legs)
+        self.hops, self.own, self.slots, self.sems = hops, own, slots, sems
+
+    def copy(self, way, step):
+        shards = self.hops.shards
+        source, target = (step - 1, step) if way == 0 else (shards - step + 1, shards - step)
+        return remote(
+            self.own if step == 1 else self.slots.at[source],
+            self.slots.at[target],
+            self.sems[0].at[way, step - 1],
+            self.sems[1].at[way, step - 1],
+            self.hops.neighbours[way],
+        )
+
+    def hop(self, step):
+        for way in range(2):
+            if 1 < step <= self.reach[way] + 1:
+                self.copy(way, step - 1).wait_recv()
+            if step <= self.reach[way]:
+                self.copy(way, step).start()
+
+    def close(self):
+        for way in range(2):
+            for step in range(1, self.reach[way] + 1):
+                self.copy(way, step).wait_send()
+
+
+def by_rows(count, body):
+    @pl.loop(0, count // ROW_STEP)
+    def _(step):
+        body(pl.ds(pl.multiple_of(step * ROW_STEP, ROW_STEP), ROW_STEP))
+
+
+class RingScatter:
+    SLOTS = 3
+
+    def __init__(self, hops, partial, sent, came, sems, credits, jobs, plan):
+        self.hops, self.partial, self.sent, self.came = hops, partial, sent, came
+        self.sems, self.credits, self.jobs = sems, credits, jobs
+        self.total = [sum(job[way] for job in jobs) for way in range(2)]
+        self.number = [{}, {}]
+        for job, step in plan:
+            for way in range(2):
+                hop = step - (max(jobs[job]) - jobs[job][way])
+                if hop >= 1:
+                    self.number[way][job, hop] = len(self.number[way])
+
+    def copy(self, way, number):
+        slot = number % self.SLOTS
+        return remote(
+            self.sent.at[way, slot],
+            self.came.at[way, slot],
+            self.sems[0].at[way, slot],
+            self.sems[1].at[way, slot],
+            self.hops.neighbours[way],
+        )
+
+    def add(self, way, job, hop, base, out):
+        number = self.number[way][job, hop]
+        self.copy(way, number).wait_recv()
+        slot = number % self.SLOTS
+
+        def body(rows):
+            out[rows, :] = (
+                base[rows, :].astype(jnp.float32) + self.came[way, slot, rows].astype(jnp.float32)
+            ).astype(out.dtype)
+
+        by_rows(out.shape[0], body)
+        if number + self.SLOTS < self.total[way]:
+            pl.semaphore_signal(
+                self.credits.at[way],
+                inc=1,
+                device_id=self.hops.neighbours[1 - way],
+                device_id_type=pl.DeviceIdType.MESH,
+            )
+
+    def hop(self, job, step):
+        longest = max(self.jobs[job])
+        for way in range(2):
+            reach = self.jobs[job][way]
+            hop = step - (longest - reach)
+            if hop < 1 or hop > reach:
+                continue
+            distance = reach - hop + 1
+            number = self.number[way][job, hop]
+            slot = number % self.SLOTS
+            if number >= self.SLOTS:
+                self.copy(way, number - self.SLOTS).wait_send()
+            self.partial(
+                job,
+                self.hops.shards - distance if way == 0 else distance,
+                self.sent.at[way, slot],
+            )
+            if hop > 1:
+                own = self.sent.at[way, slot]
+                self.add(way, job, hop - 1, own, own)
+            if number >= self.SLOTS:
+                pl.semaphore_wait(self.credits.at[way], 1)
+            self.copy(way, number).start()
+
+    def last(self, job, own):
+        self.partial(job, 0, own)
+        for way in range(2):
+            self.add(way, job, self.jobs[job][way], own, own)
+
+    def close(self):
+        for way in range(2):
+            for number in range(max(0, self.total[way] - self.SLOTS), self.total[way]):
+                self.copy(way, number).wait_send()
+
+
+class CoreSum:
+    def __init__(self, hops, sent, kept, first, chip, second, out, sems):
+        self.hops, self.sent, self.kept, self.first = hops, sent, kept, first
+        self.chip, self.second, self.out, self.sems = chip, second, out, sems
+        self.half = chip.shape[0]
+
+    def copy(self, stage):
+        rows = self.out.at[pl.ds(pl.multiple_of(self.hops.core * self.half, 128), self.half)]
+        source, target, device = (
+            (self.sent, self.first, self.hops.partner),
+            (self.chip, self.second, self.hops.across),
+            (self.chip, rows, self.hops.partner),
+        )[stage]
+        return remote(source, target, self.sems.at[0, stage], self.sems.at[1, stage], device)
+
+    def local(self):
+        rows = self.out.at[pl.ds(pl.multiple_of(self.hops.core * self.half, 128), self.half)]
+        return pltpu.make_async_copy(self.chip, rows, self.sems.at[0, 3])
+
+    def add(self, left, right):
+        def body(rows):
+            self.chip[rows, :] = (
+                left[rows, :].astype(jnp.float32) + right[rows, :].astype(jnp.float32)
+            ).astype(jnp.bfloat16)
+
+        by_rows(self.half, body)
+
+    def start(self):
+        self.copy(0).start()
+
+    def to_chip(self):
+        self.copy(0).wait_recv()
+        self.add(self.kept, self.first)
+        self.copy(1).start()
+
+    def to_all(self):
+        self.copy(1).wait()
+        self.add(self.chip, self.second)
+        self.copy(2).start()
+        self.local().start()
+
+    def done(self):
+        self.copy(0).wait_send()
+        self.copy(2).wait()
+        self.local().wait()
+
+
+RING_LIMIT = 66500000
+
+
+def gather_body(shards, own_ref, small_ref, out_ref, few_ref, *sems):
+    hops = Hops(shards)
+    hops.meet(hops.neighbours)
+    few = RingGather(hops, small_ref, few_ref, sems[2:4], True)
+    big = RingGather(hops, own_ref, out_ref, sems[0:2], True)
+    rings = (few, big)
+    copies = [
+        pltpu.make_async_copy(own_ref, out_ref.at[0], sems[4].at[0]),
+        pltpu.make_async_copy(small_ref, few_ref.at[0], sems[4].at[1]),
+    ]
+    for step in range(1, shards // 2 + 2):
+        for ring in rings:
+            ring.hop(step)
+        if step == 1:
+            for copy in copies:
+                copy.start()
+    for ring in rings:
+        ring.close()
+    for copy in copies:
+        copy.wait()
+
+
+def gather_call(own, small, shards):
+    legs = shards // 2
+    return pl.pallas_call(
+        functools.partial(gather_body, shards),
+        in_specs=[pl.BlockSpec(memory_space=pl.ANY)] * 2,
+        out_specs=[pl.BlockSpec(memory_space=pl.ANY)] * 2,
+        out_shape=[
+            jax.ShapeDtypeStruct((shards, *array.shape), array.dtype) for array in (own, small)
+        ],
+        scratch_shapes=[pltpu.SemaphoreType.DMA((2, legs))] * 4
+        + [pltpu.SemaphoreType.DMA((2,))],
+        compiler_params=pltpu.CompilerParams(collective_id=0, has_side_effects=True),
+        name="gather_ring",
+    )(own, small)
+
+
+FF_TILE = 256
+ROW_STEP = 32
+
+
+def ff_kernel(shards, parts, *refs):
+    (sent_ref, kept_ref, x_ref, grad_ref, gain_ref, own_ref) = refs[:6]
+    (mid_ref, norm_out, normsum_ref, downsum_ref, grads_ref, whole_ref) = refs[6:12]
+    (acts, whole, pairs, norm_acc, r_sent, r_came, total) = refs[12:19]
+    (out_half, kept_half, chip, first) = refs[19:23]
+    seconds = refs[23:25]
+    (x_tile, mid_tile) = refs[25:27]
+    (ag_sent, ag_came, rs_sent, rs_came, credits, sums, local) = refs[27:]
+    hops = Hops(shards)
+    hops.meet([*hops.neighbours, hops.partner, hops.across])
+    core = hops.core
+    tokens, wide = x_ref.shape
+    half = tokens // 2
+    columns = pairs.shape[2]
+    width = wide // shards
+    legs = shards // 2
+    gathers = [
+        RingGather(
+            hops,
+            own_ref.at[part],
+            whole_ref.at[part],
+            (ag_sent.at[part], ag_came.at[part]),
+            part % 2 == 0,
+        )
+        for part in range(parts)
+    ]
+
+    def partial(job, at, out):
+        @pl.loop(0, 3)
+        def _(pair):
+            left = acts[pair // 2, :, at * width : (at + 1) * width]
+            right = pairs[3 * job + pair]
+            out[:, pl.ds(pl.multiple_of(pair * columns, 128), columns)] = contract_rows(
+                left, right
+            ).astype(out.dtype)
+
+    scatter = RingScatter(
+        hops,
+        partial,
+        r_sent,
+        r_came,
+        (rs_sent, rs_came),
+        credits,
+        [(legs, legs - 1) if part % 2 == 0 else (legs - 1, legs) for part in range(parts)],
+        [(part, step) for part in range(parts) for step in range(1, legs + 1)],
+    )
+    attention = CoreSum(
+        hops, sent_ref, kept_half, first, chip, seconds[0], acts.at[0], sums.at[0]
+    )
+    attention.start()
+    take_kept = pltpu.make_async_copy(kept_ref, kept_half, local.at[0])
+    take_grad = pltpu.make_async_copy(grad_ref, acts.at[1], local.at[1])
+    take_kept.start()
+    take_grad.start()
+    gathers[0].hop(1)
+    take_kept.wait()
+    attention.to_chip()
+    gathers[0].hop(2)
+    gathers[0].hop(3)
+    gathers[0].hop(4)
+    gathers[1].hop(1)
+    attention.to_all()
+    attention.done()
+
+    @pl.loop(0, tokens // FF_TILE)
+    def _(tile):
+        rows = pl.ds(pl.multiple_of(tile * FF_TILE, FF_TILE), FF_TILE)
+        take = pltpu.make_async_copy(x_ref.at[rows], x_tile, local.at[2])
+        take.start()
+        take.wait()
+        middle = x_tile[...].astype(jnp.float32) + acts[0, rows, :].astype(jnp.float32)
+        mid_tile[...] = middle
+        put = pltpu.make_async_copy(mid_tile, mid_ref.at[rows], local.at[2])
+        put.start()
+        acts[0, rows, :] = (middle * row_scale(middle) * gain_ref[...]).astype(jnp.bfloat16)
+        put.wait()
+
+    gathers[0].hop(5)
+    take_grad.wait()
+
+    def load(part):
+        copies = [
+            pltpu.make_async_copy(
+                own_ref.at[part] if at == 0 else whole_ref.at[part, at],
+                whole.at[pl.ds(at * width, width)],
+                local.at[3 + at],
+            )
+            for at in range(shards)
+        ]
+        for copy in copies:
+            copy.start()
+        for copy in copies:
+            copy.wait()
+
+    def tiles(part, start, stop):
+        @pl.loop(start, stop)
+        def _(tile):
+            rows = pl.ds(pl.multiple_of(tile * FF_TILE, FF_TILE), FF_TILE)
+            norm = acts[0, rows, :]
+            grad = acts[1, rows, :]
+            gate_proj = rows_times(norm, whole[:, :columns])
+            up_proj = rows_times(norm, whole[:, columns : 2 * columns])
+            hidden_grad = rows_times(grad, whole[:, 2 * columns :])
+            gate = 1.0 / (1.0 + jnp.exp(-gate_proj))
+            swish = gate_proj * gate
+            gate_grad = (
+                hidden_grad * up_proj * (gate * (1.0 + gate_proj * (1.0 - gate)))
+            ).astype(jnp.bfloat16)
+            up_grad = (hidden_grad * swish).astype(jnp.bfloat16)
+            pairs[3 * part, rows, :] = gate_grad
+            pairs[3 * part + 1, rows, :] = up_grad
+            pairs[3 * part + 2, rows, :] = (swish * up_proj).astype(jnp.bfloat16)
+            value = contract_cols(gate_grad, whole[:, :columns]) + contract_cols(
+                up_grad, whole[:, columns : 2 * columns]
+            )
+            if part > 0:
+                value += norm_acc[rows, :]
+            norm_acc[rows, :] = value
+
+    count = tokens // FF_TILE
+    load(0)
+    tiles(0, 0, 2)
+    gathers[1].hop(2)
+    tiles(0, 2, count)
+    gathers[1].hop(3)
+    gathers[1].hop(4)
+    gathers[2].hop(1)
+    gathers[1].hop(5)
+    load(1)
+    tiles(1, 0, 2)
+    gathers[2].hop(2)
+    tiles(1, 2, count)
+    gathers[2].hop(3)
+    scatter.hop(0, 1)
+    gathers[2].hop(4)
+    scatter.hop(0, 2)
+    gathers[2].hop(5)
+    load(2)
+    tiles(2, 0, 2)
+    scatter.hop(0, 3)
+    tiles(2, 2, count)
+    scatter.hop(0, 4)
+    scatter.hop(1, 1)
+
+    def finish(part):
+        scatter.last(part, total)
+        put = pltpu.make_async_copy(total, grads_ref.at[part], local.at[2])
+        put.start()
+        put.wait()
+
+    mine = pl.ds(pl.multiple_of(core * half, 128), half)
+    other = pl.ds(pl.multiple_of((1 - core) * half, 128), half)
+    out_half[...] = norm_acc[other, :].astype(jnp.bfloat16)
+    norm_sum = CoreSum(
+        hops, out_half, norm_acc.at[mine], first, chip, seconds[1], normsum_ref, sums.at[1]
+    )
+    norm_sum.start()
+    finish(0)
+    scatter.hop(1, 2)
+    norm_sum.to_chip()
+
+    downs = [
+        pltpu.make_async_copy(
+            (own_ref.at[part] if at == 0 else whole_ref.at[part, at]).at[
+                :, pl.ds(2 * columns, columns)
+            ],
+            whole.at[pl.ds(at * width, width), pl.ds(part * columns, columns)],
+            local.at[3 + at],
+        )
+        for part in range(parts)
+        for at in range(shards)
+    ]
+    for part in range(parts):
+        for copy in downs[part * shards : (part + 1) * shards]:
+            copy.start()
+        for copy in downs[part * shards : (part + 1) * shards]:
+            copy.wait()
+    scatter.hop(1, 3)
+    scatter.hop(1, 4)
+    scatter.hop(2, 1)
+    norm_sum.to_all()
+    finish(1)
+    scatter.hop(2, 2)
+    norm_sum.done()
+
+    def down_tile(tile, offset):
+        rows = pl.ds(pl.multiple_of(offset + tile * FF_TILE, FF_TILE), FF_TILE)
+        value = contract_cols(pairs[2, rows, :], whole[:, :columns])
+        for part in range(1, parts):
+            value += contract_cols(
+                pairs[3 * part + 2, rows, :], whole[:, part * columns : (part + 1) * columns]
+            )
+        return value
+
+    @pl.loop(0, half // FF_TILE)
+    def _(tile):
+        rows = pl.ds(pl.multiple_of(tile * FF_TILE, FF_TILE), FF_TILE)
+        out_half[rows, :] = down_tile(tile, (1 - core) * half).astype(jnp.bfloat16)
+
+    down_sum = CoreSum(
+        hops, out_half, kept_half, first, chip, seconds[0], downsum_ref, sums.at[2]
+    )
+    down_sum.start()
+
+    @pl.loop(0, half // FF_TILE)
+    def _(tile):
+        rows = pl.ds(pl.multiple_of(tile * FF_TILE, FF_TILE), FF_TILE)
+        kept_half[rows, :] = down_tile(tile, core * half).astype(jnp.bfloat16)
+
+    down_sum.to_chip()
+    scatter.hop(2, 3)
+    scatter.hop(2, 4)
+    down_sum.to_all()
+    put_norm = pltpu.make_async_copy(acts.at[0], norm_out, local.at[0])
+    put_norm.start()
+    finish(2)
+    down_sum.done()
+    put_norm.wait()
+    for gather in gathers:
+        gather.close()
+    scatter.close()
+
+
+def ff_call(sent, kept, rows, grad, gain, own):
+    parts, width, columns3 = own.shape
+    tokens, wide = rows.shape
+    shards = wide // width
+    columns = columns3 // 3
+    half = tokens // 2
+    legs = shards // 2
+    low = jnp.bfloat16
+    anywhere = pl.BlockSpec(memory_space=pl.ANY)
+    slots = RingScatter.SLOTS
+    return pl.pallas_call(
+        functools.partial(ff_kernel, shards, parts),
+        in_specs=[anywhere] * 4 + [pl.BlockSpec(memory_space=pltpu.VMEM)] + [anywhere],
+        out_specs=[anywhere] * 6,
+        out_shape=[
+            jax.ShapeDtypeStruct((tokens, wide), jnp.float32),
+            jax.ShapeDtypeStruct((tokens, wide), low),
+            jax.ShapeDtypeStruct((tokens, wide), low),
+            jax.ShapeDtypeStruct((tokens, wide), low),
+            jax.ShapeDtypeStruct((parts, width, columns3), jnp.float32),
+            jax.ShapeDtypeStruct((parts, shards, width, columns3), low),
+        ],
+        scratch_shapes=[
+            pltpu.VMEM((2, tokens, wide), low),
+            pltpu.VMEM((wide, columns3), low),
+            pltpu.VMEM((3 * parts, tokens, columns), low),
+            pltpu.VMEM((tokens, wide), jnp.float32),
+            pltpu.VMEM((2, slots, width, columns3), low),
+            pltpu.VMEM((2, slots, width, columns3), low),
+            pltpu.VMEM((width, columns3), jnp.float32),
+        ]
+        + [pltpu.VMEM((half, wide), low)] * 6
+        + [
+            pltpu.VMEM((FF_TILE, wide), low),
+            pltpu.VMEM((FF_TILE, wide), jnp.float32),
+            pltpu.SemaphoreType.DMA((parts, 2, legs)),
+            pltpu.SemaphoreType.DMA((parts, 2, legs)),
+            pltpu.SemaphoreType.DMA((2, slots)),
+            pltpu.SemaphoreType.DMA((2, slots)),
+            pltpu.SemaphoreType.REGULAR((2,)),
+            pltpu.SemaphoreType.DMA((3, 2, 4)),
+            pltpu.SemaphoreType.DMA((3 + shards,)),
+        ],
+        compiler_params=pltpu.CompilerParams(
+            collective_id=1, has_side_effects=True, vmem_limit_bytes=RING_LIMIT
+        ),
+        name="ff_ring",
+    )(sent, kept, rows, grad, gain, own)
+
+
+def tail_kernel(shards, jobs, *refs):
+    (sent_ref, kept_ref, norm_ref, grad_ref) = refs[:4]
+    rights = refs[4:8]
+    (sum_ref, grads_ref, acts, r_sent, r_came, total) = refs[8:14]
+    (kept_half, chip, first, second) = refs[14:18]
+    (rs_sent, rs_came, credits, sums, local) = refs[18:]
+    hops = Hops(shards)
+    hops.meet([*hops.neighbours, hops.partner, hops.across])
+    wide = norm_ref.shape[1]
+    width = wide // shards
+    legs = shards // 2
+
+    def partial(job, at, out):
+        start = 0
+        for left, right in jobs[job]:
+            stop = start + rights[right].shape[1]
+            out[:, start:stop] = contract_rows(
+                acts[left, :, at * width : (at + 1) * width], rights[right][...]
+            ).astype(out.dtype)
+            start = stop
+
+    scatter = RingScatter(
+        hops,
+        partial,
+        r_sent,
+        r_came,
+        (rs_sent, rs_came),
+        credits,
+        [(legs, legs - 1) if job % 2 == 0 else (legs - 1, legs) for job in range(len(jobs))],
+        [(job, step) for step in range(1, legs + 1) for job in range(len(jobs))],
+    )
+    take = [
+        pltpu.make_async_copy(ref, target, local.at[at])
+        for at, (ref, target) in enumerate(
+            [(kept_ref, kept_half), (norm_ref, acts.at[0]), (grad_ref, acts.at[1])]
+        )
+    ]
+    norm_sum = CoreSum(
+        hops, sent_ref, kept_half, first, chip, second, sum_ref, sums.at[0]
+    )
+    norm_sum.start()
+    for copy in take:
+        copy.start()
+    for copy in take:
+        copy.wait()
+    scatter.hop(0, 1)
+    scatter.hop(1, 1)
+    norm_sum.to_chip()
+    scatter.hop(0, 2)
+    scatter.hop(1, 2)
+    scatter.hop(0, 3)
+    scatter.hop(1, 3)
+    scatter.hop(0, 4)
+    scatter.hop(1, 4)
+    norm_sum.to_all()
+    for job in range(2):
+        scatter.last(job, total)
+        put = pltpu.make_async_copy(total, grads_ref.at[job], local.at[0])
+        put.start()
+        put.wait()
+    norm_sum.done()
+    scatter.close()
+
+
+def tail_call(sent, kept, norm, grad, rights, jobs, shards):
+    tokens, wide = norm.shape
+    half, width, legs = tokens // 2, wide // shards, shards // 2
+    columns = sum(rights[right].shape[1] for _, right in jobs[0])
+    low = jnp.bfloat16
+    anywhere = pl.BlockSpec(memory_space=pl.ANY)
+    slots = RingScatter.SLOTS
+    return pl.pallas_call(
+        functools.partial(tail_kernel, shards, jobs),
+        in_specs=[anywhere] * 4 + [pl.BlockSpec(memory_space=pltpu.VMEM)] * len(rights),
+        out_specs=[anywhere] * 2,
+        out_shape=[
+            jax.ShapeDtypeStruct((tokens, wide), low),
+            jax.ShapeDtypeStruct((len(jobs), width, columns), jnp.float32),
+        ],
+        scratch_shapes=[
+            pltpu.VMEM((2, tokens, wide), low),
+            pltpu.VMEM((2, slots, width, columns), low),
+            pltpu.VMEM((2, slots, width, columns), low),
+            pltpu.VMEM((width, columns), jnp.float32),
+        ]
+        + [pltpu.VMEM((half, wide), low)] * 4
+        + [
+            pltpu.SemaphoreType.DMA((2, slots)),
+            pltpu.SemaphoreType.DMA((2, slots)),
+            pltpu.SemaphoreType.REGULAR((2,)),
+            pltpu.SemaphoreType.DMA((1, 2, 4)),
+            pltpu.SemaphoreType.DMA((3,)),
+        ],
+        compiler_params=pltpu.CompilerParams(
+            collective_id=2, has_side_effects=True, vmem_limit_bytes=48 * 1024 * 1024
+        ),
+        name="tail_ring",
+    )(sent, kept, norm, grad, *rights)
+
+
+def ring_device(
+    shards,
+    layer_input,
+    out_grad,
+    segment_ids,
+    query_weight,
+    key_weight,
+    value_matrix,
+    output_weight,
+    gate_up_weight,
+    down_weight,
+    norm_gains,
+    headnorm_gains,
+    query_weight_mean,
+    key_weight_first_moment,
+    value_weight_first_moment,
+    output_weight_mean,
+    gate_up_weight_mean,
+    down_weight_mean,
+    norm_gains_mean,
+    headnorm_gains_mean,
+    query_weight_square,
+    key_weight_second_moment,
+    value_weight_second_moment,
+    output_weight_square,
+    gate_up_weight_square,
+    down_weight_square,
+    norm_gains_square,
+    headnorm_gains_square,
+):
+    place = place_of(lax.axis_index("fsdp"), shards)
+    core = lax.axis_index("tensor") % 2
+    turn = jnp.stack([ring_place(place - at + shards, shards) for at in range(shards)])
+    turn = turn.astype(jnp.int32)
+    scalars = jnp.concatenate([turn, core[None].astype(jnp.int32)])
+    back = (place - place_of(jnp.arange(shards), shards)) % shards
+
+    gain_cols, head_cols = norm_gains.shape[1], headnorm_gains.shape[1]
+    low = jnp.bfloat16
+    packed_token_count, width = layer_input.shape
+    query_cols, key_cols = query_weight.shape[1], key_weight.shape[1]
+    local_query = query_cols // HEAD_SIZE
+    local_groups = key_cols // HEAD_SIZE
+    query_group_width = local_query // local_groups
+    score_scale = 1.0 / math.sqrt(HEAD_SIZE)
+    chunk_cols = down_weight.shape[1] // FF_CHUNKS
+    states = [
+        (query_weight, query_weight_mean, query_weight_square),
+        (key_weight, key_weight_first_moment, key_weight_second_moment),
+        (value_matrix, value_weight_first_moment, value_weight_second_moment),
+        (output_weight, output_weight_mean, output_weight_square),
+        (gate_up_weight, gate_up_weight_mean, gate_up_weight_square),
+        (down_weight, down_weight_mean, down_weight_square),
+        (norm_gains, norm_gains_mean, norm_gains_square),
+        (headnorm_gains, headnorm_gains_mean, headnorm_gains_square),
+    ]
+
+    attention_block = jnp.concatenate(
+        [
+            query_weight.astype(low),
+            key_weight.astype(low),
+            value_matrix.astype(low),
+            output_weight.astype(low),
+        ],
+        axis=1,
+    )
+    own_gains = jnp.concatenate([norm_gains, headnorm_gains], axis=1).astype(low)
+    own_gains = jnp.pad(own_gains, ((0, 14), (0, -own_gains.shape[1] % 128)))
+    attention_full, gains = gather_call(attention_block, own_gains, shards)
+    attention_full = attention_full.reshape(width, -1)
+    gains = jnp.swapaxes(gains[:, :2].astype(jnp.float32), 0, 1)
+    norm_gain = gains[:, :, :gain_cols].reshape(2, 1, -1)
+    head_gain = gains[:, :, gain_cols : gain_cols + head_cols][:, back].reshape(2, -1)
+    inward_window = (query_cols + 2 * key_cols, 0)
+    outward_window = (query_cols, (query_cols + 2 * key_cols) // query_cols)
+    ff_block = jnp.stack(
+        [
+            jnp.concatenate(
+                [
+                    gate_up_weight[0, :, cols].astype(low),
+                    gate_up_weight[1, :, cols].astype(low),
+                    down_weight[:, cols].astype(low),
+                ],
+                axis=1,
+            )
+            for cols in (
+                slice(chunk * chunk_cols, (chunk + 1) * chunk_cols) for chunk in range(FF_CHUNKS)
+            )
+        ]
+    )
+    token_positions = positions_of(segment_ids)
+    token_index = jnp.arange(packed_token_count, dtype=jnp.int32)
+
+    def head_map(projected, gain, heads):
+        return rotary_embedding(
+            root_mean_scale(projected.reshape(packed_token_count, heads, HEAD_SIZE)) * gain,
+            token_positions,
+        )
+
+    input_rows, grad_low, normed_one = row_call(
+        turned_in, scalars, [layer_input, out_grad], [norm_gain[0]], [low, low, low]
+    )
+    query_proj, key_projected, value_projected = full_call(
+        functools.partial(
+            project_body, (query_cols, query_cols + key_cols, query_cols + 2 * key_cols)
+        ),
+        scalars,
+        [normed_one],
+        attention_full,
+        inward_window,
+        [(query_cols, jnp.float32), (key_cols, jnp.float32), (key_cols, low)],
+        [],
+        "project",
+    )
+    query_heads = (
+        head_map(query_proj, head_gain[0], local_query)
+        .astype(low)
+        .reshape(packed_token_count, local_groups, query_group_width, HEAD_SIZE)
+    )
+    per_head_keys = head_map(key_projected, head_gain[1], local_groups).astype(low)
+    per_head_values = value_projected.reshape(packed_token_count, local_groups, HEAD_SIZE)
+    block_rows = min(512, packed_token_count)
+    block_count = packed_token_count // block_rows
+
+    def block_scores(row_start, row_stop):
+        raw_scores = (
+            jnp.einsum(
+                "qhgd,khd->hgqk",
+                query_heads[row_start:row_stop],
+                per_head_keys[:row_stop],
+                preferred_element_type=jnp.float32,
+            )
+            * score_scale
+        )
+        allowed = (segment_ids[row_start:row_stop, None] == segment_ids[None, :row_stop]) & (
+            token_index[None, :row_stop] <= token_index[row_start:row_stop, None]
+        )
+        return jnp.where(allowed, raw_scores, MASKED)
+
+    mixed_blocks = []
+    log_sums = []
+    for block_index in range(block_count):
+        row_start = block_index * block_rows
+        row_stop = row_start + block_rows
+        scores = block_scores(row_start, row_stop)
+        row_max = jnp.max(scores, axis=-1, keepdims=True)
+        exponent = jnp.exp(scores - row_max)
+        row_sum = jnp.sum(exponent, axis=-1, keepdims=True)
+        weights_block = (exponent / row_sum).astype(low)
+        log_sums.append(row_max + jnp.log(row_sum))
+        mixed_blocks.append(
+            jnp.einsum(
+                "hgqk,khd->qhgd",
+                weights_block,
+                per_head_values[:row_stop],
+                preferred_element_type=jnp.float32,
+            )
+        )
+    mixed = (
+        jnp.concatenate(mixed_blocks, axis=0)
+        .reshape(packed_token_count, local_query * HEAD_SIZE)
+        .astype(low)
+    )
+    kept, sent = full_call(
+        back_body, scalars, [mixed], attention_full, outward_window, [], [(width, low)], "attention_out"
+    )
+    middle, normed_two, norm_sum, down_sum, ff_sums, _ = ff_call(
+        sent, kept, input_rows, grad_low, norm_gain[1], ff_block
+    )
+    middle_grad, middle_grad_low, gain_two_grad = row_call(
+        second_back,
+        scalars,
+        [middle, grad_low, norm_sum],
+        [norm_gain[1]],
+        [jnp.float32, low],
+        sums=1,
+    )
+    (mixed_grad,) = full_call(
+        functools.partial(project_body, (query_cols,)),
+        scalars,
+        [middle_grad_low],
+        attention_full,
+        outward_window,
+        [(query_cols, low)],
+        [],
+        "mixed_back",
+    )
+    mixed_grad = mixed_grad.reshape(packed_token_count, local_groups, query_group_width, HEAD_SIZE)
+    query_grad_blocks = []
+    key_grad_acc = jnp.zeros((packed_token_count, local_groups, HEAD_SIZE), jnp.float32)
+    value_grad_acc = jnp.zeros((packed_token_count, local_groups, HEAD_SIZE), jnp.float32)
+    for block_index in range(block_count):
+        row_start = block_index * block_rows
+        row_stop = row_start + block_rows
+        scores = block_scores(row_start, row_stop)
+        probs = jnp.exp(scores - log_sums[block_index])
+        grad_block = mixed_grad[row_start:row_stop]
+        prob_grad = jnp.einsum(
+            "qhgd,khd->hgqk",
+            grad_block,
+            per_head_values[:row_stop],
+            preferred_element_type=jnp.float32,
+        )
+        row_inner = jnp.sum(probs * prob_grad, axis=-1, keepdims=True)
+        score_grad = (probs * (prob_grad - row_inner)).astype(low)
+        query_grad_blocks.append(
+            jnp.einsum(
+                "hgqk,khd->qhgd",
+                score_grad,
+                per_head_keys[:row_stop],
+                preferred_element_type=jnp.float32,
+            )
+            * score_scale
+        )
+        key_grad_acc = key_grad_acc.at[:row_stop].add(
+            jnp.einsum(
+                "hgqk,qhgd->khd",
+                score_grad,
+                query_heads[row_start:row_stop],
+                preferred_element_type=jnp.float32,
+            )
+            * score_scale
+        )
+        value_grad_acc = value_grad_acc.at[:row_stop].add(
+            jnp.einsum(
+                "hgqk,qhgd->khd",
+                probs.astype(low),
+                grad_block,
+                preferred_element_type=jnp.float32,
+            )
+        )
+    query_grad_heads = (
+        jnp.concatenate(query_grad_blocks, axis=0)
+        .reshape(packed_token_count, local_query, HEAD_SIZE)
+        .astype(low)
+        .astype(jnp.float32)
+    )
+    key_grad_heads = key_grad_acc.astype(low).astype(jnp.float32)
+    value_grad_low = value_grad_acc.astype(low).reshape(
+        packed_token_count, local_groups * HEAD_SIZE
+    )
+    query_map_out, query_map_back = jax.vjp(
+        lambda projected, gain: head_map(projected, gain, local_query), query_proj, head_gain[0]
+    )
+    query_proj_grad, head_query_grad = query_map_back(query_grad_heads)
+    key_map_out, key_map_back = jax.vjp(
+        lambda projected, gain: head_map(projected, gain, local_groups), key_projected, head_gain[1]
+    )
+    key_proj_grad, head_key_grad = key_map_back(key_grad_heads)
+    query_proj_low = query_proj_grad.astype(low)
+    key_proj_low = key_proj_grad.astype(low)
+    kept, sent = full_call(
+        back_body,
+        scalars,
+        [query_proj_low, key_proj_low, value_grad_low],
+        attention_full,
+        inward_window,
+        [],
+        [(width, low)],
+        "projection_back",
+    )
+    norm_one_sum, attention_sums = tail_call(
+        sent,
+        kept,
+        normed_one,
+        middle_grad_low,
+        [query_proj_low, key_proj_low, value_grad_low, mixed],
+        (((0, 0), (0, 1)), ((0, 2), (1, 3))),
+        shards,
+    )
+    (layer_output,) = row_call(layer_out, scalars, [middle, down_sum], [], [jnp.float32])
+    head_grads = jnp.stack([head_query_grad, head_key_grad])
+    head_grads = head_grads + lax.ppermute(head_grads, "tensor", CORE_PAIRS)
+    head_grads = head_grads + lax.ppermute(head_grads, "tensor", CHIP_PAIRS)
+    head_pieces = head_grads.reshape(2, shards, head_cols)[:, turn]
+    early_pieces = [
+        jnp.concatenate(
+            [
+                gain_two_grad[:, at * gain_cols : (at + 1) * gain_cols],
+                head_pieces[0:1, at],
+                head_pieces[1:2, at],
+            ],
+            axis=1,
+        )
+        for at in range(shards)
+    ]
+    early_sum = functools.reduce(jnp.add, spread(early_pieces, shards))
+    input_grad, gain_one_grad = row_call(
+        first_back,
+        scalars,
+        [middle_grad, input_rows, norm_one_sum],
+        [norm_gain[0]],
+        [jnp.float32],
+        sums=1,
+    )
+    late_pieces = spread(
+        [gain_one_grad[:, at * gain_cols : (at + 1) * gain_cols] for at in range(shards)], shards
+    )
+    ff_updates = adam_update(
+        ff_sums, [(0, 0), (0, 1), (1, None)], states[4:6], parts=FF_CHUNKS
+    )
+    inner_updates = adam_update(attention_sums[0], [(0, None), (1, None)], states[0:2])
+    outer_updates = adam_update(attention_sums[1], [(0, None), (1, None)], states[2:4])
+    late_sum = functools.reduce(jnp.add, late_pieces)
+    gain_shards = [
+        jnp.concatenate([late_sum, early_sum[:, :gain_cols]], axis=0),
+        early_sum[:, gain_cols:].reshape(2, head_cols),
+    ]
+    updates = [inner_updates[:4], inner_updates[4:], outer_updates[:4], outer_updates[4:]]
+    updates += [ff_updates[:4], ff_updates[4:]]
+    for (weight, mean, square), grad in zip(states[6:], gain_shards):
+        updates.append([grad, *adam_step(weight, grad, mean, square, GAIN_RATE, 0.0)])
+    return tuple([layer_output, input_grad] + [update[kind] for kind in range(4) for update in updates])
+
+
 def solution(mesh):
+    shards, parts = mesh.shape["fsdp"], mesh.shape["tensor"]
+    ringed = parts == 4 and shards == 8
     return jax.shard_map(
-        per_device,
+        functools.partial(ring_device, shards) if ringed else plain_device,
         mesh=mesh,
         in_specs=(
             P("fsdp", None),

time: 1320 us -> 823 us (0.62)
  waiting for transfers between devices: 868 us -> 2.6 us
  Pallas kernels: 0 us -> 669 us
  matrix products: 160 us -> 21.8 us
  blocking collectives: 73.6 us -> 0 us
  other arithmetic: 117 us -> 57.3 us
  local copies, waits for them, and re-layouts: 79.2 us -> 37.7 us
  starting transfers between devices: 0.37 us -> 21.8 us
  between operations: 15.9 us -> 2.61 us
    pallas_call x0 -> x14, Pallas kernels: none -> 669 us  [the longest x1 414 us: ff_call(): pl.pallas_call(functools.partial(ff_kernel, shards, parts), in_specs=[any...]
    reduce_scatter x3 -> x0, waiting for transfers between devices: 342 us -> none  [the longest x1 173 us: per_device(): lax.psum_scatter(gate_up_grad.astype(jnp.bfloat16), 'fsdp', scatter_dimen...]
    all_gather x3 -> x0, waiting for transfers between devices: 310 us -> none  [the longest x1 169 us: per_device(): lax.all_gather(gate_up_weight.astype(jnp.bfloat16), 'fsdp', axis=1, tiled...]
    psum x3 -> x0, waiting for transfers between devices: 217 us -> none  [the longest x1 77.8 us: per_device(): lax.psum(attention_part.astype(jnp.bfloat16), 'tensor').astype(jnp.float32)]
    dot_general x31 -> x10, matrix products: 156 us -> 18.8 us  [the longest x2 8.7 us: ring_device(): jnp.einsum('qhgd,khd->hgqk', grad_block, per_head_values[:row_stop], pref...]
    unnamed x244 -> x165, local copies, waits for them, and re-layouts: 70.3 us -> 10.2 us
    unnamed x1 -> x0, blocking collectives: 39.2 us -> none
    all_gather x1 -> x0, blocking collectives: 28.5 us -> none  [per_device(): lax.all_gather(jnp.concatenate([norm_gains, headnorm_gains], axis=1).asty...]
  transfers between devices with their start and end apart: 9 -> 16, of which waited for: 9 -> 2; matrix products, arithmetic and copies ran while one was open for 16% -> 3% of each run, Pallas kernels for 0% -> 16%
where the time goes in v2:
time: 823 us; the launch traced here: 813 us
  Pallas kernels  669 us (81%)
  other arithmetic  57.3 us (7%)
  local copies, waits for them, and re-layouts  37.7 us (5%)
  matrix products  21.8 us (3%)
  starting transfers between devices  21.8 us (3%)
    pallas_call x1, Pallas kernels, ff_call(): pl.pallas_call(functools.partial(ff_kernel, shards, parts), in_specs=[any...  414 us
    pallas_call x1, Pallas kernels, gather_call(): pl.pallas_call(functools.partial(gather_body, shards), in_specs=[pl.Block...  76.3 us
    pallas_call x1, Pallas kernels, tail_call(): pl.pallas_call(functools.partial(tail_kernel, shards, jobs), in_specs=[an...  70.9 us
    pallas_call x4, Pallas kernels, row_call(): pl.pallas_call(body, grid_spec=pltpu.PrefetchScalarGridSpec(num_scalar_pr...  46.5 us
    pallas_call x4, Pallas kernels, full_call(): pl.pallas_call(kernel, grid_spec=pltpu.PrefetchScalarGridSpec(num_scalar_...  34.2 us
    pallas_call x3, Pallas kernels, adam_update(): pl.pallas_call(functools.partial(adam_body, places), grid=(parts, rows //...  26.7 us
    ppermute x14, starting transfers between devices, spread(): lax.ppermute(pieces[shards - step], 'fsdp', ring_pairs(shards, step))  21.3 us
  transfers between devices with their start and end apart: 16, of which 2 were waited for; matrix products, arithmetic and copies ran while one was open for 3% of the time, Pallas kernels for 16%

profile of v2, /device:TPU:0, one launch (start us, length us, event | category | flops | bytes accessed | tf_op | source)
XLA Modules:
  0.0 812.7 jit_solution(5887029438648954978)
XLA Ops:
  9.6 76.3 %gather_ring.1 = (bf16[8,256,1536]{2,1,0:T(8,128)(2,1)}, bf16[8,16,384]{2,1,0:T(8,128)(2,1)}) custom-call(bf16[256,1536]{1,0:T(8,128)(2,1)} %pad_maximum_fusion.3.own_ref, bf16[16,384]{1,0:T(8,128)(2,1)} %fusion.68.small_ref), custom_call_target="tpu_custom_call" | custom-call | tf_op jit(solution)/shard_map/gather_ring/pallas_call | solution.py:879
  88.0 9.2 %turned_in.1 = (bf16[1024,2048]{1,0:T(8,128)(2,1)}, bf16[1024,2048]{1,0:T(8,128)(2,1)}, bf16[1024,2048]{1,0:T(8,128)(2,1)}) custom-call(s32[9]{0:T(128)} %concatenate.90.scalars, bf16[1024,2048]{1,0:T(8,128)(2,1)} %x_ref.1, bf16[1024,2048]{1,0:T(8,128)(2,1)} %g_ref.1, f32[1,2048]{1,0:T(1,128)} %bitcast.260), custom_call_target="tpu_custom_call" | custom-call | flops 16777216 | bytes 25165824 | tf_op jit(solution)/shard_map/turned_in/pallas_call | solution.py:456
  97.2 9.2 %project.1 = (f32[1024,512]{1,0:T(8,128)}, f32[1024,256]{1,0:T(8,128)}, bf16[1024,256]{1,0:T(8,128)(2,1)}) custom-call(s32[9]{0:T(128)} %concatenate.90.scalars, bf16[1024,2048]{1,0:T(8,128)(2,1)} %get-tuple-element.146.refs_0_.refs_2_, bf16[2048,1536]{1,0:T(8,128)(2,1)} %bitcast.241), custom_call_target="tpu_custom_call" | custom-call | flops 4294967296 | bytes 17179868 | tf_op jit(solution)/shard_map/project/pallas_call | solution.py:570
  107.5 2.0 reshape.802
  113.7 1.9 reshape.801
  116.5 1.9 multiply_reduce_fusion.2
  120.7 1.5 reshape.800
  122.2 3.2 multiply_reduce_fusion.4
  126.7 1.9 multiply_cosine_fusion
  129.0 2.4 multiply_multiply_fusion
  131.9 2.2 subtract_convert_fusion
  134.1 1.4 fusion.50
  140.5 2.0 fusion.94
  146.0 1.7 fusion.45
  149.2 7.6 attention_out.1
  157.0 1.7 pad_maximum_fusion.refs_5_
  158.7 414.4 %ff_ring.1 = (f32[1024,2048]{1,0:T(8,128)}, bf16[1024,2048]{1,0:T(8,128)(2,1)}, bf16[1024,2048]{1,0:T(8,128)(2,1)}, bf16[1024,2048]{1,0:T(8,128)(2,1)}, f32[3,25...) custom-call(bf16[512,2048]{1,0:T(8,128)(2,1)} %get-tuple-element.151.refs_0_, ...), custom_call_target="tpu_custom_call" | custom-call | tf_op jit(solution)/shard_map/ff_ring/pallas_call | solution.py:1130
  573.2 14.7 %second_back.1 = (f32[1024,2048]{1,0:T(8,128)}, bf16[1024,2048]{1,0:T(8,128)(2,1)}, f32[1,2048]{1,0:T(1,128)}) custom-call(s32[9]{0:T(128)} %concatenate.90.scalars, f32[1024,2048]{1,0:T(8,128)} %get-tuple-element.155.mid_ref, bf16[1024,2048]{1,0:T(8,128)(2,1)} %get-tuple-element.154.refs_3_.g_ref, bf16[1024,2048]{1,0:T(8,128)(2,1)} %get-tuple-element.157.came_ref, ...), custom_call_target="tpu_custom_call" | custom-call | flops 16777216 | bytes 25165824 | tf_op jit(solution)/shard_map/second_back/pallas_call | solution.py:456
  587.8 6.9 mixed_back.1
  596.3 3.3 fusion.7
  601.1 1.5 fusion.41
  603.7 5.4 fusion
  609.5 2.6 fusion.2
  616.1 1.7 copy.383
  617.9 1.7 multiply_add_fusion.3
  619.5 2.8 copy.384
  622.4 2.6 multiply_reduce_fusion.3
  625.0 3.0 multiply_add_fusion.1
  628.2 5.0 multiply_reduce_fusion
  634.5 2.4 fusion.29
  636.9 2.0 copy.382.refs_2_.refs_6_
  639.0 2.9 copy_bitcast_fusion.1.refs_1_.refs_5_
  643.3 6.4 fusion.14
  650.9 10.6 %projection_back.1 = (bf16[512,2048]{1,0:T(8,128)(2,1)}, bf16[512,2048]{1,0:T(8,128)(2,1)}) custom-call(s32[9]{0:T(128)} %concatenate.90.scalars, bf16[1024,512]{1,0:T(8,128)(2,1)} %bitcast.235, bf16[1024,256]{1,0:T(8,128)(2,1)} %copy_bitcast_fusion.1.refs_1_.refs_5_, bf16[1024,256]{1,0:T(8,128)(2,1)} %copy.382.refs_2_.refs_6_, bf16[2048,1536]{1,0:T(8,128)(2,1)} %bitcast.244), custom_call_target="tpu_custom_call" | custom-call | flops 4294967296 | bytes 17179868 | tf_op jit(solution)/shard_map/projection_back/pallas_call | solution.py:570
  661.5 70.9 %tail_ring.1 = (bf16[1024,2048]{1,0:T(8,128)(2,1)}, f32[2,256,768]{2,1,0:T(8,128)S(1)}) custom-call(bf16[512,2048]{1,0:T(8,128)(2,1)} %get-tuple-element.160.refs_0_, bf16[512,2048]{1,0:T(8,128)(2,1)} %get-tuple-element.161.refs_1_, bf16[1024,2048]{1,0:T(8,128)(2,1)} %get-tuple-element.146.refs_0_.refs_2_, ...), custom_call_target="tpu_custom_call" | custom-call | tf_op jit(solution)/shard_map/tail_ring/pallas_call | solution.py:1241
  733.6 13.8 %first_back.1 = (f32[1024,2048]{1,0:T(8,128)}, f32[1,2048]{1,0:T(1,128)}) custom-call(s32[9]{0:T(128)} %concatenate.90.scalars, f32[1024,2048]{1,0:T(8,128)} %get-tuple-element.158.dx_ref, bf16[1024,2048]{1,0:T(8,128)(2,1)} %get-tuple-element.153.refs_2_.x_ref, bf16[1024,2048]{1,0:T(8,128)(2,1)} %get-tuple-element.162.came_ref, f32[1,2048]{1,0:T(1,128)} %bitcast.261), custom_call_target="tpu_custom_call" | custom-call | flops 16777216 | bytes 25165824 | tf_op jit(solution)/shard_map/first_back/pallas_call | solution.py:456
  748.6 1.5 collective-permute-start.6
  750.1 1.9 collective-permute-start.5
  752.0 2.4 collective-permute-start.4
  755.8 18.0 %adam_update.5 = (f32[2,256,1536]{2,1,0:T(8,128)}, f32[2,256,1536]{2,1,0:T(8,128)}, f32[2,256,1536]{2,1,0:T(8,128)}, f32[2,256,1536]{2,1,0:T(8,128)}, f32[256,15...) custom-call(f32[3,256,1536]{2,1,0:T(8,128)} %get-tuple-element.169.grad_ref, ...), custom_call_target="tpu_custom_call" | custom-call | flops 23592960 | bytes 37748736 | tf_op jit(solution)/shard_map/adam_update/pallas_call | solution.py:642
  773.7 4.4 adam_update.4
  778.2 4.3 adam_update.3
  782.7 8.8 %layer_out.1 = f32[1024,2048]{1,0:T(8,128)} custom-call(s32[9]{0:T(128)} %concatenate.90.scalars, f32[1024,2048]{1,0:T(8,128)} %get-tuple-element.155.mid_ref, bf16[1024,2048]{1,0:T(8,128)(2,1)} %get-tuple-element.156.came_ref), custom_call_target="tpu_custom_call" | custom-call | flops 16777216 | bytes 25165824 | tf_op jit(solution)/shard_map/layer_out/pallas_call | solution.py:456
  791.4 2.4 collective-permute-start.3
  796.6 1.9 collective-permute-start.9
  798.5 2.4 collective-permute-start.10
  802.3 3.2 collective-permute-start.12
  808.6 2.3 collective-permute-done.13
  (286 shorter events, 56.2 us)
Async XLA Ops:
  0.7 7.3 copy-start.39
  86.7 10.5 %copy-start.57 = (f32[2,8,384]{2,0,1:T(2,128)}, f32[2,8,384]{2,0,1:T(2,128)S(1)}, u32[]{:S(2)}) copy-start(f32[2,8,384]{2,0,1:T(2,128)S(1)} %convert_bitcast_fusion) | copy-start | bytes 73732
  113.6 14.9 %copy-start.69 = (f32[128]{0:T(128)}, f32[128]{0:T(128)S(1)}, u32[]{:S(2)}) copy-start(f32[128]{0:T(128)S(1)} %mul.527) | copy-start | bytes 1540
  113.7 15.2 %copy-start.63 = (f32[128]{0:T(128)}, f32[128]{0:T(128)S(1)}, u32[]{:S(2)}) copy-start(f32[128]{0:T(128)S(1)} %mul.542) | copy-start | bytes 1540
  115.7 13.3 %copy-start.10 = (f32[1024,4,128]{2,1,0:T(4,128)}, f32[1024,4,128]{2,1,0:T(4,128)S(1)}, u32[]{:S(2)}) copy-start(f32[1024,4,128]{2,1,0:T(4,128)S(1)} %reshape.801) | copy-start | bytes 6291460
  131.9 8.6 %copy-start.25 = (bf16[1024,2,64]{2,0,1:T(8,128)(2,1)}, bf16[1024,2,64]{2,0,1:T(8,128)(2,1)S(1)}, u32[]{:S(2)}) copy-start(bf16[1024,2,64]{2,0,1:T(8,128)(2,1)S(1)} %get-tuple-element.216) | copy-start | bytes 786436
  149.1 7.7 copy-start.48
  149.1 7.7 copy-start.49
  149.1 7.7 copy-start.50
  149.1 7.7 copy-start.40
  149.1 7.8 copy-start.41
  149.1 7.8 copy-start.42
  149.2 7.7 copy-start.43
  149.2 7.7 copy-start.46
  149.2 7.7 copy-start.47
  603.7 5.8 slice-start.1
  622.3 5.8 copy-start.11
  625.0 8.6 %copy-start.9 = (f32[2,2,512,512]{2,3,1,0:T(8,128)S(1)}, f32[2,2,512,512]{2,3,1,0:T(8,128)}, u32[]{:S(2)}) copy-start(f32[2,2,512,512]{2,3,1,0:T(8,128)} %copy-done.7) | copy-start | bytes 12582916
  625.0 9.5 %slice-start.2 = ((s8[8388608]{0:T(1024)(128)(4,1)}), s8[4194304]{0:T(1024)(128)(4,1)S(1)}, s32[]{:S(2)}) async-start(s8[8388608]{0:T(1024)(128)(4,1)} %bitcast.239), calls=%async_computation.2 | async-start | bytes 8388608
  628.2 6.3 slice-start.3
  633.2 149.3 %collective-permute-start.7 = (f32[2,128]{1,0:T(2,128)S(1)}, f32[2,128]{1,0:T(2,128)S(1)}, u32[]{:S(2)}, u32[]{:S(2)}) collective-permute-start(f32[2,128]{1,0:T(2,128)S(1)} %pad_maximum_fusion.13), channel_id=1, source_target_pairs={{0,1},{1,0},{2,3},{3,2},{4,5},{5,4},{6,7},{7,6},{8,9},{9,8},{10,11... | collective-permute-start | bytes 3080 | tf_op jit(solution)/shard_map/ppermute | solution.py:1542
  650.9 10.6 %copy-start = (bf16[1024,512]{1,0:T(8,128)(2,1)S(1)}, bf16[1024,512]{1,0:T(8,128)(2,1)}, u32[]{:S(2)}) copy-start(bf16[1024,512]{1,0:T(8,128)(2,1)} %copy.367.refs_0_.refs_7_) | copy-start | bytes 3145732
  650.9 10.6 %copy-start.1 = (bf16[128,8,4,128]{3,1,2,0:T(8,128)(2,1)S(1)}, bf16[128,8,4,128]{3,1,2,0:T(8,128)(2,1)}, u32[]{:S(2)}) copy-start(bf16[128,8,4,128]{3,1,2,0:T(8,128)(2,1)} %copy.411) | copy-start | bytes 3145732
  650.9 10.6 %copy-start.2 = (bf16[1024,256]{1,0:T(8,128)(2,1)S(1)}, bf16[1024,256]{1,0:T(8,128)(2,1)}, u32[]{:S(2)}) copy-start(bf16[1024,256]{1,0:T(8,128)(2,1)} %copy.382.refs_2_.refs_6_) | copy-start | bytes 1572868
  650.9 10.6 %copy-start.3 = (bf16[1024,256]{1,0:T(8,128)(2,1)S(1)}, bf16[1024,256]{1,0:T(8,128)(2,1)}, u32[]{:S(2)}) copy-start(bf16[1024,256]{1,0:T(8,128)(2,1)} %copy_bitcast_fusion.1.refs_1_.refs_5_) | copy-start | bytes 1572868
  733.6 20.9 %copy-start.67 = (f32[1,2048]{1,0:T(1,128)S(1)}, f32[1,2048]{1,0:T(1,128)}, u32[]{:S(2)}) copy-start(f32[1,2048]{1,0:T(1,128)} %get-tuple-element.173) | copy-start | bytes 24580
  733.6 21.0 %copy-start.5 = (f32[2,256,768]{2,1,0:T(8,128)S(1)}, f32[2,256,768]{2,1,0:T(8,128)}, u32[]{:S(2)}) copy-start(f32[2,256,768]{2,1,0:T(8,128)} %copy-done.4) | copy-start | bytes 4718596
  748.1 46.9 %collective-permute-start = (f32[1,256]{1,0:T(1,128)S(1)}, f32[1,256]{1,0:T(1,128)S(1)}, u32[]{:S(2)}, u32[]{:S(2)}) collective-permute-start(f32[1,256]{1,0:T(1,128)S(1)} %get-tuple-element.232), channel_id=1, source_target_pairs={{0,8},{8,16},{16,24},{24,28},{28,20},{20,12},{12,4},{4,0},{1,9},{9... | collective-permute-start | bytes 3080 | tf_op jit(solution)/shard_map/ppermute | solution.py:442
  748.6 47.8 %collective-permute-start.6 = (f32[1,256]{1,0:T(1,128)S(1)}, f32[1,256]{1,0:T(1,128)S(1)}, u32[]{:S(2)}, u32[]{:S(2)}) collective-permute-start(f32[1,256]{1,0:T(1,128)S(1)} %get-tuple-element.233), channel_id=1, source_target_pairs={{0,4},{8,0},{16,8},{24,16},{28,24},{20,28},{12,20},{4,12},{1,5},{9... | collective-permute-start | bytes 3080 | tf_op jit(solution)/shard_map/ppermute | solution.py:442
  750.1 46.5 %collective-permute-start.5 = (f32[1,256]{1,0:T(1,128)S(1)}, f32[1,256]{1,0:T(1,128)S(1)}, u32[]{:S(2)}, u32[]{:S(2)}) collective-permute-start(f32[1,256]{1,0:T(1,128)S(1)} %get-tuple-element.234), channel_id=1, source_target_pairs={{0,12},{8,4},{16,0},{24,8},{28,16},{20,24},{12,28},{4,20},{1,13},{... | collective-permute-start | bytes 3080 | tf_op jit(solution)/shard_map/ppermute | solution.py:442
  752.0 46.5 %collective-permute-start.4 = (f32[1,256]{1,0:T(1,128)S(1)}, f32[1,256]{1,0:T(1,128)S(1)}, u32[]{:S(2)}, u32[]{:S(2)}) collective-permute-start(f32[1,256]{1,0:T(1,128)S(1)} %get-tuple-element.235), channel_id=1, source_target_pairs={{0,20},{8,12},{16,4},{24,0},{28,8},{20,16},{12,24},{4,28},{1,21},{... | collective-permute-start | bytes 3080 | tf_op jit(solution)/shard_map/ppermute | solution.py:442
  782.5 8.9 %collective-permute-start.8 = (f32[2,128]{1,0:T(2,128)S(1)}, f32[2,128]{1,0:T(2,128)S(1)}, u32[]{:S(2)}, u32[]{:S(2)}) collective-permute-start(f32[2,128]{1,0:T(2,128)S(1)} %fusion.83), channel_id=1, source_target_pairs={{0,2},{2,0},{1,3},{3,1},{4,6},{6,4},{5,7},{7,5},{8,10},{10,8},{9,1... | collective-permute-start | bytes 3080 | tf_op jit(solution)/shard_map/ppermute | solution.py:1543
  782.6 28.4 %copy-start.73 = (f32[2,16]{1,0:T(2,128)S(1)}, f32[2,16]{1,0:T(2,128)}, u32[]{:S(2)}) copy-start(f32[2,16]{1,0:T(2,128)} %param.49) | copy-start | bytes 388
  782.6 28.4 %copy-start.74 = (f32[2,16]{1,0:T(2,128)S(1)}, f32[2,16]{1,0:T(2,128)}, u32[]{:S(2)}) copy-start(f32[2,16]{1,0:T(2,128)} %param.57) | copy-start | bytes 388
  782.6 28.4 %copy-start.75 = (f32[2,16]{1,0:T(2,128)S(1)}, f32[2,16]{1,0:T(2,128)}, u32[]{:S(2)}) copy-start(f32[2,16]{1,0:T(2,128)} %param.65) | copy-start | bytes 388
  782.6 29.0 %copy-start.68 = (f32[2,256]{1,0:T(2,128)S(1)}, f32[2,256]{1,0:T(2,128)}, u32[]{:S(2)}) copy-start(f32[2,256]{1,0:T(2,128)} %param.48) | copy-start | bytes 6148
  782.6 29.0 %copy-start.71 = (f32[2,256]{1,0:T(2,128)S(1)}, f32[2,256]{1,0:T(2,128)}, u32[]{:S(2)}) copy-start(f32[2,256]{1,0:T(2,128)} %param.56) | copy-start | bytes 6148
  782.6 29.0 %copy-start.72 = (f32[2,256]{1,0:T(2,128)S(1)}, f32[2,256]{1,0:T(2,128)}, u32[]{:S(2)}) copy-start(f32[2,256]{1,0:T(2,128)} %param.64) | copy-start | bytes 6148
  791.4 9.5 %collective-permute-start.3 = (f32[1,256]{1,0:T(1,128)S(1)}, f32[1,256]{1,0:T(1,128)S(1)}, u32[]{:S(2)}, u32[]{:S(2)}) collective-permute-start(f32[1,256]{1,0:T(1,128)S(1)} %get-tuple-element.236), channel_id=1, source_target_pairs={{0,28},{8,20},{16,12},{24,4},{28,0},{20,8},{12,16},{4,24},{1,29},{... | collective-permute-start | bytes 3080 | tf_op jit(solution)/shard_map/ppermute | solution.py:442
  795.0 7.3 collective-permute-start.2
  796.3 9.1 %collective-permute-start.1 = (f32[1,256]{1,0:T(1,128)S(1)}, f32[1,256]{1,0:T(1,128)S(1)}, u32[]{:S(2)}, u32[]{:S(2)}) collective-permute-start(f32[1,256]{1,0:T(1,128)S(1)} %get-tuple-element.238), channel_id=1, source_target_pairs={{0,16},{8,24},{16,28},{24,20},{28,12},{20,4},{12,0},{4,8},{1,17},{... | collective-permute-start | bytes 3080 | tf_op jit(solution)/shard_map/ppermute | solution.py:442
  796.6 9.6 %collective-permute-start.9 = (f32[1,288]{1,0:T(1,128)S(1)}, f32[1,288]{1,0:T(1,128)S(1)}, u32[]{:S(2)}, u32[]{:S(2)}) collective-permute-start(f32[1,288]{1,0:T(1,128)S(1)} %pad_maximum_fusion.6), channel_id=1, source_target_pairs={{0,8},{8,16},{16,24},{24,28},{28,20},{20,12},{12,4},{4,0},{1,9},{9... | collective-permute-start | bytes 3464 | tf_op jit(solution)/shard_map/ppermute | solution.py:442
  798.5 8.7 %collective-permute-start.10 = (f32[1,288]{1,0:T(1,128)S(1)}, f32[1,288]{1,0:T(1,128)S(1)}, u32[]{:S(2)}, u32[]{:S(2)}) collective-permute-start(f32[1,288]{1,0:T(1,128)S(1)} %pad_maximum_fusion.7), channel_id=1, source_target_pairs={{0,16},{8,24},{16,28},{24,20},{28,12},{20,4},{12,0},{4,8},{1,17},{... | collective-permute-start | bytes 3464 | tf_op jit(solution)/shard_map/ppermute | solution.py:442
  800.9 7.3 collective-permute-start.11
  802.3 6.3 collective-permute-start.12
  805.5 5.4 collective-permute-start.13
  806.2 4.7 collective-permute-start.14
  807.2 3.7 collective-permute-start.15
  (51 other events, 137.9 us)

commit v3 on v2

--- a/solution.py
+++ b/solution.py
@@ -412,11 +412,9 @@
     return tuple(results)
 
 
-CORE_PAIRS = [(0, 1), (1, 0), (2, 3), (3, 2)]
-CHIP_PAIRS = [(0, 2), (2, 0), (1, 3), (3, 1)]
 FF_CHUNKS = 3
-ROW_TILE = 256
-FULL_TILE = 256
+ROW_TILE = 128
+ROW_GROUP = 16
 
 
 def ring_place(place, shards):
@@ -428,20 +426,6 @@
 def place_of(index, shards):
     row, column = index // 2, index % 2
     return row + column * (shards - 1 - 2 * row)
-
-
-def ring_pairs(shards, step):
-    return [
-        (ring_place(place, shards), ring_place(place + step + shards, shards))
-        for place in range(shards)
-    ]
-
-
-def spread(pieces, shards):
-    return [pieces[0]] + [
-        lax.ppermute(pieces[shards - step], "fsdp", ring_pairs(shards, step))
-        for step in range(1, shards)
-    ]
 
 
 def row_scale(values):
@@ -460,10 +444,11 @@
             grid=(tiles,),
             in_specs=[row] * len(arrays)
             + [whole] * len(gains),
-            out_specs=[row] * len(outs) + [whole] * sums,
+            out_specs=[row] * len(outs)
+            + [pl.BlockSpec((8, width), lambda tile, *_: (0, 0))] * sums,
         ),
         out_shape=[jax.ShapeDtypeStruct((tokens, width), kind) for kind in outs]
-        + [jax.ShapeDtypeStruct((1, width), jnp.float32)] * sums,
+        + [jax.ShapeDtypeStruct((8, width), jnp.float32)] * sums,
         cost_estimate=pl.CostEstimate(
             flops=cost * tokens * width, bytes_accessed=3 * cost * tokens * width // 2, transcendentals=0
         ),
@@ -471,65 +456,98 @@
     )(scalars, *arrays, *gains)
 
 
+def row_groups(ref, body):
+    @pl.loop(0, ref.shape[0] // ROW_GROUP)
+    def _(step):
+        body(pl.ds(pl.multiple_of(step * ROW_GROUP, ROW_GROUP), ROW_GROUP))
+
+
+def count_of(scalars):
+    return (len(scalars) if isinstance(scalars, list) else scalars.shape[0]) - 1
+
+
 def turned_in(scalars, x_ref, g_ref, gain_ref, xr_ref, gr_ref, n_ref):
-    shards = scalars.shape[0] - 1
+    shards = count_of(scalars)
     width = x_ref.shape[1] // shards
-    scale = row_scale(x_ref[...].astype(jnp.float32))
+    sources = [pl.ds(pl.multiple_of(scalars[at] * width, 128), width) for at in range(shards)]
+
+    def body(rows):
+        scale = row_scale(x_ref[rows, :].astype(jnp.float32))
+        for at in range(shards):
+            target = slice(at * width, (at + 1) * width)
+            values = x_ref[rows, sources[at]]
+            xr_ref[rows, target] = values
+            gr_ref[rows, target] = g_ref[rows, sources[at]]
+            n_ref[rows, target] = (
+                values.astype(jnp.float32) * scale * gain_ref[:, target]
+            ).astype(n_ref.dtype)
+
+    row_groups(x_ref, body)
+
+
+def put_back(scalars, out_ref, rows, value):
+    shards = count_of(scalars)
+    width = value.shape[1] // shards
     for at in range(shards):
-        source = pl.ds(pl.multiple_of(scalars[at] * width, 128), width)
-        target = slice(at * width, (at + 1) * width)
-        values = x_ref[:, source]
-        xr_ref[:, target] = values
-        gr_ref[:, target] = g_ref[:, source]
-        n_ref[:, target] = (values.astype(jnp.float32) * scale * gain_ref[:, target]).astype(
-            n_ref.dtype
-        )
-
-
-def layer_out(scalars, mid_ref, came_ref, out_ref):
-    shards = scalars.shape[0] - 1
-    width = mid_ref.shape[1] // shards
-    value = mid_ref[...] + came_ref[...].astype(jnp.float32)
-    for at in range(shards):
-        out_ref[:, pl.ds(pl.multiple_of(scalars[at] * width, 128), width)] = value[
+        out_ref[rows, pl.ds(pl.multiple_of(scalars[at] * width, 128), width)] = value[
             :, at * width : (at + 1) * width
         ]
+
+
+def layer_out(scalars, mid_ref, came_ref, out_ref):
+    def body(rows):
+        put_back(
+            scalars, out_ref, rows, mid_ref[rows, :] + came_ref[rows, :].astype(jnp.float32)
+        )
+
+    row_groups(mid_ref, body)
 
 
 def norm_grad(values, grad, gain, sum_ref):
     scale = row_scale(values)
     unit = values * scale
+    share = grad * unit
+    sum_ref[...] += jnp.sum(share.reshape(-1, 8, share.shape[1]), axis=0)
     inner = grad * gain
-
+    return scale * (inner - unit * jnp.mean(inner * unit, axis=-1, keepdims=True))
+
+
+def clear_first(sum_ref):
     @pl.when(pl.program_id(0) == 0)
     def _():
         sum_ref[...] = jnp.zeros_like(sum_ref)
 
-    sum_ref[...] += jnp.sum(grad * unit, axis=0, keepdims=True)
-    return scale * (inner - unit * jnp.mean(inner * unit, axis=-1, keepdims=True))
-
 
 def second_back(scalars, mid_ref, g_ref, came_ref, gain_ref, dx_ref, low_ref, sum_ref):
-    grad = came_ref[...].astype(jnp.float32)
-    value = g_ref[...].astype(jnp.float32) + norm_grad(mid_ref[...], grad, gain_ref[...], sum_ref)
-    dx_ref[...] = value
-    low_ref[...] = value.astype(low_ref.dtype)
+    clear_first(sum_ref)
+
+    def body(rows):
+        grad = came_ref[rows, :].astype(jnp.float32)
+        value = g_ref[rows, :].astype(jnp.float32) + norm_grad(
+            mid_ref[rows, :], grad, gain_ref[...], sum_ref
+        )
+        dx_ref[rows, :] = value
+        low_ref[rows, :] = value.astype(low_ref.dtype)
+
+    row_groups(mid_ref, body)
 
 
 def first_back(scalars, dx_ref, x_ref, came_ref, gain_ref, out_ref, sum_ref):
-    shards = scalars.shape[0] - 1
-    width = x_ref.shape[1] // shards
-    grad = came_ref[...].astype(jnp.float32)
-    value = dx_ref[...] + norm_grad(
-        x_ref[...].astype(jnp.float32), grad, gain_ref[...], sum_ref
-    )
-    for at in range(shards):
-        out_ref[:, pl.ds(pl.multiple_of(scalars[at] * width, 128), width)] = value[
-            :, at * width : (at + 1) * width
-        ]
-
-
-def full_call(body, scalars, lefts, matrix, window, outs, halves, name):
+    clear_first(sum_ref)
+
+    def body(rows):
+        value = dx_ref[rows, :] + norm_grad(
+            x_ref[rows, :].astype(jnp.float32),
+            came_ref[rows, :].astype(jnp.float32),
+            gain_ref[...],
+            sum_ref,
+        )
+        put_back(scalars, out_ref, rows, value)
+
+    row_groups(x_ref, body)
+
+
+def full_call(body, scalars, lefts, matrix, window, outs, halves, name, extras=()):
     tokens = lefts[0].shape[0]
     tiles = tokens // FULL_TILE
     half = tiles // 2
@@ -540,10 +558,11 @@
 
     def kernel(scalars, *refs):
         left_refs, whole = refs[: len(lefts)], refs[len(lefts)]
-        out_refs = refs[len(lefts) + 1 : len(lefts) + 1 + len(outs)]
-        half_refs = refs[len(lefts) + 1 + len(outs) :]
+        extra_refs = refs[len(lefts) + 1 : len(lefts) + 1 + len(extras)]
+        rest = refs[len(lefts) + 1 + len(extras) :]
+        out_refs, half_refs = rest[: len(outs)], rest[len(outs) :]
         step = pl.program_id(0)
-        values = body(left_refs, whole, out_refs)
+        values = body(left_refs, whole, extra_refs, out_refs)
         for place, value in enumerate(values):
             kept, sent = half_refs[2 * place : 2 * place + 2]
 
@@ -573,7 +592,8 @@
             num_scalar_prefetch=1,
             grid=(tiles,),
             in_specs=[row_spec(left.shape[1]) for left in lefts]
-            + [pl.BlockSpec((matrix.shape[0], columns), lambda step, _: (0, at))],
+            + [pl.BlockSpec((matrix.shape[0], columns), lambda step, _: (0, at))]
+            + [pl.BlockSpec(extra.shape, lambda step, _: (0, 0)) for extra in extras],
             out_specs=[row_spec(width) for width, _ in outs] + half_out,
         ),
         out_shape=[jax.ShapeDtypeStruct((tokens, width), kind) for width, kind in outs]
@@ -584,14 +604,14 @@
         ],
         cost_estimate=pl.CostEstimate(flops=work, bytes_accessed=work // 250, transcendentals=0),
         name=name,
-    )(scalars, *lefts, matrix)
+    )(scalars, *lefts, matrix, *extras)
 
 
 def rows_times(left, right):
     return jnp.dot(left, right, preferred_element_type=jnp.float32)
 
 
-def project_body(cuts, lefts, whole, outs):
+def project_body(cuts, lefts, whole, extras, outs):
     start = 0
     for out, stop in zip(outs, cuts):
         out[...] = rows_times(lefts[0][...], whole[:, start:stop]).astype(out.dtype)
@@ -599,7 +619,7 @@
     return []
 
 
-def back_body(lefts, whole, outs):
+def back_body(lefts, whole, extras, outs):
     start, value = 0, None
     for left in lefts:
         stop = start + left.shape[1]
@@ -609,15 +629,19 @@
     return [value]
 
 
-def adam_body(places, grad_ref, *refs):
-    count = len({place[0] for place in places})
-    states, outs = refs[: 3 * count], refs[3 * count :]
+def adam_body(places, count, *refs):
+    arrays = len({place[0] for place in places})
+    grad_refs, refs = refs[:count], refs[count:]
+    states, outs = refs[: 3 * arrays], refs[3 * arrays :]
     start = 0
     for array, plane in places:
         at = (Ellipsis,) if plane is None else (plane,)
         weight, mean, square = (states[3 * array + kind][at] for kind in range(3))
         stop = start + weight.shape[-1]
-        grad = grad_ref[:, start:stop]
+        grad = grad_refs[0][:, start:stop]
+        for part in range(1, count):
+            other = grad_refs[part][:, start:stop].astype(jnp.float32)
+            grad = jnp.where(pl.program_id(0) == part, other, grad)
         step, mean_next, square_next = adam_step(
             weight, grad, mean, square, MATRIX_RATE, WEIGHT_DECAY
         )
@@ -626,23 +650,28 @@
         start = stop
 
 
-def adam_update(grads, places, states, parts=None):
-    rows, columns = grads.shape[-2:]
+def adam_update(grads, places, states):
+    parts = len(grads)
+    rows, columns = grads[0].shape
     tile = min(64, rows)
-    if parts is None:
-        grads, parts = grads[None], 1
 
     def window(array):
         lead = array.shape[:-2]
         shape = lead + (tile, array.shape[-1] // parts)
         return pl.BlockSpec(shape, lambda part, at: (0,) * len(lead) + (at, part))
 
+    def grad_index(own, part, at):
+        return (jnp.where(part == own, at, 0), 0)
+
     flat = [array for group in states for array in group]
     out_like = [group[0] for group in states for _ in range(4)]
     return pl.pallas_call(
-        functools.partial(adam_body, places),
+        functools.partial(adam_body, places, parts),
         grid=(parts, rows // tile),
-        in_specs=[pl.BlockSpec((None, tile, columns), lambda part, at: (part, at, 0))]
+        in_specs=[
+            pl.BlockSpec((tile, columns), functools.partial(grad_index, own))
+            for own in range(parts)
+        ]
         + [window(array) for array in flat],
         out_specs=[window(array) for array in out_like],
         out_shape=[jax.ShapeDtypeStruct(array.shape, jnp.float32) for array in out_like],
@@ -652,7 +681,7 @@
             transcendentals=0,
         ),
         name="adam_update",
-    )(grads, *flat)
+    )(*grads, *flat)
 
 
 class Hops:
@@ -688,34 +717,45 @@
     )
 
 
+HALVES = 2
+
+
+def half_rows(ref, half):
+    rows = ref.shape[0] // HALVES
+    return ref.at[pl.ds(half * rows, rows)]
+
+
 class RingGather:
     def __init__(self, hops, own, slots, sems, forward):
         legs = hops.shards // 2
-        self.reach = (legs, legs - 1) if forward else (legs - 1, legs)
+        reach = (legs, legs - 1) if forward else (legs - 1, legs)
+        self.reach = [reach if half % 2 == 0 else reach[::-1] for half in range(HALVES)]
         self.hops, self.own, self.slots, self.sems = hops, own, slots, sems
 
-    def copy(self, way, step):
+    def copy(self, way, step, half):
         shards = self.hops.shards
         source, target = (step - 1, step) if way == 0 else (shards - step + 1, shards - step)
         return remote(
-            self.own if step == 1 else self.slots.at[source],
-            self.slots.at[target],
-            self.sems[0].at[way, step - 1],
-            self.sems[1].at[way, step - 1],
+            half_rows(self.own if step == 1 else self.slots.at[source], half),
+            half_rows(self.slots.at[target], half),
+            self.sems[0].at[way, step - 1, half],
+            self.sems[1].at[way, step - 1, half],
             self.hops.neighbours[way],
         )
 
     def hop(self, step):
-        for way in range(2):
-            if 1 < step <= self.reach[way] + 1:
-                self.copy(way, step - 1).wait_recv()
-            if step <= self.reach[way]:
-                self.copy(way, step).start()
+        for half in range(HALVES):
+            for way in range(2):
+                if 1 < step <= self.reach[half][way] + 1:
+                    self.copy(way, step - 1, half).wait_recv()
+                if step <= self.reach[half][way]:
+                    self.copy(way, step, half).start()
 
     def close(self):
-        for way in range(2):
-            for step in range(1, self.reach[way] + 1):
-                self.copy(way, step).wait_send()
+        for half in range(HALVES):
+            for way in range(2):
+                for step in range(1, self.reach[half][way] + 1):
+                    self.copy(way, step, half).wait_send()
 
 
 def by_rows(count, body):
@@ -734,72 +774,77 @@
         self.number = [{}, {}]
         for job, step in plan:
             for way in range(2):
-                hop = step - (max(jobs[job]) - jobs[job][way])
-                if hop >= 1:
-                    self.number[way][job, hop] = len(self.number[way])
-
-    def copy(self, way, number):
+                if step <= jobs[job][way]:
+                    self.number[way][job, step] = len(self.number[way])
+
+    def copy(self, way, number, half):
         slot = number % self.SLOTS
         return remote(
-            self.sent.at[way, slot],
-            self.came.at[way, slot],
-            self.sems[0].at[way, slot],
-            self.sems[1].at[way, slot],
+            half_rows(self.sent.at[way, slot], half),
+            half_rows(self.came.at[way, slot], half),
+            self.sems[0].at[way, slot, half],
+            self.sems[1].at[way, slot, half],
             self.hops.neighbours[way],
         )
 
-    def add(self, way, job, hop, base, out):
+    def add(self, way, job, hop, half, out):
         number = self.number[way][job, hop]
-        self.copy(way, number).wait_recv()
+        self.copy(way, number, half).wait_recv()
         slot = number % self.SLOTS
-
-        def body(rows):
+        count = out.shape[0] // HALVES
+
+        @pl.loop(0, count // ROW_STEP)
+        def _(step):
+            rows = pl.ds(pl.multiple_of(half * count + step * ROW_STEP, ROW_STEP), ROW_STEP)
             out[rows, :] = (
-                base[rows, :].astype(jnp.float32) + self.came[way, slot, rows].astype(jnp.float32)
+                out[rows, :].astype(jnp.float32) + self.came[way, slot, rows].astype(jnp.float32)
             ).astype(out.dtype)
 
-        by_rows(out.shape[0], body)
         if number + self.SLOTS < self.total[way]:
             pl.semaphore_signal(
-                self.credits.at[way],
+                self.credits.at[way, half],
                 inc=1,
                 device_id=self.hops.neighbours[1 - way],
                 device_id_type=pl.DeviceIdType.MESH,
             )
 
-    def hop(self, job, step):
-        longest = max(self.jobs[job])
+    def prepare(self, job, hop):
         for way in range(2):
-            reach = self.jobs[job][way]
-            hop = step - (longest - reach)
-            if hop < 1 or hop > reach:
+            distance = self.jobs[job][way] - hop + 1
+            if distance < 1:
                 continue
-            distance = reach - hop + 1
             number = self.number[way][job, hop]
-            slot = number % self.SLOTS
             if number >= self.SLOTS:
-                self.copy(way, number - self.SLOTS).wait_send()
+                for half in range(HALVES):
+                    self.copy(way, number - self.SLOTS, half).wait_send()
             self.partial(
                 job,
                 self.hops.shards - distance if way == 0 else distance,
-                self.sent.at[way, slot],
+                self.sent.at[way, number % self.SLOTS],
             )
-            if hop > 1:
-                own = self.sent.at[way, slot]
-                self.add(way, job, hop - 1, own, own)
-            if number >= self.SLOTS:
-                pl.semaphore_wait(self.credits.at[way], 1)
-            self.copy(way, number).start()
+
+    def hop(self, job, hop):
+        for half in range(HALVES):
+            for way in range(2):
+                if hop > self.jobs[job][way]:
+                    continue
+                number = self.number[way][job, hop]
+                if hop > 1:
+                    self.add(way, job, hop - 1, half, self.sent.at[way, number % self.SLOTS])
+                if number >= self.SLOTS:
+                    pl.semaphore_wait(self.credits.at[way, half], 1)
+                self.copy(way, number, half).start()
 
     def last(self, job, own):
-        self.partial(job, 0, own)
-        for way in range(2):
-            self.add(way, job, self.jobs[job][way], own, own)
+        for half in range(HALVES):
+            for way in range(2):
+                self.add(way, job, self.jobs[job][way], half, own)
 
     def close(self):
         for way in range(2):
             for number in range(max(0, self.total[way] - self.SLOTS), self.total[way]):
-                self.copy(way, number).wait_send()
+                for half in range(HALVES):
+                    self.copy(way, number, half).wait_send()
 
 
 class CoreSum:
@@ -852,42 +897,195 @@
 RING_LIMIT = 66500000
 
 
-def gather_body(shards, own_ref, small_ref, out_ref, few_ref, *sems):
+FULL_TILE = 256
+
+
+def gather_body(shards, gain_cols, query_cols, key_cols, *refs):
+    (own_ref, small_ref, x_ref, g_ref, ff_ref, cosine_ref, sine_ref, first_ref) = refs[:8]
+    (out_ref, few_ref, early_ref, xr_ref, gr_ref, n_ref) = refs[8:14]
+    (query_raw, key_raw, query_ref, key_ref, value_ref, mixed_ref) = refs[14:20]
+    (kept_ref, sent_ref) = refs[20:22]
+    (few, gain, head_gain, whole) = refs[22:26]
+    (big_sent, big_came, ff_sent, ff_came, few_sent, few_came, local) = refs[26:]
     hops = Hops(shards)
-    hops.meet(hops.neighbours)
-    few = RingGather(hops, small_ref, few_ref, sems[2:4], True)
-    big = RingGather(hops, own_ref, out_ref, sems[0:2], True)
-    rings = (few, big)
+    place = place_of(lax.axis_index("fsdp"), shards)
+    ahead = [{"fsdp": ring_place(place + at, shards)} for at in range(1, shards)]
+    hops.meet(ahead)
+    smalls = [
+        remote(small_ref, few.at[at], few_sent.at[at - 1], few_came.at[at - 1], ahead[at - 1])
+        for at in range(1, shards)
+    ]
+    for copy in smalls:
+        copy.start()
+    big = RingGather(hops, own_ref, out_ref, (big_sent, big_came), True)
+    early = RingGather(hops, ff_ref.at[0], early_ref, (ff_sent, ff_came), True)
+    big.hop(1)
     copies = [
-        pltpu.make_async_copy(own_ref, out_ref.at[0], sems[4].at[0]),
-        pltpu.make_async_copy(small_ref, few_ref.at[0], sems[4].at[1]),
+        pltpu.make_async_copy(own_ref, out_ref.at[0], local.at[0]),
+        pltpu.make_async_copy(small_ref, few.at[0], local.at[1]),
     ]
-    for step in range(1, shards // 2 + 2):
-        for ring in rings:
-            ring.hop(step)
-        if step == 1:
-            for copy in copies:
-                copy.start()
-    for ring in rings:
-        ring.close()
+    for copy in copies:
+        copy.start()
     for copy in copies:
         copy.wait()
-
-
-def gather_call(own, small, shards):
+    for copy in smalls:
+        copy.wait_recv()
+    put = pltpu.make_async_copy(few, few_ref, local.at[1])
+    put.start()
+    turn = [ring_place(place - at + shards, shards) for at in range(shards)]
+    heads = jnp.zeros((few.shape[1], HEAD_SIZE), jnp.float32)
+    for at in range(shards):
+        gain[:, at * gain_cols : (at + 1) * gain_cols] = few[at, 0:1, :gain_cols].astype(
+            jnp.float32
+        )
+        heads += pltpu.roll(
+            few[at, :, gain_cols : gain_cols + HEAD_SIZE].astype(jnp.float32),
+            turn[at] * (HEAD_SIZE // shards),
+            1,
+        )
+    head_gain[...] = heads
+    scalars = turn + [hops.core]
+    tokens, width = x_ref.shape
+    tiles = tokens // ROW_TILE
     legs = shards // 2
+
+    def turned_part(part):
+        def index(tile):
+            return (tile + part * (tiles // legs), 0)
+
+        pltpu.emit_pipeline(
+            lambda *refs: turned_in(scalars, *refs[:2], gain, *refs[2:]),
+            grid=(tiles // legs,),
+            in_specs=[pl.BlockSpec((ROW_TILE, width), index)] * 2,
+            out_specs=[pl.BlockSpec((ROW_TILE, width), index)] * 3,
+        )(x_ref, g_ref, xr_ref, gr_ref, n_ref)
+
+    for part in range(legs):
+        turned_part(part)
+        if part + 2 <= legs:
+            big.hop(part + 2)
+    early.hop(1)
+    big.hop(legs + 1)
+    loads = [
+        pltpu.make_async_copy(
+            out_ref.at[at],
+            whole.at[pl.ds(at * out_ref.shape[1], out_ref.shape[1])],
+            local.at[2 + at],
+        )
+        for at in range(shards)
+    ]
+    for copy in loads:
+        copy.start()
+    for copy in loads:
+        copy.wait()
+    inward = query_cols + 2 * key_cols
+
+    def project_part(part):
+        def index(tile):
+            return (tile + part * (tokens // FULL_TILE // 2), 0)
+
+        def spec(array):
+            return pl.BlockSpec((FULL_TILE, array.shape[1]), index)
+
+        outs = [query_raw, key_raw, query_ref, key_ref, value_ref]
+        lefts = [n_ref, cosine_ref, sine_ref]
+        pltpu.emit_pipeline(
+            lambda *refs: turn_body(
+                query_cols, key_cols, refs[:3], whole.at[:, pl.ds(0, inward)], [head_gain], refs[3:]
+            )
+            and None,
+            grid=(tokens // FULL_TILE // 2,),
+            in_specs=[spec(left) for left in lefts],
+            out_specs=[spec(out) for out in outs],
+        )(*lefts, *outs)
+
+    groups = key_cols // HEAD_SIZE
+
+    def attention_part(group):
+        def spec(array):
+            return pl.BlockSpec((tokens, array.shape[1] // groups), lambda _: (0, group))
+
+        arrays = [query_ref, key_ref, value_ref, mixed_ref]
+        pltpu.emit_pipeline(
+            lambda query, key, value, out: attention_body(query, key, value, first_ref, out),
+            grid=(1,),
+            in_specs=[spec(array) for array in arrays[:3]],
+            out_specs=[spec(mixed_ref)],
+        )(*arrays)
+
+    half = tokens // 2
+
+    def out_part(core, out):
+        rows = mixed_ref.at[pl.ds(pl.multiple_of(core * half, half), half)]
+
+        def body(left, value):
+            value[...] = contract_cols(left[...], whole[:, inward:]).astype(value.dtype)
+
+        pltpu.emit_pipeline(
+            body,
+            grid=(half // FULL_TILE,),
+            in_specs=[pl.BlockSpec((FULL_TILE, query_cols), lambda tile: (tile, 0))],
+            out_specs=[pl.BlockSpec((FULL_TILE, width), lambda tile: (tile, 0))],
+        )(rows, out)
+
+    project_part(0)
+    early.hop(2)
+    project_part(1)
+    attention_part(0)
+    early.hop(3)
+    for group in range(1, groups):
+        attention_part(group)
+    early.hop(4)
+    out_part(1 - hops.core, sent_ref)
+    out_part(hops.core, kept_ref)
+    early.hop(5)
+    big.close()
+    early.close()
+    for copy in smalls:
+        copy.wait_send()
+    put.wait()
+
+
+def gather_call(own, small, rows, grads, ff_block, cosine, sine, first, gain_cols, cuts):
+    tokens, width = rows.shape
+    shards = width // own.shape[0]
+    legs = shards // 2
+    query_cols, key_cols = cuts
+    low = jnp.bfloat16
+    anywhere = pl.BlockSpec(memory_space=pl.ANY)
+
+    def like(columns, kind=low, count=tokens):
+        return jax.ShapeDtypeStruct((count, columns), kind)
+
     return pl.pallas_call(
-        functools.partial(gather_body, shards),
-        in_specs=[pl.BlockSpec(memory_space=pl.ANY)] * 2,
-        out_specs=[pl.BlockSpec(memory_space=pl.ANY)] * 2,
+        functools.partial(gather_body, shards, gain_cols, query_cols, key_cols),
+        in_specs=[anywhere] * 7 + [pl.BlockSpec(memory_space=pltpu.VMEM)],
+        out_specs=[anywhere] * 14,
         out_shape=[
-            jax.ShapeDtypeStruct((shards, *array.shape), array.dtype) for array in (own, small)
+            jax.ShapeDtypeStruct((shards, *shape), low)
+            for shape in (own.shape, small.shape, ff_block.shape[1:])
+        ]
+        + [like(width)] * 3
+        + [like(query_cols, jnp.float32), like(key_cols, jnp.float32)]
+        + [like(query_cols), like(key_cols), like(key_cols), like(query_cols)]
+        + [like(width, low, tokens // 2)] * 2,
+        scratch_shapes=[
+            pltpu.VMEM((shards, *small.shape), small.dtype),
+            pltpu.VMEM((1, width), jnp.float32),
+            pltpu.VMEM((small.shape[0], HEAD_SIZE), jnp.float32),
+            pltpu.VMEM((width, own.shape[1]), low),
+        ]
+        + [pltpu.SemaphoreType.DMA((2, legs, HALVES))] * 4
+        + [
+            pltpu.SemaphoreType.DMA((shards - 1,)),
+            pltpu.SemaphoreType.DMA((shards - 1,)),
+            pltpu.SemaphoreType.DMA((2 + shards,)),
         ],
-        scratch_shapes=[pltpu.SemaphoreType.DMA((2, legs))] * 4
-        + [pltpu.SemaphoreType.DMA((2,))],
-        compiler_params=pltpu.CompilerParams(collective_id=0, has_side_effects=True),
+        compiler_params=pltpu.CompilerParams(
+            collective_id=0, has_side_effects=True, vmem_limit_bytes=56 * 1024 * 1024
+        ),
         name="gather_ring",
-    )(own, small)
+    )(own, small, rows, grads, ff_block, cosine, sine, first)
 
 
 FF_TILE = 256
@@ -895,13 +1093,14 @@
 
 
 def ff_kernel(shards, parts, *refs):
-    (sent_ref, kept_ref, x_ref, grad_ref, gain_ref, own_ref) = refs[:6]
-    (mid_ref, norm_out, normsum_ref, downsum_ref, grads_ref, whole_ref) = refs[6:12]
-    (acts, whole, pairs, norm_acc, r_sent, r_came, total) = refs[12:19]
-    (out_half, kept_half, chip, first) = refs[19:23]
-    seconds = refs[23:25]
-    (x_tile, mid_tile) = refs[25:27]
-    (ag_sent, ag_came, rs_sent, rs_came, credits, sums, local) = refs[27:]
+    (sent_ref, kept_ref, x_ref, grad_ref, gain_ref, own_ref, early_ref) = refs[:7]
+    (mid_ref, normsum_ref, downsum_ref, grads_ref, late_ref, whole_ref) = refs[7:13]
+    (acts, whole, pairs, norm_acc, r_sent, r_came, total, late) = refs[13:21]
+    (out_half, kept_half, chip, first) = refs[21:25]
+    seconds = refs[25:27]
+    (x_tile, mid_tile) = refs[27:29]
+    (ag_sent, ag_came, rs_sent, rs_came, credits, sums, local) = refs[29:]
+    place = place_of(lax.axis_index("fsdp"), shards)
     hops = Hops(shards)
     hops.meet([*hops.neighbours, hops.partner, hops.across])
     core = hops.core
@@ -914,12 +1113,17 @@
         RingGather(
             hops,
             own_ref.at[part],
-            whole_ref.at[part],
-            (ag_sent.at[part], ag_came.at[part]),
+            whole_ref.at[part - 1],
+            (ag_sent.at[part - 1], ag_came.at[part - 1]),
             part % 2 == 0,
         )
-        for part in range(parts)
+        for part in range(1, parts)
     ]
+
+    def chunk_block(part, at):
+        if at == 0:
+            return own_ref.at[part]
+        return early_ref.at[at] if part == 0 else whole_ref.at[part - 1, at]
 
     def partial(job, at, out):
         @pl.loop(0, 3)
@@ -937,8 +1141,8 @@
         r_came,
         (rs_sent, rs_came),
         credits,
-        [(legs, legs - 1) if part % 2 == 0 else (legs - 1, legs) for part in range(parts)],
-        [(part, step) for part in range(parts) for step in range(1, legs + 1)],
+        [(legs, legs - 1) if part % 2 == 0 else (legs - 1, legs) for part in range(parts - 1)],
+        [(part, step) for part in range(parts - 1) for step in range(1, legs + 1)],
     )
     attention = CoreSum(
         hops, sent_ref, kept_half, first, chip, seconds[0], acts.at[0], sums.at[0]
@@ -953,9 +1157,9 @@
     attention.to_chip()
     gathers[0].hop(2)
     gathers[0].hop(3)
+    attention.to_all()
     gathers[0].hop(4)
     gathers[1].hop(1)
-    attention.to_all()
     attention.done()
 
     @pl.loop(0, tokens // FF_TILE)
@@ -971,15 +1175,12 @@
         acts[0, rows, :] = (middle * row_scale(middle) * gain_ref[...]).astype(jnp.bfloat16)
         put.wait()
 
-    gathers[0].hop(5)
     take_grad.wait()
 
     def load(part):
         copies = [
             pltpu.make_async_copy(
-                own_ref.at[part] if at == 0 else whole_ref.at[part, at],
-                whole.at[pl.ds(at * width, width)],
-                local.at[3 + at],
+                chunk_block(part, at), whole.at[pl.ds(at * width, width)], local.at[3 + at]
             )
             for at in range(shards)
         ]
@@ -1014,69 +1215,98 @@
             norm_acc[rows, :] = value
 
     count = tokens // FF_TILE
+    mine = pl.ds(pl.multiple_of(core * half, 128), half)
+    other = pl.ds(pl.multiple_of((1 - core) * half, 128), half)
+    norm_sum = CoreSum(
+        hops, out_half, norm_acc.at[mine], first, chip, seconds[1], normsum_ref, sums.at[1]
+    )
+    puts = [
+        pltpu.make_async_copy(total, grads_ref.at[part], local.at[2]) for part in range(parts - 1)
+    ]
+
+    def own_block(part):
+        if part > 0:
+            puts[part - 1].wait()
+        partial(part, 0, total)
+
+    def finish(part):
+        scatter.last(part, total)
+        puts[part].start()
+
+    lates = [
+        pltpu.make_async_copy(
+            late.at[at % 2],
+            late_ref.at[ring_place(place - at + shards, shards)],
+            local.at[3 + shards + at % 2],
+        )
+        for at in range(shards)
+    ]
+
+    def leave(at):
+        if at > 1:
+            lates[at - 2].wait()
+        partial(parts - 1, at, late.at[at % 2])
+        lates[at].start()
+
     load(0)
     tiles(0, 0, 2)
+    gathers[0].hop(5)
+    tiles(0, 2, count)
     gathers[1].hop(2)
-    tiles(0, 2, count)
-    gathers[1].hop(3)
-    gathers[1].hop(4)
-    gathers[2].hop(1)
-    gathers[1].hop(5)
     load(1)
     tiles(1, 0, 2)
-    gathers[2].hop(2)
+    gathers[1].hop(3)
     tiles(1, 2, count)
-    gathers[2].hop(3)
+    scatter.prepare(0, 1)
+    gathers[1].hop(4)
     scatter.hop(0, 1)
-    gathers[2].hop(4)
-    scatter.hop(0, 2)
-    gathers[2].hop(5)
+    scatter.prepare(0, 2)
+    gathers[1].hop(5)
     load(2)
     tiles(2, 0, 2)
+    scatter.hop(0, 2)
+    scatter.prepare(0, 3)
+    tiles(2, 2, count)
+
+    def cast_half(rows):
+        out_half[rows, :] = norm_acc[
+            pl.ds(pl.multiple_of((1 - core) * half + rows.start, ROW_STEP), ROW_STEP), :
+        ].astype(jnp.bfloat16)
+
+    by_rows(half, cast_half)
+    norm_sum.start()
     scatter.hop(0, 3)
-    tiles(2, 2, count)
+    scatter.prepare(0, 4)
+    norm_sum.to_chip()
+    scatter.prepare(1, 1)
+    leave(0)
     scatter.hop(0, 4)
     scatter.hop(1, 1)
-
-    def finish(part):
-        scatter.last(part, total)
-        put = pltpu.make_async_copy(total, grads_ref.at[part], local.at[2])
-        put.start()
-        put.wait()
-
-    mine = pl.ds(pl.multiple_of(core * half, 128), half)
-    other = pl.ds(pl.multiple_of((1 - core) * half, 128), half)
-    out_half[...] = norm_acc[other, :].astype(jnp.bfloat16)
-    norm_sum = CoreSum(
-        hops, out_half, norm_acc.at[mine], first, chip, seconds[1], normsum_ref, sums.at[1]
-    )
-    norm_sum.start()
+    own_block(0)
+    scatter.prepare(1, 2)
+    leave(1)
     finish(0)
     scatter.hop(1, 2)
-    norm_sum.to_chip()
-
-    downs = [
-        pltpu.make_async_copy(
-            (own_ref.at[part] if at == 0 else whole_ref.at[part, at]).at[
-                :, pl.ds(2 * columns, columns)
-            ],
-            whole.at[pl.ds(at * width, width), pl.ds(part * columns, columns)],
-            local.at[3 + at],
-        )
-        for part in range(parts)
-        for at in range(shards)
-    ]
+    scatter.prepare(1, 3)
+    leave(2)
+    leave(3)
     for part in range(parts):
-        for copy in downs[part * shards : (part + 1) * shards]:
+        copies = [
+            pltpu.make_async_copy(
+                chunk_block(part, at).at[:, pl.ds(2 * columns, columns)],
+                whole.at[pl.ds(at * width, width), pl.ds(part * columns, columns)],
+                local.at[3 + at],
+            )
+            for at in range(shards)
+        ]
+        for copy in copies:
             copy.start()
-        for copy in downs[part * shards : (part + 1) * shards]:
+        for copy in copies:
             copy.wait()
     scatter.hop(1, 3)
-    scatter.hop(1, 4)
-    scatter.hop(2, 1)
+    scatter.prepare(1, 4)
+    leave(4)
     norm_sum.to_all()
-    finish(1)
-    scatter.hop(2, 2)
     norm_sum.done()
 
     def down_tile(tile, offset):
@@ -1104,20 +1334,22 @@
         kept_half[rows, :] = down_tile(tile, core * half).astype(jnp.bfloat16)
 
     down_sum.to_chip()
-    scatter.hop(2, 3)
-    scatter.hop(2, 4)
+    scatter.hop(1, 4)
+    own_block(1)
+    for at in range(5, shards):
+        leave(at)
+    finish(1)
     down_sum.to_all()
-    put_norm = pltpu.make_async_copy(acts.at[0], norm_out, local.at[0])
-    put_norm.start()
-    finish(2)
     down_sum.done()
-    put_norm.wait()
+    puts[parts - 2].wait()
+    for copy in lates[-2:]:
+        copy.wait()
     for gather in gathers:
         gather.close()
     scatter.close()
 
 
-def ff_call(sent, kept, rows, grad, gain, own):
+def ff_call(sent, kept, rows, grad, gain, own, early):
     parts, width, columns3 = own.shape
     tokens, wide = rows.shape
     shards = wide // width
@@ -1129,15 +1361,15 @@
     slots = RingScatter.SLOTS
     return pl.pallas_call(
         functools.partial(ff_kernel, shards, parts),
-        in_specs=[anywhere] * 4 + [pl.BlockSpec(memory_space=pltpu.VMEM)] + [anywhere],
+        in_specs=[anywhere] * 4 + [pl.BlockSpec(memory_space=pltpu.VMEM)] + [anywhere] * 2,
         out_specs=[anywhere] * 6,
         out_shape=[
             jax.ShapeDtypeStruct((tokens, wide), jnp.float32),
             jax.ShapeDtypeStruct((tokens, wide), low),
             jax.ShapeDtypeStruct((tokens, wide), low),
-            jax.ShapeDtypeStruct((tokens, wide), low),
-            jax.ShapeDtypeStruct((parts, width, columns3), jnp.float32),
-            jax.ShapeDtypeStruct((parts, shards, width, columns3), low),
+            jax.ShapeDtypeStruct((parts - 1, width, columns3), jnp.float32),
+            jax.ShapeDtypeStruct((shards, width, columns3), low),
+            jax.ShapeDtypeStruct((parts - 1, shards, width, columns3), low),
         ],
         scratch_shapes=[
             pltpu.VMEM((2, tokens, wide), low),
@@ -1147,24 +1379,25 @@
             pltpu.VMEM((2, slots, width, columns3), low),
             pltpu.VMEM((2, slots, width, columns3), low),
             pltpu.VMEM((width, columns3), jnp.float32),
+            pltpu.VMEM((2, width, columns3), low),
         ]
         + [pltpu.VMEM((half, wide), low)] * 6
         + [
             pltpu.VMEM((FF_TILE, wide), low),
             pltpu.VMEM((FF_TILE, wide), jnp.float32),
-            pltpu.SemaphoreType.DMA((parts, 2, legs)),
-            pltpu.SemaphoreType.DMA((parts, 2, legs)),
-            pltpu.SemaphoreType.DMA((2, slots)),
-            pltpu.SemaphoreType.DMA((2, slots)),
-            pltpu.SemaphoreType.REGULAR((2,)),
+            pltpu.SemaphoreType.DMA((parts - 1, 2, legs, HALVES)),
+            pltpu.SemaphoreType.DMA((parts - 1, 2, legs, HALVES)),
+            pltpu.SemaphoreType.DMA((2, slots, HALVES)),
+            pltpu.SemaphoreType.DMA((2, slots, HALVES)),
+            pltpu.SemaphoreType.REGULAR((2, HALVES)),
             pltpu.SemaphoreType.DMA((3, 2, 4)),
-            pltpu.SemaphoreType.DMA((3 + shards,)),
+            pltpu.SemaphoreType.DMA((5 + shards,)),
         ],
         compiler_params=pltpu.CompilerParams(
             collective_id=1, has_side_effects=True, vmem_limit_bytes=RING_LIMIT
         ),
         name="ff_ring",
-    )(sent, kept, rows, grad, gain, own)
+    )(sent, kept, rows, grad, gain, own, early)
 
 
 def tail_kernel(shards, jobs, *refs):
@@ -1207,26 +1440,29 @@
     norm_sum = CoreSum(
         hops, sent_ref, kept_half, first, chip, second, sum_ref, sums.at[0]
     )
+    puts = [pltpu.make_async_copy(total, grads_ref.at[job], local.at[0]) for job in range(2)]
     norm_sum.start()
     for copy in take:
         copy.start()
     for copy in take:
         copy.wait()
+    scatter.prepare(0, 1)
     scatter.hop(0, 1)
+    scatter.prepare(1, 1)
     scatter.hop(1, 1)
     norm_sum.to_chip()
-    scatter.hop(0, 2)
-    scatter.hop(1, 2)
-    scatter.hop(0, 3)
-    scatter.hop(1, 3)
-    scatter.hop(0, 4)
-    scatter.hop(1, 4)
+    for step in range(2, legs + 1):
+        for job in range(2):
+            scatter.prepare(job, step)
+            scatter.hop(job, step)
+    for job in range(2):
+        if job > 0:
+            puts[job - 1].wait()
+        partial(job, 0, total)
+        scatter.last(job, total)
+        puts[job].start()
     norm_sum.to_all()
-    for job in range(2):
-        scatter.last(job, total)
-        put = pltpu.make_async_copy(total, grads_ref.at[job], local.at[0])
-        put.start()
-        put.wait()
+    puts[1].wait()
     norm_sum.done()
     scatter.close()
 
@@ -1254,9 +1490,9 @@
         ]
         + [pltpu.VMEM((half, wide), low)] * 4
         + [
-            pltpu.SemaphoreType.DMA((2, slots)),
-            pltpu.SemaphoreType.DMA((2, slots)),
-            pltpu.SemaphoreType.REGULAR((2,)),
+            pltpu.SemaphoreType.DMA((2, slots, HALVES)),
+            pltpu.SemaphoreType.DMA((2, slots, HALVES)),
+            pltpu.SemaphoreType.REGULAR((2, HALVES)),
             pltpu.SemaphoreType.DMA((1, 2, 4)),
             pltpu.SemaphoreType.DMA((3,)),
         ],
@@ -1265,6 +1501,207 @@
         ),
         name="tail_ring",
     )(sent, kept, norm, grad, *rights)
+
+
+ATTENTION_ROWS = 256
+
+
+def head_turn(raw, cosine, sine, gain):
+    scaled = raw * row_scale(raw) * gain
+    return scaled * cosine + pltpu.roll(scaled, HEAD_SIZE // 2, 1) * sine
+
+
+def head_back(grad, raw, cosine, sine, gain):
+    turned = grad * cosine - pltpu.roll(grad, HEAD_SIZE // 2, 1) * sine
+    scale = row_scale(raw)
+    unit = raw * scale
+    inner = turned * gain
+    raw_grad = scale * (inner - unit * jnp.mean(inner * unit, axis=-1, keepdims=True))
+    return raw_grad, jnp.sum(turned * unit, axis=0, keepdims=True)
+
+
+def turn_body(query_cols, key_cols, lefts, whole, extras, outs):
+    normed, cosine_ref, sine_ref = lefts
+    query_raw, key_raw, query_out, key_out, value_out = outs
+    cosine, sine = cosine_ref[...], sine_ref[...]
+    raw = rows_times(normed[...], whole[:, : query_cols + key_cols])
+    query_raw[...] = raw[:, :query_cols]
+    key_raw[...] = raw[:, query_cols:]
+    value_out[...] = rows_times(normed[...], whole[:, query_cols + key_cols :]).astype(
+        value_out.dtype
+    )
+    for out, base, gain in ((query_out, 0, 0), (key_out, query_cols, 1)):
+        for start in range(0, out.shape[1], HEAD_SIZE):
+            out[:, start : start + HEAD_SIZE] = head_turn(
+                raw[:, base + start : base + start + HEAD_SIZE],
+                cosine,
+                sine,
+                extras[0][gain : gain + 1, :],
+            ).astype(out.dtype)
+    return []
+
+
+def attention_probs(query, keys, first_ref, row_start):
+    rows, stop = query.shape[0], keys.shape[0]
+    scores = contract_cols(query, keys) * (1.0 / math.sqrt(HEAD_SIZE))
+    column = lax.broadcasted_iota(jnp.int32, (rows, stop), 1)
+    row = lax.broadcasted_iota(jnp.int32, (rows, stop), 0) + row_start
+    first = first_ref[row_start : row_start + rows, :]
+    scores = jnp.where((column <= row) & (column >= first), scores, MASKED)
+    exponent = jnp.exp(scores - jnp.max(scores, axis=-1, keepdims=True))
+    return exponent * (1.0 / jnp.sum(exponent, axis=-1, keepdims=True))
+
+
+def attention_body(query_ref, key_ref, value_ref, first_ref, out_ref):
+    low = out_ref.dtype
+    for start in range(0, query_ref.shape[1], HEAD_SIZE):
+        head = slice(start, start + HEAD_SIZE)
+        for row in range(0, query_ref.shape[0], ATTENTION_ROWS):
+            rows, stop = slice(row, row + ATTENTION_ROWS), row + ATTENTION_ROWS
+            probs = attention_probs(query_ref[rows, head], key_ref[:stop, :], first_ref, row)
+            out_ref[rows, head] = rows_times(probs.astype(low), value_ref[:stop, :]).astype(low)
+
+
+def attention_back_body(
+    query_ref,
+    key_ref,
+    value_ref,
+    grad_ref,
+    query_raw,
+    key_raw,
+    cosine_ref,
+    sine_ref,
+    gain_ref,
+    first_ref,
+    query_out,
+    key_out,
+    value_out,
+    sums_ref,
+    key_acc,
+    value_acc,
+):
+    low = query_out.dtype
+    scale = 1.0 / math.sqrt(HEAD_SIZE)
+    key_acc[...] = jnp.zeros_like(key_acc)
+    value_acc[...] = jnp.zeros_like(value_acc)
+    query_sum = jnp.zeros((1, HEAD_SIZE), jnp.float32)
+    for start in range(0, query_ref.shape[1], HEAD_SIZE):
+        head = slice(start, start + HEAD_SIZE)
+        for row in range(0, query_ref.shape[0], ATTENTION_ROWS):
+            rows, stop = slice(row, row + ATTENTION_ROWS), row + ATTENTION_ROWS
+            query, grad = query_ref[rows, head], grad_ref[rows, head]
+            probs = attention_probs(query, key_ref[:stop, :], first_ref, row)
+            prob_grad = contract_cols(grad, value_ref[:stop, :])
+            inner = jnp.sum(probs * prob_grad, axis=-1, keepdims=True)
+            score_grad = (probs * (prob_grad - inner)).astype(low)
+            key_acc[:stop, :] += contract_rows(score_grad, query)
+            value_acc[:stop, :] += contract_rows(probs.astype(low), grad)
+            query_grad = (rows_times(score_grad, key_ref[:stop, :]) * scale).astype(low)
+            raw_grad, gain_grad = head_back(
+                query_grad.astype(jnp.float32),
+                query_raw[rows, head],
+                cosine_ref[rows, :],
+                sine_ref[rows, :],
+                gain_ref[0:1, :],
+            )
+            query_out[rows, head] = raw_grad.astype(low)
+            query_sum += gain_grad
+    key_sum = jnp.zeros((1, HEAD_SIZE), jnp.float32)
+    for row in range(0, key_ref.shape[0], ATTENTION_ROWS):
+        rows = slice(row, row + ATTENTION_ROWS)
+        key_grad = (key_acc[rows, :] * scale).astype(low)
+        raw_grad, gain_grad = head_back(
+            key_grad.astype(jnp.float32),
+            key_raw[rows, :],
+            cosine_ref[rows, :],
+            sine_ref[rows, :],
+            gain_ref[1:2, :],
+        )
+        key_out[rows, :] = raw_grad.astype(low)
+        key_sum += gain_grad
+    value_out[...] = value_acc[...].astype(low)
+    sums_ref[0:1, :] = query_sum
+    sums_ref[1:2, :] = key_sum
+
+
+def by_group(body, arrays, outs, groups, name, scratch=(), whole=()):
+    tokens = arrays[0].shape[0]
+
+    def columns(width):
+        return pl.BlockSpec((tokens, width // groups), lambda group: (0, group))
+
+    pair = tokens * tokens * arrays[0].shape[1]
+    return pl.pallas_call(
+        body,
+        grid=(groups,),
+        in_specs=[columns(array.shape[1]) for array in arrays]
+        + [pl.BlockSpec(array.shape, lambda group: (0, 0)) for array in whole],
+        out_specs=[
+            columns(out.shape[1])
+            if len(out.shape) == 2
+            else pl.BlockSpec((None, *out.shape[1:]), lambda group: (group, 0, 0))
+            for out in outs
+        ],
+        out_shape=list(outs),
+        scratch_shapes=list(scratch),
+        cost_estimate=pl.CostEstimate(
+            flops=4 * pair, bytes_accessed=tokens * 4096, transcendentals=pair // 128
+        ),
+        name=name,
+    )(*arrays, *whole)
+
+
+def gains_body(shards, pieces, out_ref, came, total, late, sums):
+    hops = Hops(shards)
+    place = place_of(lax.axis_index("fsdp"), shards)
+    peers = [{"fsdp": ring_place(place - at + shards, shards)} for at in range(1, shards)]
+    hops.meet([*peers, hops.partner, hops.across])
+    copies = [
+        remote(
+            pieces.at[at], came.at[at - 1], sums.at[0, at - 1], sums.at[1, at - 1], peers[at - 1]
+        )
+        for at in range(1, shards)
+    ]
+    for copy in copies:
+        copy.start()
+    value = pieces[0]
+    for at in range(1, shards):
+        copies[at - 1].wait_recv()
+        value += came[at - 1]
+    for stage, peer in enumerate((hops.partner, hops.across)):
+        total[stage] = value
+        copy = remote(
+            total.at[stage],
+            late.at[stage],
+            sums.at[0, shards - 1 + stage],
+            sums.at[1, shards - 1 + stage],
+            peer,
+        )
+        copy.start()
+        copy.wait()
+        value += late[stage]
+    own = lax.broadcasted_iota(jnp.int32, value.shape, 1) < value.shape[1] - HEAD_SIZE
+    out_ref[...] = jnp.where(own, total[0], value)
+    for copy in copies:
+        copy.wait_send()
+
+
+def gains_call(pieces):
+    shards, rows, columns = pieces.shape
+    return pl.pallas_call(
+        functools.partial(gains_body, shards),
+        in_specs=[pl.BlockSpec(memory_space=pltpu.VMEM)],
+        out_specs=pl.BlockSpec(memory_space=pltpu.VMEM),
+        out_shape=jax.ShapeDtypeStruct((rows, columns), pieces.dtype),
+        scratch_shapes=[
+            pltpu.VMEM((shards - 1, rows, columns), pieces.dtype),
+            pltpu.VMEM((2, rows, columns), pieces.dtype),
+            pltpu.VMEM((2, rows, columns), pieces.dtype),
+            pltpu.SemaphoreType.DMA((2, shards + 1)),
+        ],
+        compiler_params=pltpu.CompilerParams(collective_id=3, has_side_effects=True),
+        name="gain_sums",
+    )(pieces)
 
 
 def ring_device(
@@ -1308,10 +1745,7 @@
     low = jnp.bfloat16
     packed_token_count, width = layer_input.shape
     query_cols, key_cols = query_weight.shape[1], key_weight.shape[1]
-    local_query = query_cols // HEAD_SIZE
     local_groups = key_cols // HEAD_SIZE
-    query_group_width = local_query // local_groups
-    score_scale = 1.0 / math.sqrt(HEAD_SIZE)
     chunk_cols = down_weight.shape[1] // FF_CHUNKS
     states = [
         (query_weight, query_weight_mean, query_weight_square),
@@ -1335,11 +1769,6 @@
     )
     own_gains = jnp.concatenate([norm_gains, headnorm_gains], axis=1).astype(low)
     own_gains = jnp.pad(own_gains, ((0, 14), (0, -own_gains.shape[1] % 128)))
-    attention_full, gains = gather_call(attention_block, own_gains, shards)
-    attention_full = attention_full.reshape(width, -1)
-    gains = jnp.swapaxes(gains[:, :2].astype(jnp.float32), 0, 1)
-    norm_gain = gains[:, :, :gain_cols].reshape(2, 1, -1)
-    head_gain = gains[:, :, gain_cols : gain_cols + head_cols][:, back].reshape(2, -1)
     inward_window = (query_cols + 2 * key_cols, 0)
     outward_window = (query_cols, (query_cols + 2 * key_cols) // query_cols)
     ff_block = jnp.stack(
@@ -1358,84 +1787,50 @@
         ]
     )
     token_positions = positions_of(segment_ids)
-    token_index = jnp.arange(packed_token_count, dtype=jnp.int32)
-
-    def head_map(projected, gain, heads):
-        return rotary_embedding(
-            root_mean_scale(projected.reshape(packed_token_count, heads, HEAD_SIZE)) * gain,
-            token_positions,
-        )
-
-    input_rows, grad_low, normed_one = row_call(
-        turned_in, scalars, [layer_input, out_grad], [norm_gain[0]], [low, low, low]
-    )
-    query_proj, key_projected, value_projected = full_call(
-        functools.partial(
-            project_body, (query_cols, query_cols + key_cols, query_cols + 2 * key_cols)
-        ),
-        scalars,
-        [normed_one],
+    first_key = (jnp.arange(packed_token_count, dtype=jnp.int32) - token_positions)[:, None]
+    frequencies = ROPE_BASE ** (
+        -2.0 * jnp.arange(HEAD_SIZE // 2).astype(jnp.float32) / HEAD_SIZE
+    )
+    angles = token_positions.astype(jnp.float32)[:, None] * frequencies[None, :]
+    cosine = jnp.tile(jnp.cos(angles), (1, 2))
+    sine = jnp.sin(angles)
+    sine = jnp.concatenate([-sine, sine], axis=1)
+
+    (
         attention_full,
-        inward_window,
-        [(query_cols, jnp.float32), (key_cols, jnp.float32), (key_cols, low)],
-        [],
-        "project",
-    )
-    query_heads = (
-        head_map(query_proj, head_gain[0], local_query)
-        .astype(low)
-        .reshape(packed_token_count, local_groups, query_group_width, HEAD_SIZE)
-    )
-    per_head_keys = head_map(key_projected, head_gain[1], local_groups).astype(low)
-    per_head_values = value_projected.reshape(packed_token_count, local_groups, HEAD_SIZE)
-    block_rows = min(512, packed_token_count)
-    block_count = packed_token_count // block_rows
-
-    def block_scores(row_start, row_stop):
-        raw_scores = (
-            jnp.einsum(
-                "qhgd,khd->hgqk",
-                query_heads[row_start:row_stop],
-                per_head_keys[:row_stop],
-                preferred_element_type=jnp.float32,
-            )
-            * score_scale
-        )
-        allowed = (segment_ids[row_start:row_stop, None] == segment_ids[None, :row_stop]) & (
-            token_index[None, :row_stop] <= token_index[row_start:row_stop, None]
-        )
-        return jnp.where(allowed, raw_scores, MASKED)
-
-    mixed_blocks = []
-    log_sums = []
-    for block_index in range(block_count):
-        row_start = block_index * block_rows
-        row_stop = row_start + block_rows
-        scores = block_scores(row_start, row_stop)
-        row_max = jnp.max(scores, axis=-1, keepdims=True)
-        exponent = jnp.exp(scores - row_max)
-        row_sum = jnp.sum(exponent, axis=-1, keepdims=True)
-        weights_block = (exponent / row_sum).astype(low)
-        log_sums.append(row_max + jnp.log(row_sum))
-        mixed_blocks.append(
-            jnp.einsum(
-                "hgqk,khd->qhgd",
-                weights_block,
-                per_head_values[:row_stop],
-                preferred_element_type=jnp.float32,
-            )
-        )
-    mixed = (
-        jnp.concatenate(mixed_blocks, axis=0)
-        .reshape(packed_token_count, local_query * HEAD_SIZE)
-        .astype(low)
-    )
-    kept, sent = full_call(
-        back_body, scalars, [mixed], attention_full, outward_window, [], [(width, low)], "attention_out"
-    )
-    middle, normed_two, norm_sum, down_sum, ff_sums, _ = ff_call(
-        sent, kept, input_rows, grad_low, norm_gain[1], ff_block
-    )
+        gains,
+        ff_early,
+        input_rows,
+        grad_low,
+        normed_one,
+        query_raw,
+        key_raw,
+        query_heads,
+        key_heads,
+        value_heads,
+        mixed,
+        kept,
+        sent,
+    ) = gather_call(
+        attention_block,
+        own_gains,
+        layer_input,
+        out_grad,
+        ff_block,
+        cosine,
+        sine,
+        first_key,
+        gain_cols,
+        (query_cols, key_cols),
+    )
+    attention_full = attention_full.reshape(width, -1)
+    gains = jnp.swapaxes(gains[:, :2].astype(jnp.float32), 0, 1)
+    norm_gain = gains[:, :, :gain_cols].reshape(2, 1, -1)
+    head_gain = gains[:, :, gain_cols : gain_cols + head_cols][:, back].reshape(2, -1)
+    middle, norm_sum, down_sum, ff_sums, ff_late, _ = ff_call(
+        sent, kept, input_rows, grad_low, norm_gain[1], ff_block, ff_early
+    )
+    ff_last = lax.psum_scatter(ff_late, "fsdp", scatter_dimension=0, tiled=False)
     middle_grad, middle_grad_low, gain_two_grad = row_call(
         second_back,
         scalars,
@@ -1454,70 +1849,20 @@
         [],
         "mixed_back",
     )
-    mixed_grad = mixed_grad.reshape(packed_token_count, local_groups, query_group_width, HEAD_SIZE)
-    query_grad_blocks = []
-    key_grad_acc = jnp.zeros((packed_token_count, local_groups, HEAD_SIZE), jnp.float32)
-    value_grad_acc = jnp.zeros((packed_token_count, local_groups, HEAD_SIZE), jnp.float32)
-    for block_index in range(block_count):
-        row_start = block_index * block_rows
-        row_stop = row_start + block_rows
-        scores = block_scores(row_start, row_stop)
-        probs = jnp.exp(scores - log_sums[block_index])
-        grad_block = mixed_grad[row_start:row_stop]
-        prob_grad = jnp.einsum(
-            "qhgd,khd->hgqk",
-            grad_block,
-            per_head_values[:row_stop],
-            preferred_element_type=jnp.float32,
-        )
-        row_inner = jnp.sum(probs * prob_grad, axis=-1, keepdims=True)
-        score_grad = (probs * (prob_grad - row_inner)).astype(low)
-        query_grad_blocks.append(
-            jnp.einsum(
-                "hgqk,khd->qhgd",
-                score_grad,
-                per_head_keys[:row_stop],
-                preferred_element_type=jnp.float32,
-            )
-            * score_scale
-        )
-        key_grad_acc = key_grad_acc.at[:row_stop].add(
-            jnp.einsum(
-                "hgqk,qhgd->khd",
-                score_grad,
-                query_heads[row_start:row_stop],
-                preferred_element_type=jnp.float32,
-            )
-            * score_scale
-        )
-        value_grad_acc = value_grad_acc.at[:row_stop].add(
-            jnp.einsum(
-                "hgqk,qhgd->khd",
-                probs.astype(low),
-                grad_block,
-                preferred_element_type=jnp.float32,
-            )
-        )
-    query_grad_heads = (
-        jnp.concatenate(query_grad_blocks, axis=0)
-        .reshape(packed_token_count, local_query, HEAD_SIZE)
-        .astype(low)
-        .astype(jnp.float32)
-    )
-    key_grad_heads = key_grad_acc.astype(low).astype(jnp.float32)
-    value_grad_low = value_grad_acc.astype(low).reshape(
-        packed_token_count, local_groups * HEAD_SIZE
-    )
-    query_map_out, query_map_back = jax.vjp(
-        lambda projected, gain: head_map(projected, gain, local_query), query_proj, head_gain[0]
-    )
-    query_proj_grad, head_query_grad = query_map_back(query_grad_heads)
-    key_map_out, key_map_back = jax.vjp(
-        lambda projected, gain: head_map(projected, gain, local_groups), key_projected, head_gain[1]
-    )
-    key_proj_grad, head_key_grad = key_map_back(key_grad_heads)
-    query_proj_low = query_proj_grad.astype(low)
-    key_proj_low = key_proj_grad.astype(low)
+    query_proj_low, key_proj_low, value_grad_low, head_sums = by_group(
+        attention_back_body,
+        [query_heads, key_heads, value_heads, mixed_grad, query_raw, key_raw],
+        [
+            jax.ShapeDtypeStruct(query_heads.shape, low),
+            jax.ShapeDtypeStruct(key_heads.shape, low),
+            jax.ShapeDtypeStruct(key_heads.shape, low),
+            jax.ShapeDtypeStruct((local_groups, 2, HEAD_SIZE), jnp.float32),
+        ],
+        local_groups,
+        "attention_back",
+        scratch=[pltpu.VMEM((packed_token_count, HEAD_SIZE), jnp.float32)] * 2,
+        whole=[cosine, sine, head_gain, first_key],
+    )
     kept, sent = full_call(
         back_body,
         scalars,
@@ -1538,22 +1883,6 @@
         shards,
     )
     (layer_output,) = row_call(layer_out, scalars, [middle, down_sum], [], [jnp.float32])
-    head_grads = jnp.stack([head_query_grad, head_key_grad])
-    head_grads = head_grads + lax.ppermute(head_grads, "tensor", CORE_PAIRS)
-    head_grads = head_grads + lax.ppermute(head_grads, "tensor", CHIP_PAIRS)
-    head_pieces = head_grads.reshape(2, shards, head_cols)[:, turn]
-    early_pieces = [
-        jnp.concatenate(
-            [
-                gain_two_grad[:, at * gain_cols : (at + 1) * gain_cols],
-                head_pieces[0:1, at],
-                head_pieces[1:2, at],
-            ],
-            axis=1,
-        )
-        for at in range(shards)
-    ]
-    early_sum = functools.reduce(jnp.add, spread(early_pieces, shards))
     input_grad, gain_one_grad = row_call(
         first_back,
         scalars,
@@ -1562,18 +1891,27 @@
         [jnp.float32],
         sums=1,
     )
-    late_pieces = spread(
-        [gain_one_grad[:, at * gain_cols : (at + 1) * gain_cols] for at in range(shards)], shards
-    )
+    head_grads = jnp.sum(head_sums, axis=0).reshape(2, shards, head_cols)[:, turn]
+    pieces = jnp.concatenate(
+        [
+            jnp.sum(gain_one_grad, axis=0).reshape(shards, 1, gain_cols),
+            jnp.sum(gain_two_grad, axis=0).reshape(shards, 1, gain_cols),
+            jnp.pad(
+                jnp.swapaxes(head_grads, 0, 1).reshape(shards, 1, 2 * head_cols),
+                ((0, 0), (0, 0), (0, HEAD_SIZE - 2 * head_cols)),
+            ),
+        ],
+        axis=2,
+    )
+    gain_sums = gains_call(pieces)
     ff_updates = adam_update(
-        ff_sums, [(0, 0), (0, 1), (1, None)], states[4:6], parts=FF_CHUNKS
-    )
-    inner_updates = adam_update(attention_sums[0], [(0, None), (1, None)], states[0:2])
-    outer_updates = adam_update(attention_sums[1], [(0, None), (1, None)], states[2:4])
-    late_sum = functools.reduce(jnp.add, late_pieces)
+        [ff_sums[0], ff_sums[1], ff_last], [(0, 0), (0, 1), (1, None)], states[4:6]
+    )
+    inner_updates = adam_update([attention_sums[0]], [(0, None), (1, None)], states[0:2])
+    outer_updates = adam_update([attention_sums[1]], [(0, None), (1, None)], states[2:4])
     gain_shards = [
-        jnp.concatenate([late_sum, early_sum[:, :gain_cols]], axis=0),
-        early_sum[:, gain_cols:].reshape(2, head_cols),
+        gain_sums[:, : 2 * gain_cols].reshape(2, gain_cols),
+        gain_sums[:, 2 * gain_cols : 2 * gain_cols + 2 * head_cols].reshape(2, head_cols),
     ]
     updates = [inner_updates[:4], inner_updates[4:], outer_updates[:4], outer_updates[4:]]
     updates += [ff_updates[:4], ff_updates[4:]]

time: 823 us -> 725 us (0.88)
  other arithmetic: 57.3 us -> 22.6 us
  local copies, waits for them, and re-layouts: 37.7 us -> 15.9 us
  matrix products: 21.8 us -> 0 us
  starting transfers between devices: 21.8 us -> 0.04 us
  between operations: 2.61 us -> 15.2 us
    pallas_call x1, Pallas kernels: 414 us -> 298 us  [ff_call(): pl.pallas_call(functools.partial(ff_kernel, shards, parts), in_specs=[any...]
    pallas_call x4 -> x6, Pallas kernels: 103 us -> 201 us  [the longest x1 141 us: gather_call(): pl.pallas_call(functools.partial(gather_body, shards, gain_cols, query_co...]
    pallas_call x1, Pallas kernels: 70.9 us -> 98.4 us  [tail_call(): pl.pallas_call(functools.partial(tail_kernel, shards, jobs), in_specs=[an...]
    dot_general x12 -> x0, matrix products: 21.8 us -> none  [the longest x2 8.7 us: ring_device(): jnp.einsum('qhgd,khd->hgqk', grad_block, per_head_values[:row_stop], pref...]
    ppermute x16 -> x0, starting transfers between devices: 21.8 us -> none  [the longest x14 21.3 us: spread(): lax.ppermute(pieces[shards - step], 'fsdp', ring_pairs(shards, step))]
    pallas_call x4 -> x2, Pallas kernels: 34.2 us -> 17.2 us  [full_call(): pl.pallas_call(kernel, grid_spec=pltpu.PrefetchScalarGridSpec(num_scalar_...]
    convert_element_type x6 -> x1, other arithmetic: 13.4 us -> 0.01 us  [ring_device(): angles = token_positions.astype(jnp.float32)[:, None] * frequencies[None, :]]
    reduce_sum x6 -> x3, other arithmetic: 14.5 us -> 2.42 us  [the longest x1 0.86 us: ring_device(): jnp.sum(gain_two_grad, axis=0).reshape(shards, 1, gain_cols)]
  transfers between devices with their start and end apart: 16 -> 1, of which waited for: 2 -> 0; matrix products, arithmetic and copies ran while one was open for 3% -> 2% of each run, Pallas kernels for 16% -> 29%
where the time goes in v3:
time: 725 us; the launch traced here: 717 us
  Pallas kernels  663 us (91%)
  other arithmetic  22.6 us (3%)
  local copies, waits for them, and re-layouts  15.9 us (2%)
  between operations  15.2 us (2%)
    pallas_call x1, Pallas kernels, ff_call(): pl.pallas_call(functools.partial(ff_kernel, shards, parts), in_specs=[any...  298 us
    pallas_call x1, Pallas kernels, gather_call(): pl.pallas_call(functools.partial(gather_body, shards, gain_cols, query_co...  141 us
    pallas_call x1, Pallas kernels, tail_call(): pl.pallas_call(functools.partial(tail_kernel, shards, jobs), in_specs=[an...  98.4 us
    pallas_call x3, Pallas kernels, row_call(): pl.pallas_call(body, grid_spec=pltpu.PrefetchScalarGridSpec(num_scalar_pr...  48.1 us
    pallas_call x3, Pallas kernels, adam_update(): pl.pallas_call(functools.partial(adam_body, places, parts), grid=(parts,...  27 us
    pallas_call x1, Pallas kernels, by_group(): pl.pallas_call(body, grid=(groups,), in_specs=[columns(array.shape[1]) fo...  21 us
    pallas_call x2, Pallas kernels, full_call(): pl.pallas_call(kernel, grid_spec=pltpu.PrefetchScalarGridSpec(num_scalar_...  17.2 us
  transfers between devices with their start and end apart: 1, of which 0 were waited for; matrix products, arithmetic and copies ran while one was open for 2% of the time, Pallas kernels for 29%

profile of v3, /device:TPU:0, one launch (start us, length us, event | category | flops | bytes accessed | tf_op | source)
XLA Modules:
  0.0 717.1 jit_solution(13965908061042718526)
XLA Ops:
  7.3 0.8 convert.21
  8.1 0.7 convert.20
  8.8 1.3 convert_reduce_fusion
  10.1 1.0 convert_element_type.63
  11.1 1.6 convert_element_type.64
  12.7 1.8 convert_element_type.62
  14.5 1.8 convert_element_type.65
  16.5 0.9 subtract_subtract_fusion.refs_7_.first_ref
  17.4 0.9 fusion.17
  18.3 3.1 fusion
  21.4 1.2 copy.80
  22.7 0.9 tile.4
  23.5 2.0 copy.82.refs_5_.cosine_ref
  25.9 0.6 fusion.7.refs_1_
  26.9 1.0 pad_maximum_fusion.2.refs_6_.sine_ref
  28.2 1.7 pad_maximum_fusion.refs_4_.refs_5_
  29.8 0.9 pad_maximum_fusion.1.refs_0_
  30.8 141.1 %gather_ring.1 = (bf16[8,256,1536]{2,1,0:T(8,128)(2,1)}, bf16[8,16,384]{2,1,0:T(8,128)(2,1)}, bf16[8,256,1536]{2,1,0:T(8,128)(2,1)}, bf16[1024,2048]{1,0:T(8,128...) custom-call(bf16[256,1536]{1,0:T(8,128)(2,1)} %pad_maximum_fusion.1., ...), custom_call_target="tpu_custom_call" | custom-call | tf_op jit(solution)/shard_map/gather_ring/pallas_call | solution.py:1060
  171.9 0.8 convert_bitcast_fusion
  172.7 0.6 fusion.18
  173.3 298.2 %ff_ring.1 = (f32[1024,2048]{1,0:T(8,128)}, bf16[1024,2048]{1,0:T(8,128)(2,1)}, bf16[1024,2048]{1,0:T(8,128)(2,1)}, f32[2,256,1536]{2,1,0:T(8,128)}, bf16[8,256,...) custom-call(bf16[512,2048]{1,0:T(8,128)(2,1)} %get-tuple-element.90.refs_0_, ...), custom_call_target="tpu_custom_call" | custom-call | tf_op jit(solution)/shard_map/ff_ring/pallas_call | solution.py:1362
  472.1 0.6 gather_fusion
  472.7 0.6 reshape.584.gain_ref
  473.4 0.6 concatenate.45.scalars
  474.0 19.1 %second_back.1 = (f32[1024,2048]{1,0:T(8,128)}, bf16[1024,2048]{1,0:T(8,128)(2,1)}, f32[8,2048]{1,0:T(8,128)}) custom-call(s32[9]{0:T(128)} %concatenate.45.scalars, f32[1024,2048]{1,0:T(8,128)} %get-tuple-element.96.mid_ref, bf16[1024,2048]{1,0:T(8,128)(2,1)} %get-tuple-element.93.refs_3_.g_ref, bf16[1024,2048]{1,0:T(8,128)(2,1)} %get-tuple-element.98.came_ref, ...), custom_call_target="tpu_custom_call" | custom-call | flops 16777216 | bytes 25165824 | tf_op jit(solution)/shard_map/second_back/pallas_call | solution.py:440
  493.1 0.9 reduce_sum.41
  493.9 6.9 mixed_back.1.grad_ref
  500.9 21.0 %attention_back.1 = (bf16[1024,512]{1,0:T(8,128)(2,1)}, bf16[1024,256]{1,0:T(8,128)(2,1)}, bf16[1024,256]{1,0:T(8,128)(2,1)}, f32[2,2,128]{2,1,0:T(2,128)}) custom-call(bf16[1024,512]{1,0:T(8,128)(2,1)} %get-tuple-element.100.query_ref, bf16[1024,256]{1,0:T(8,128)(2,1)} %get-tuple-element.101.key_ref, bf16[1024,256]{1,0:T(8,128)(2,1)} %get-tuple-element.102.value_ref, ...), custom_call_target="tpu_custom_call" | custom-call | flops 2147483648 | bytes 4194304 | tf_op jit(solution)/shard_map/attention_back/pallas_call | solution.py:1634
  521.9 0.7 reduce_sum.42
  522.8 0.6 gather_fusion.1
  523.5 10.3 %projection_back.1 = (bf16[512,2048]{1,0:T(8,128)(2,1)}, bf16[512,2048]{1,0:T(8,128)(2,1)}) custom-call(s32[9]{0:T(128)} %concatenate.45.scalars, bf16[1024,512]{1,0:T(8,128)(2,1)} %get-tuple-element.107.refs_0_.refs_4_, bf16[1024,256]{1,0:T(8,128)(2,1)} %get-tuple-element.108.refs_1_.refs_5_, bf16[1024,256]{1,0:T(8,128)(2,1)} %get-tuple-element.109.refs_2_.refs_6_, ...), custom_call_target="tpu_custom_call" | custom-call | flops 4294967296 | bytes 17179868 | tf_op jit(solution)/shard_map/projection_back/pallas_call | solution.py:589
  533.8 1.2 copy-done.1
  535.0 1.0 copy-done.3
  536.1 98.4 %tail_ring.1 = (bf16[1024,2048]{1,0:T(8,128)(2,1)}, f32[2,256,768]{2,1,0:T(8,128)S(1)}) custom-call(bf16[512,2048]{1,0:T(8,128)(2,1)} %get-tuple-element.110.refs_0_, bf16[512,2048]{1,0:T(8,128)(2,1)} %get-tuple-element.111.refs_1_, bf16[1024,2048]{1,0:T(8,128)(2,1)} %get-tuple-element.112.refs_2_, bf16[1024,2048]{1,0:T(8,128)(2,1)} %get-tuple-element.103.refs_0_.refs_3_, ...), custom_call_target="tpu_custom_call" | custom-call | tf_op jit(solution)/shard_map/tail_ring/pallas_call | solution.py:1477
  634.5 18.0 %first_back.1 = (f32[1024,2048]{1,0:T(8,128)}, f32[8,2048]{1,0:T(8,128)}) custom-call(s32[9]{0:T(128)} %concatenate.45.scalars, f32[1024,2048]{1,0:T(8,128)} %get-tuple-element.99.dx_ref, bf16[1024,2048]{1,0:T(8,128)(2,1)} %get-tuple-element.92.refs_2_.x_ref, bf16[1024,2048]{1,0:T(8,128)(2,1)} %get-tuple-element.114.came_ref, f32[1,2048]{1,0:T(1,128)} %bitcast.65), custom_call_target="tpu_custom_call" | custom-call | flops 16777216 | bytes 25165824 | tf_op jit(solution)/shard_map/first_back/pallas_call | solution.py:440
  652.5 0.9 reduce_sum.40
  653.4 0.6 fusion.4.pieces
  654.0 12.1 %gain_sums.1 = f32[1,640]{1,0:T(1,128)} custom-call(f32[8,1,640]{2,1,0:T(1,128)} %fusion.4.pieces), custom_call_target="tpu_custom_call" | custom-call | tf_op jit(solution)/shard_map/gain_sums/pallas_call | solution.py:1691
  666.1 0.7 slice_reduce_fusion
  666.8 0.6 slice_reduce_fusion.1
  667.5 1.2 slice_bitcast_fusion.2
  668.7 4.4 adam_update.4
  673.2 4.3 adam_update.3
  677.6 11.0 %layer_out.1 = f32[1024,2048]{1,0:T(8,128)} custom-call(s32[9]{0:T(128)} %concatenate.45.scalars, f32[1024,2048]{1,0:T(8,128)} %get-tuple-element.96.mid_ref, bf16[1024,2048]{1,0:T(8,128)(2,1)} %get-tuple-element.97.came_ref), custom_call_target="tpu_custom_call" | custom-call | flops 16777216 | bytes 25165824 | tf_op jit(solution)/shard_map/layer_out/pallas_call | solution.py:440
  688.6 0.6 subtract_subtract_fusion.2
  689.2 0.6 subtract_subtract_fusion.1
  689.8 1.8 slice_bitcast_fusion
  691.7 18.3 %adam_update.5 = (f32[2,256,1536]{2,1,0:T(8,128)}, f32[2,256,1536]{2,1,0:T(8,128)}, f32[2,256,1536]{2,1,0:T(8,128)}, f32[2,256,1536]{2,1,0:T(8,128)}, f32[256,15...) custom-call(f32[256,1536]{1,0:T(8,128)} %get-tuple-element.153.refs_0_, ...), custom_call_target="tpu_custom_call" | custom-call | flops 23592960 | bytes 37748736 | tf_op jit(solution)/shard_map/adam_update/pallas_call | solution.py:668
  (67 shorter events, 1.8 us)
Async XLA Ops:
  7.2 10.1 %copy-start.5 = (f32[256,1536]{1,0:T(8,128)S(1)}, f32[256,1536]{1,0:T(8,128)}, u32[]{:S(2)}) copy-start(f32[256,1536]{1,0:T(8,128)} %refs_6_.5) | copy-start | bytes 4718596
  7.2 684.4 %reduce-scatter.2.cloned.1.call-start = ((), (), s32[]{:S(2)}) async-start(), calls=%async_computation.1 | async-start | bytes 7077888 | tf_op jit(solution)/shard_map/reduce_scatter | solution.py:1833
  18.3 7.2 %copy-start.4 = (f32[2,256,1536]{2,1,0:T(8,128)S(1)}, f32[2,256,1536]{2,1,0:T(8,128)}, u32[]{:S(2)}) copy-start(f32[2,256,1536]{2,1,0:T(8,128)} %refs_3_.7) | copy-start | bytes 9437188
  25.7 1.0 copy-start.7
  25.7 1.2 copy-start.8
  25.7 2.2 copy-start.13
  25.9 2.1 copy-start.11
  25.9 2.1 copy-start.12
  28.1 1.7 copy-start.9
  28.1 1.7 copy-start.10
  28.1 1.7 copy-start.14
  523.5 10.3 %copy-start = (bf16[1024,512]{1,0:T(8,128)(2,1)S(1)}, bf16[1024,512]{1,0:T(8,128)(2,1)}, u32[]{:S(2)}) copy-start(bf16[1024,512]{1,0:T(8,128)(2,1)} %get-tuple-element.113.refs_7_) | copy-start | bytes 3145732
  523.5 10.3 %copy-start.2 = (bf16[1024,256]{1,0:T(8,128)(2,1)S(1)}, bf16[1024,256]{1,0:T(8,128)(2,1)}, u32[]{:S(2)}) copy-start(bf16[1024,256]{1,0:T(8,128)(2,1)} %get-tuple-element.108.refs_1_.refs_5_) | copy-start | bytes 1572868
  533.8 1.2 copy-start.1
  535.0 1.0 copy-start.3
  666.8 22.4 %copy-start.16 = (f32[2,256]{1,0:T(2,128)}, f32[2,256]{1,0:T(2,128)S(1)}, u32[]{:S(2)}) copy-start(f32[2,256]{1,0:T(2,128)S(1)} %reshape.589) | copy-start | bytes 6148
  667.5 21.1 %copy-start.22 = (f32[2,16]{1,0:T(2,128)}, f32[2,16]{1,0:T(2,128)S(1)}, u32[]{:S(2)}) copy-start(f32[2,16]{1,0:T(2,128)S(1)} %reshape.590) | copy-start | bytes 388
  677.5 11.1 %copy-start.19 = (f32[2,16]{1,0:T(2,128)S(1)}, f32[2,16]{1,0:T(2,128)}, u32[]{:S(2)}) copy-start(f32[2,16]{1,0:T(2,128)} %param.37) | copy-start | bytes 388
  677.5 11.1 %copy-start.20 = (f32[2,16]{1,0:T(2,128)S(1)}, f32[2,16]{1,0:T(2,128)}, u32[]{:S(2)}) copy-start(f32[2,16]{1,0:T(2,128)} %param.45) | copy-start | bytes 388
  677.5 11.1 %copy-start.21 = (f32[2,16]{1,0:T(2,128)S(1)}, f32[2,16]{1,0:T(2,128)}, u32[]{:S(2)}) copy-start(f32[2,16]{1,0:T(2,128)} %param.53) | copy-start | bytes 388
  677.5 11.7 %copy-start.15 = (f32[2,256]{1,0:T(2,128)S(1)}, f32[2,256]{1,0:T(2,128)}, u32[]{:S(2)}) copy-start(f32[2,256]{1,0:T(2,128)} %param.36) | copy-start | bytes 6148
  677.5 11.7 %copy-start.17 = (f32[2,256]{1,0:T(2,128)S(1)}, f32[2,256]{1,0:T(2,128)}, u32[]{:S(2)}) copy-start(f32[2,256]{1,0:T(2,128)} %param.44) | copy-start | bytes 6148
  677.5 11.7 %copy-start.18 = (f32[2,256]{1,0:T(2,128)S(1)}, f32[2,256]{1,0:T(2,128)}, u32[]{:S(2)}) copy-start(f32[2,256]{1,0:T(2,128)} %param.52) | copy-start | bytes 6148
  677.6 12.3 %copy-start.6 = (f32[2,256,1536]{2,1,0:T(8,128)S(1)}, f32[2,256,1536]{2,1,0:T(8,128)}, u32[]{:S(2)}) copy-start(f32[2,256,1536]{2,1,0:T(8,128)} %get-tuple-element.121) | copy-start | bytes 9437188
Sparse Core Ops, SparseCore 0:
  471.7 145.5 reduce-scatter.1

commit v4 on v3

--- a/solution.py
+++ b/solution.py
@@ -432,7 +432,7 @@
     return lax.rsqrt(jnp.mean(values * values, axis=-1, keepdims=True) + EPSILON)
 
 
-def row_call(body, scalars, arrays, gains, outs, sums=0, cost=8):
+def row_call(body, scalars, arrays, gains, outs, sums=0, cost=8, matrix=None, columns=0, at=0):
     tokens, width = arrays[0].shape
     tiles = tokens // ROW_TILE
     row = pl.BlockSpec((ROW_TILE, width), lambda tile, *_: (tile, 0))
@@ -443,17 +443,24 @@
             num_scalar_prefetch=1,
             grid=(tiles,),
             in_specs=[row] * len(arrays)
-            + [whole] * len(gains),
+            + [whole] * len(gains)
+            + ([] if matrix is None else [pl.BlockSpec((width, columns), lambda *_: (0, at))]),
             out_specs=[row] * len(outs)
+            + (
+                []
+                if matrix is None
+                else [pl.BlockSpec((ROW_TILE, columns), lambda tile, *_: (tile, 0))]
+            )
             + [pl.BlockSpec((8, width), lambda tile, *_: (0, 0))] * sums,
         ),
         out_shape=[jax.ShapeDtypeStruct((tokens, width), kind) for kind in outs]
+        + ([] if matrix is None else [jax.ShapeDtypeStruct((tokens, columns), jnp.bfloat16)])
         + [jax.ShapeDtypeStruct((8, width), jnp.float32)] * sums,
         cost_estimate=pl.CostEstimate(
             flops=cost * tokens * width, bytes_accessed=3 * cost * tokens * width // 2, transcendentals=0
         ),
         name=body.__name__,
-    )(scalars, *arrays, *gains)
+    )(scalars, *arrays, *gains, *([] if matrix is None else [matrix]))
 
 
 def row_groups(ref, body):
@@ -497,19 +504,38 @@
 def layer_out(scalars, mid_ref, came_ref, out_ref):
     def body(rows):
         put_back(
-            scalars, out_ref, rows, mid_ref[rows, :] + came_ref[rows, :].astype(jnp.float32)
+            scalars,
+            out_ref,
+            rows,
+            mid_ref[rows, :].astype(jnp.float32) + came_ref[rows, :].astype(jnp.float32),
         )
 
     row_groups(mid_ref, body)
 
 
-def norm_grad(values, grad, gain, sum_ref):
-    scale = row_scale(values)
-    unit = values * scale
-    share = grad * unit
-    sum_ref[...] += jnp.sum(share.reshape(-1, 8, share.shape[1]), axis=0)
-    inner = grad * gain
-    return scale * (inner - unit * jnp.mean(inner * unit, axis=-1, keepdims=True))
+LANES = 128
+
+
+def norm_back(rows, values_ref, grad_ref, gain_ref, base_ref, sum_ref, put):
+    width = values_ref.shape[1]
+
+    def lanes(ref, start):
+        return ref[rows, start : start + LANES].astype(jnp.float32)
+
+    squares = products = 0.0
+    for start in range(0, width, LANES):
+        values = lanes(values_ref, start)
+        squares += values * values
+        products += lanes(grad_ref, start) * gain_ref[:, start : start + LANES] * values
+    mean = jnp.sum(squares, axis=-1, keepdims=True) * (1.0 / width)
+    scale = lax.rsqrt(mean + EPSILON)
+    slope = scale * scale * scale * (jnp.sum(products, axis=-1, keepdims=True) * (1.0 / width))
+    for start in range(0, width, LANES):
+        values, grad = lanes(values_ref, start), lanes(grad_ref, start)
+        share = grad * (values * scale)
+        sum_ref[:, start : start + LANES] += jnp.sum(share.reshape(-1, 8, LANES), axis=0)
+        inner = grad * gain_ref[:, start : start + LANES]
+        put(start, lanes(base_ref, start) + (scale * inner - slope * values))
 
 
 def clear_first(sum_ref):
@@ -518,31 +544,32 @@
         sum_ref[...] = jnp.zeros_like(sum_ref)
 
 
-def second_back(scalars, mid_ref, g_ref, came_ref, gain_ref, dx_ref, low_ref, sum_ref):
+def second_back(
+    scalars, mid_ref, g_ref, came_ref, gain_ref, whole, low_ref, out_ref, sum_ref
+):
     clear_first(sum_ref)
 
     def body(rows):
-        grad = came_ref[rows, :].astype(jnp.float32)
-        value = g_ref[rows, :].astype(jnp.float32) + norm_grad(
-            mid_ref[rows, :], grad, gain_ref[...], sum_ref
-        )
-        dx_ref[rows, :] = value
-        low_ref[rows, :] = value.astype(low_ref.dtype)
+        def put(start, value):
+            low_ref[rows, start : start + LANES] = value.astype(low_ref.dtype)
+
+        norm_back(rows, mid_ref, came_ref, gain_ref, g_ref, sum_ref, put)
 
     row_groups(mid_ref, body)
+    out_ref[...] = rows_times(low_ref[...], whole[...]).astype(out_ref.dtype)
 
 
 def first_back(scalars, dx_ref, x_ref, came_ref, gain_ref, out_ref, sum_ref):
     clear_first(sum_ref)
+    width = x_ref.shape[1] // count_of(scalars)
 
     def body(rows):
-        value = dx_ref[rows, :] + norm_grad(
-            x_ref[rows, :].astype(jnp.float32),
-            came_ref[rows, :].astype(jnp.float32),
-            gain_ref[...],
-            sum_ref,
-        )
-        put_back(scalars, out_ref, rows, value)
+        def put(start, value):
+            at, inside = start // width, start % width
+            target = pl.multiple_of(scalars[at] * width + inside, LANES)
+            out_ref[rows, pl.ds(target, LANES)] = value
+
+        norm_back(rows, x_ref, came_ref, gain_ref, dx_ref, sum_ref, put)
 
     row_groups(x_ref, body)
 
@@ -611,14 +638,6 @@
     return jnp.dot(left, right, preferred_element_type=jnp.float32)
 
 
-def project_body(cuts, lefts, whole, extras, outs):
-    start = 0
-    for out, stop in zip(outs, cuts):
-        out[...] = rows_times(lefts[0][...], whole[:, start:stop]).astype(out.dtype)
-        start = stop
-    return []
-
-
 def back_body(lefts, whole, extras, outs):
     start, value = 0, None
     for left in lefts:
@@ -653,7 +672,7 @@
 def adam_update(grads, places, states):
     parts = len(grads)
     rows, columns = grads[0].shape
-    tile = min(64, rows)
+    tile = min(128, rows)
 
     def window(array):
         lead = array.shape[:-2]
@@ -901,12 +920,13 @@
 
 
 def gather_body(shards, gain_cols, query_cols, key_cols, *refs):
-    (own_ref, small_ref, x_ref, g_ref, ff_ref, cosine_ref, sine_ref, first_ref) = refs[:8]
-    (out_ref, few_ref, early_ref, xr_ref, gr_ref, n_ref) = refs[8:14]
-    (query_raw, key_raw, query_ref, key_ref, value_ref, mixed_ref) = refs[14:20]
-    (kept_ref, sent_ref) = refs[20:22]
-    (few, gain, head_gain, whole) = refs[22:26]
-    (big_sent, big_came, ff_sent, ff_came, few_sent, few_came, local) = refs[26:]
+    (own_ref, small_ref, x_ref, g_ref, gate_up_ref, down_ref) = refs[:6]
+    (cosine_ref, sine_ref, first_ref) = refs[6:9]
+    (out_ref, few_ref, early_ref, ff_ref, xr_ref, gr_ref, n_ref) = refs[9:16]
+    (query_raw, key_raw, query_ref, key_ref, value_ref, mixed_ref) = refs[16:22]
+    (kept_ref, sent_ref) = refs[22:24]
+    (few, gain, head_gain, whole) = refs[24:28]
+    (big_sent, big_came, ff_sent, ff_came, few_sent, few_came, local) = refs[28:]
     hops = Hops(shards)
     place = place_of(lax.axis_index("fsdp"), shards)
     ahead = [{"fsdp": ring_place(place + at, shards)} for at in range(1, shards)]
@@ -960,11 +980,33 @@
             out_specs=[pl.BlockSpec((ROW_TILE, width), index)] * 3,
         )(x_ref, g_ref, xr_ref, gr_ref, n_ref)
 
+    def cast_part(part):
+        rows, columns = ff_ref.shape[1], ff_ref.shape[2] // 3
+        tile = rows // 2
+
+        def body(gate_up, down, out):
+            out[:, :columns] = gate_up[0].astype(out.dtype)
+            out[:, columns : 2 * columns] = gate_up[1].astype(out.dtype)
+            out[:, 2 * columns :] = down[...].astype(out.dtype)
+
+        pltpu.emit_pipeline(
+            body,
+            grid=(rows // tile,),
+            in_specs=[
+                pl.BlockSpec((2, tile, columns), lambda at: (0, at, part)),
+                pl.BlockSpec((tile, columns), lambda at: (at, part)),
+            ],
+            out_specs=[pl.BlockSpec((tile, 3 * columns), lambda at: (at, 0))],
+        )(gate_up_ref, down_ref, ff_ref.at[part])
+
     for part in range(legs):
+        if part < ff_ref.shape[0]:
+            cast_part(part)
+        if part == legs - 1:
+            early.hop(1)
         turned_part(part)
         if part + 2 <= legs:
             big.hop(part + 2)
-    early.hop(1)
     big.hop(legs + 1)
     loads = [
         pltpu.make_async_copy(
@@ -1046,12 +1088,35 @@
     put.wait()
 
 
-def gather_call(own, small, rows, grads, ff_block, cosine, sine, first, gain_cols, cuts):
+def cast_body(*refs):
+    start = 0
+    for ref in refs[:-1]:
+        stop = start + ref.shape[1]
+        refs[-1][:, start:stop] = ref[...].astype(refs[-1].dtype)
+        start = stop
+
+
+def side_by_side(arrays):
+    rows = arrays[0].shape[0]
+    columns = sum(array.shape[1] for array in arrays)
+    tile = rows // 2
+    return pl.pallas_call(
+        cast_body,
+        grid=(rows // tile,),
+        in_specs=[pl.BlockSpec((tile, array.shape[1]), lambda at: (at, 0)) for array in arrays],
+        out_specs=pl.BlockSpec((tile, columns), lambda at: (at, 0)),
+        out_shape=jax.ShapeDtypeStruct((rows, columns), jnp.bfloat16),
+        name="side_by_side",
+    )(*arrays)
+
+
+def gather_call(own, small, rows, grads, gate_up, down, cosine, sine, first, gain_cols, cuts):
     tokens, width = rows.shape
     shards = width // own.shape[0]
     legs = shards // 2
     query_cols, key_cols = cuts
     low = jnp.bfloat16
+    chunk = (down.shape[0], 3 * down.shape[1] // FF_CHUNKS)
     anywhere = pl.BlockSpec(memory_space=pl.ANY)
 
     def like(columns, kind=low, count=tokens):
@@ -1059,12 +1124,13 @@
 
     return pl.pallas_call(
         functools.partial(gather_body, shards, gain_cols, query_cols, key_cols),
-        in_specs=[anywhere] * 7 + [pl.BlockSpec(memory_space=pltpu.VMEM)],
-        out_specs=[anywhere] * 14,
+        in_specs=[anywhere] * 8 + [pl.BlockSpec(memory_space=pltpu.VMEM)],
+        out_specs=[anywhere] * 15,
         out_shape=[
             jax.ShapeDtypeStruct((shards, *shape), low)
-            for shape in (own.shape, small.shape, ff_block.shape[1:])
+            for shape in (own.shape, small.shape, chunk)
         ]
+        + [jax.ShapeDtypeStruct((FF_CHUNKS, *chunk), low)]
         + [like(width)] * 3
         + [like(query_cols, jnp.float32), like(key_cols, jnp.float32)]
         + [like(query_cols), like(key_cols), like(key_cols), like(query_cols)]
@@ -1085,7 +1151,7 @@
             collective_id=0, has_side_effects=True, vmem_limit_bytes=56 * 1024 * 1024
         ),
         name="gather_ring",
-    )(own, small, rows, grads, ff_block, cosine, sine, first)
+    )(own, small, rows, grads, gate_up, down, cosine, sine, first)
 
 
 FF_TILE = 256
@@ -1094,12 +1160,12 @@
 
 def ff_kernel(shards, parts, *refs):
     (sent_ref, kept_ref, x_ref, grad_ref, gain_ref, own_ref, early_ref) = refs[:7]
-    (mid_ref, normsum_ref, downsum_ref, grads_ref, late_ref, whole_ref) = refs[7:13]
-    (acts, whole, pairs, norm_acc, r_sent, r_came, total, late) = refs[13:21]
-    (out_half, kept_half, chip, first) = refs[21:25]
-    seconds = refs[25:27]
-    (x_tile, mid_tile) = refs[27:29]
-    (ag_sent, ag_came, rs_sent, rs_came, credits, sums, local) = refs[29:]
+    (mid_ref, normsum_ref, downkept_ref, downsent_ref, grads_ref, late_ref, whole_ref) = refs[7:14]
+    (acts, whole, pairs, norm_acc, r_sent, r_came, total, late) = refs[14:22]
+    (out_half, kept_half, chip, first) = refs[22:26]
+    seconds = refs[26:28]
+    (x_tile, mid_tile) = refs[28:30]
+    (ag_sent, ag_came, rs_sent, rs_came, credits, sums, local) = refs[30:]
     place = place_of(lax.axis_index("fsdp"), shards)
     hops = Hops(shards)
     hops.meet([*hops.neighbours, hops.partner, hops.across])
@@ -1157,9 +1223,9 @@
     attention.to_chip()
     gathers[0].hop(2)
     gathers[0].hop(3)
-    attention.to_all()
     gathers[0].hop(4)
     gathers[1].hop(1)
+    attention.to_all()
     attention.done()
 
     @pl.loop(0, tokens // FF_TILE)
@@ -1169,7 +1235,7 @@
         take.start()
         take.wait()
         middle = x_tile[...].astype(jnp.float32) + acts[0, rows, :].astype(jnp.float32)
-        mid_tile[...] = middle
+        mid_tile[...] = middle.astype(mid_tile.dtype)
         put = pltpu.make_async_copy(mid_tile, mid_ref.at[rows], local.at[2])
         put.start()
         acts[0, rows, :] = (middle * row_scale(middle) * gain_ref[...]).astype(jnp.bfloat16)
@@ -1303,12 +1369,6 @@
             copy.start()
         for copy in copies:
             copy.wait()
-    scatter.hop(1, 3)
-    scatter.prepare(1, 4)
-    leave(4)
-    norm_sum.to_all()
-    norm_sum.done()
-
     def down_tile(tile, offset):
         rows = pl.ds(pl.multiple_of(offset + tile * FF_TILE, FF_TILE), FF_TILE)
         value = contract_cols(pairs[2, rows, :], whole[:, :columns])
@@ -1316,31 +1376,37 @@
             value += contract_cols(
                 pairs[3 * part + 2, rows, :], whole[:, part * columns : (part + 1) * columns]
             )
-        return value
+        return value.astype(jnp.bfloat16)
+
+    scatter.hop(1, 3)
+    scatter.prepare(1, 4)
+    leave(4)
 
     @pl.loop(0, half // FF_TILE)
     def _(tile):
         rows = pl.ds(pl.multiple_of(tile * FF_TILE, FF_TILE), FF_TILE)
-        out_half[rows, :] = down_tile(tile, (1 - core) * half).astype(jnp.bfloat16)
-
-    down_sum = CoreSum(
-        hops, out_half, kept_half, first, chip, seconds[0], downsum_ref, sums.at[2]
-    )
-    down_sum.start()
+        kept_half[rows, :] = down_tile(tile, core * half)
+
+    put_kept = pltpu.make_async_copy(kept_half, downkept_ref, local.at[0])
+    put_kept.start()
+    scatter.hop(1, 4)
+    norm_sum.to_all()
+    own_block(1)
+    leave(5)
+    finish(1)
+    norm_sum.done()
 
     @pl.loop(0, half // FF_TILE)
     def _(tile):
         rows = pl.ds(pl.multiple_of(tile * FF_TILE, FF_TILE), FF_TILE)
-        kept_half[rows, :] = down_tile(tile, core * half).astype(jnp.bfloat16)
-
-    down_sum.to_chip()
-    scatter.hop(1, 4)
-    own_block(1)
-    for at in range(5, shards):
+        out_half[rows, :] = down_tile(tile, (1 - core) * half)
+
+    put_sent = pltpu.make_async_copy(out_half, downsent_ref, local.at[1])
+    put_sent.start()
+    for at in range(6, shards):
         leave(at)
-    finish(1)
-    down_sum.to_all()
-    down_sum.done()
+    put_kept.wait()
+    put_sent.wait()
     puts[parts - 2].wait()
     for copy in lates[-2:]:
         copy.wait()
@@ -1362,11 +1428,12 @@
     return pl.pallas_call(
         functools.partial(ff_kernel, shards, parts),
         in_specs=[anywhere] * 4 + [pl.BlockSpec(memory_space=pltpu.VMEM)] + [anywhere] * 2,
-        out_specs=[anywhere] * 6,
+        out_specs=[anywhere] * 7,
         out_shape=[
-            jax.ShapeDtypeStruct((tokens, wide), jnp.float32),
             jax.ShapeDtypeStruct((tokens, wide), low),
             jax.ShapeDtypeStruct((tokens, wide), low),
+            jax.ShapeDtypeStruct((half, wide), low),
+            jax.ShapeDtypeStruct((half, wide), low),
             jax.ShapeDtypeStruct((parts - 1, width, columns3), jnp.float32),
             jax.ShapeDtypeStruct((shards, width, columns3), low),
             jax.ShapeDtypeStruct((parts - 1, shards, width, columns3), low),
@@ -1384,13 +1451,13 @@
         + [pltpu.VMEM((half, wide), low)] * 6
         + [
             pltpu.VMEM((FF_TILE, wide), low),
-            pltpu.VMEM((FF_TILE, wide), jnp.float32),
+            pltpu.VMEM((FF_TILE, wide), low),
             pltpu.SemaphoreType.DMA((parts - 1, 2, legs, HALVES)),
             pltpu.SemaphoreType.DMA((parts - 1, 2, legs, HALVES)),
             pltpu.SemaphoreType.DMA((2, slots, HALVES)),
             pltpu.SemaphoreType.DMA((2, slots, HALVES)),
             pltpu.SemaphoreType.REGULAR((2, HALVES)),
-            pltpu.SemaphoreType.DMA((3, 2, 4)),
+            pltpu.SemaphoreType.DMA((2, 2, 4)),
             pltpu.SemaphoreType.DMA((5 + shards,)),
         ],
         compiler_params=pltpu.CompilerParams(
@@ -1401,11 +1468,12 @@
 
 
 def tail_kernel(shards, jobs, *refs):
-    (sent_ref, kept_ref, norm_ref, grad_ref) = refs[:4]
-    rights = refs[4:8]
-    (sum_ref, grads_ref, acts, r_sent, r_came, total) = refs[8:14]
-    (kept_half, chip, first, second) = refs[14:18]
-    (rs_sent, rs_came, credits, sums, local) = refs[18:]
+    (sent_ref, kept_ref, norm_ref, grad_ref, downsent_ref, downkept_ref) = refs[:6]
+    rights = refs[6:10]
+    (sum_ref, downsum_ref, grads_ref, acts, r_sent, r_came, total) = refs[10:17]
+    (kept_half, chip, first, second) = refs[17:21]
+    (down_half, down_chip, down_first, down_second) = refs[21:25]
+    (rs_sent, rs_came, credits, sums, local) = refs[25:]
     hops = Hops(shards)
     hops.meet([*hops.neighbours, hops.partner, hops.across])
     wide = norm_ref.shape[1]
@@ -1434,14 +1502,23 @@
     take = [
         pltpu.make_async_copy(ref, target, local.at[at])
         for at, (ref, target) in enumerate(
-            [(kept_ref, kept_half), (norm_ref, acts.at[0]), (grad_ref, acts.at[1])]
+            [
+                (kept_ref, kept_half),
+                (norm_ref, acts.at[0]),
+                (grad_ref, acts.at[1]),
+                (downkept_ref, down_half),
+            ]
         )
     ]
     norm_sum = CoreSum(
         hops, sent_ref, kept_half, first, chip, second, sum_ref, sums.at[0]
     )
     puts = [pltpu.make_async_copy(total, grads_ref.at[job], local.at[0]) for job in range(2)]
+    down_sum = CoreSum(
+        hops, downsent_ref, down_half, down_first, down_chip, down_second, downsum_ref, sums.at[1]
+    )
     norm_sum.start()
+    down_sum.start()
     for copy in take:
         copy.start()
     for copy in take:
@@ -1451,23 +1528,26 @@
     scatter.prepare(1, 1)
     scatter.hop(1, 1)
     norm_sum.to_chip()
+    down_sum.to_chip()
     for step in range(2, legs + 1):
         for job in range(2):
             scatter.prepare(job, step)
             scatter.hop(job, step)
+    norm_sum.to_all()
     for job in range(2):
         if job > 0:
             puts[job - 1].wait()
         partial(job, 0, total)
         scatter.last(job, total)
         puts[job].start()
-    norm_sum.to_all()
+    norm_sum.done()
+    down_sum.to_all()
+    down_sum.done()
     puts[1].wait()
-    norm_sum.done()
     scatter.close()
 
 
-def tail_call(sent, kept, norm, grad, rights, jobs, shards):
+def tail_call(sent, kept, norm, grad, down_sent, down_kept, rights, jobs, shards):
     tokens, wide = norm.shape
     half, width, legs = tokens // 2, wide // shards, shards // 2
     columns = sum(rights[right].shape[1] for _, right in jobs[0])
@@ -1476,9 +1556,10 @@
     slots = RingScatter.SLOTS
     return pl.pallas_call(
         functools.partial(tail_kernel, shards, jobs),
-        in_specs=[anywhere] * 4 + [pl.BlockSpec(memory_space=pltpu.VMEM)] * len(rights),
-        out_specs=[anywhere] * 2,
+        in_specs=[anywhere] * 6 + [pl.BlockSpec(memory_space=pltpu.VMEM)] * len(rights),
+        out_specs=[anywhere] * 3,
         out_shape=[
+            jax.ShapeDtypeStruct((tokens, wide), low),
             jax.ShapeDtypeStruct((tokens, wide), low),
             jax.ShapeDtypeStruct((len(jobs), width, columns), jnp.float32),
         ],
@@ -1488,19 +1569,19 @@
             pltpu.VMEM((2, slots, width, columns), low),
             pltpu.VMEM((width, columns), jnp.float32),
         ]
-        + [pltpu.VMEM((half, wide), low)] * 4
+        + [pltpu.VMEM((half, wide), low)] * 8
         + [
             pltpu.SemaphoreType.DMA((2, slots, HALVES)),
             pltpu.SemaphoreType.DMA((2, slots, HALVES)),
             pltpu.SemaphoreType.REGULAR((2, HALVES)),
-            pltpu.SemaphoreType.DMA((1, 2, 4)),
-            pltpu.SemaphoreType.DMA((3,)),
+            pltpu.SemaphoreType.DMA((2, 2, 4)),
+            pltpu.SemaphoreType.DMA((4,)),
         ],
         compiler_params=pltpu.CompilerParams(
             collective_id=2, has_side_effects=True, vmem_limit_bytes=48 * 1024 * 1024
         ),
         name="tail_ring",
-    )(sent, kept, norm, grad, *rights)
+    )(sent, kept, norm, grad, down_sent, down_kept, *rights)
 
 
 ATTENTION_ROWS = 256
@@ -1746,7 +1827,6 @@
     packed_token_count, width = layer_input.shape
     query_cols, key_cols = query_weight.shape[1], key_weight.shape[1]
     local_groups = key_cols // HEAD_SIZE
-    chunk_cols = down_weight.shape[1] // FF_CHUNKS
     states = [
         (query_weight, query_weight_mean, query_weight_square),
         (key_weight, key_weight_first_moment, key_weight_second_moment),
@@ -1758,34 +1838,11 @@
         (headnorm_gains, headnorm_gains_mean, headnorm_gains_square),
     ]
 
-    attention_block = jnp.concatenate(
-        [
-            query_weight.astype(low),
-            key_weight.astype(low),
-            value_matrix.astype(low),
-            output_weight.astype(low),
-        ],
-        axis=1,
-    )
+    attention_block = side_by_side([query_weight, key_weight, value_matrix, output_weight])
     own_gains = jnp.concatenate([norm_gains, headnorm_gains], axis=1).astype(low)
     own_gains = jnp.pad(own_gains, ((0, 14), (0, -own_gains.shape[1] % 128)))
     inward_window = (query_cols + 2 * key_cols, 0)
     outward_window = (query_cols, (query_cols + 2 * key_cols) // query_cols)
-    ff_block = jnp.stack(
-        [
-            jnp.concatenate(
-                [
-                    gate_up_weight[0, :, cols].astype(low),
-                    gate_up_weight[1, :, cols].astype(low),
-                    down_weight[:, cols].astype(low),
-                ],
-                axis=1,
-            )
-            for cols in (
-                slice(chunk * chunk_cols, (chunk + 1) * chunk_cols) for chunk in range(FF_CHUNKS)
-            )
-        ]
-    )
     token_positions = positions_of(segment_ids)
     first_key = (jnp.arange(packed_token_count, dtype=jnp.int32) - token_positions)[:, None]
     frequencies = ROPE_BASE ** (
@@ -1800,6 +1857,7 @@
         attention_full,
         gains,
         ff_early,
+        ff_block,
         input_rows,
         grad_low,
         normed_one,
@@ -1816,7 +1874,8 @@
         own_gains,
         layer_input,
         out_grad,
-        ff_block,
+        gate_up_weight,
+        down_weight,
         cosine,
         sine,
         first_key,
@@ -1827,27 +1886,20 @@
     gains = jnp.swapaxes(gains[:, :2].astype(jnp.float32), 0, 1)
     norm_gain = gains[:, :, :gain_cols].reshape(2, 1, -1)
     head_gain = gains[:, :, gain_cols : gain_cols + head_cols][:, back].reshape(2, -1)
-    middle, norm_sum, down_sum, ff_sums, ff_late, _ = ff_call(
+    middle, norm_sum, down_kept, down_sent, ff_sums, ff_late, _ = ff_call(
         sent, kept, input_rows, grad_low, norm_gain[1], ff_block, ff_early
     )
     ff_last = lax.psum_scatter(ff_late, "fsdp", scatter_dimension=0, tiled=False)
-    middle_grad, middle_grad_low, gain_two_grad = row_call(
+    middle_grad_low, mixed_grad, gain_two_grad = row_call(
         second_back,
         scalars,
         [middle, grad_low, norm_sum],
         [norm_gain[1]],
-        [jnp.float32, low],
+        [low],
         sums=1,
-    )
-    (mixed_grad,) = full_call(
-        functools.partial(project_body, (query_cols,)),
-        scalars,
-        [middle_grad_low],
-        attention_full,
-        outward_window,
-        [(query_cols, low)],
-        [],
-        "mixed_back",
+        matrix=attention_full,
+        columns=outward_window[0],
+        at=outward_window[1],
     )
     query_proj_low, key_proj_low, value_grad_low, head_sums = by_group(
         attention_back_body,
@@ -1873,11 +1925,13 @@
         [(width, low)],
         "projection_back",
     )
-    norm_one_sum, attention_sums = tail_call(
+    norm_one_sum, down_sum, attention_sums = tail_call(
         sent,
         kept,
         normed_one,
         middle_grad_low,
+        down_sent,
+        down_kept,
         [query_proj_low, key_proj_low, value_grad_low, mixed],
         (((0, 0), (0, 1)), ((0, 2), (1, 3))),
         shards,
@@ -1886,7 +1940,7 @@
     input_grad, gain_one_grad = row_call(
         first_back,
         scalars,
-        [middle_grad, input_rows, norm_one_sum],
+        [middle_grad_low, input_rows, norm_one_sum],
         [norm_gain[0]],
         [jnp.float32],
         sums=1,

time: 725 us -> 669 us (0.923)
  Pallas kernels: 663 us -> 627 us
  other arithmetic: 22.6 us -> 11.3 us
    pallas_call x1, Pallas kernels: 298 us -> 269 us  [ff_call(): pl.pallas_call(functools.partial(ff_kernel, shards, parts), in_specs=[any...]
    pallas_call x2 -> x1, Pallas kernels: 17.2 us -> 10.5 us  [full_call(): pl.pallas_call(kernel, grid_spec=pltpu.PrefetchScalarGridSpec(num_scalar_...]
where the time goes in v4:
time: 669 us; the launch traced here: 665 us
  Pallas kernels  627 us (94%)
  between operations  15 us (2%)
  local copies, waits for them, and re-layouts  11.6 us (2%)
  other arithmetic  11.3 us (2%)
    pallas_call x1, Pallas kernels, ff_call(): pl.pallas_call(functools.partial(ff_kernel, shards, parts), in_specs=[any...  269 us
    pallas_call x1, Pallas kernels, gather_call(): pl.pallas_call(functools.partial(gather_body, shards, gain_cols, query_co...  143 us
    pallas_call x1, Pallas kernels, tail_call(): pl.pallas_call(functools.partial(tail_kernel, shards, jobs), in_specs=[an...  105 us
    pallas_call x3, Pallas kernels, row_call(): pl.pallas_call(body, grid_spec=pltpu.PrefetchScalarGridSpec(num_scalar_pr...  42 us
    pallas_call x3, Pallas kernels, adam_update(): pl.pallas_call(functools.partial(adam_body, places, parts), grid=(parts,...  22.3 us
    pallas_call x1, Pallas kernels, by_group(): pl.pallas_call(body, grid=(groups,), in_specs=[columns(array.shape[1]) fo...  20.8 us
  transfers between devices with their start and end apart: 1, of which 0 were waited for; matrix products, arithmetic and copies ran while one was open for 2% of the time, Pallas kernels for 29%

profile of v4, /device:TPU:0, one launch (start us, length us, event | category | flops | bytes accessed | tf_op | source)
XLA Modules:
  0.0 664.8 jit_solution(2139757325608928523)
XLA Ops:
  7.2 0.0 reduce-scatter.2.cloned.1.call-start
  7.3 0.7 convert.8
  8.0 0.7 convert.7
  8.6 1.3 convert_reduce_fusion
  10.0 0.2 copy.81
  10.2 0.9 subtract_subtract_fusion.refs_8_.first_ref
  11.1 1.9 fusion
  13.0 0.2 copy.80
  13.2 1.0 copy.82.refs_6_.cosine_ref
  14.2 0.6 fusion.7.refs_1_
  14.8 1.0 pad_maximum_fusion.refs_7_.sine_ref
  15.8 2.6 side_by_side.1.refs_0_
  18.4 143.3 %gather_ring.1 = (bf16[8,256,1536]{2,1,0:T(8,128)(2,1)}, bf16[8,16,384]{2,1,0:T(8,128)(2,1)}, bf16[8,256,1536]{2,1,0:T(8,128)(2,1)}, bf16[3,256,1536]{2,1,0:T(8,...) custom-call(bf16[256,1536]{1,0:T(8,128)(2,1)} %side_by_side.1.refs_0, ...), custom_call_target="tpu_custom_call" | custom-call | tf_op jit(solution)/shard_map/gather_ring/pallas_call | solution.py:1125
  161.7 0.8 convert_bitcast_fusion
  162.5 0.6 fusion.17
  163.2 269.2 %ff_ring.1 = (bf16[1024,2048]{1,0:T(8,128)(2,1)}, bf16[1024,2048]{1,0:T(8,128)(2,1)}, bf16[512,2048]{1,0:T(8,128)(2,1)}, bf16[512,2048]{1,0:T(8,128)(2,1)}, f32[...) custom-call(bf16[512,2048]{1,0:T(8,128)(2,1)} %get-tuple-element.93.refs_0_, ...), custom_call_target="tpu_custom_call" | custom-call | tf_op jit(solution)/shard_map/ff_ring/pallas_call | solution.py:1428
  432.4 0.0 reduce-scatter.2.cloned.1.call-update
  432.9 0.6 gather_fusion
  433.5 0.6 reshape.578.gain_ref
  434.2 0.6 concatenate.33.scalars
  434.8 17.0 %second_back.1 = (bf16[1024,2048]{1,0:T(8,128)(2,1)}, bf16[1024,512]{1,0:T(8,128)(2,1)}, f32[8,2048]{1,0:T(8,128)}) custom-call(s32[9]{0:T(128)} %concatenate.33.scalars, bf16[1024,2048]{1,0:T(8,128)(2,1)} %get-tuple-element.100.mid_ref, bf16[1024,2048]{1,0:T(8,128)(2,1)} %get-tuple-element.96.refs_3_.g_ref, bf16[1024,2048]{1,0:T(8,128)(2,1)} %get-tuple-element.104.came_ref, ...), custom_call_target="tpu_custom_call" | custom-call | flops 16777216 | bytes 25165824 | tf_op jit(solution)/shard_map/second_back/pallas_call | solution.py:440
  451.8 20.8 %attention_back.1 = (bf16[1024,512]{1,0:T(8,128)(2,1)}, bf16[1024,256]{1,0:T(8,128)(2,1)}, bf16[1024,256]{1,0:T(8,128)(2,1)}, f32[2,2,128]{2,1,0:T(2,128)}) custom-call(bf16[1024,512]{1,0:T(8,128)(2,1)} %get-tuple-element.101.query_ref, bf16[1024,256]{1,0:T(8,128)(2,1)} %get-tuple-element.102.key_ref, bf16[1024,256]{1,0:T(8,128)(2,1)} %get-tuple-element.103.value_ref, ...), custom_call_target="tpu_custom_call" | custom-call | flops 2147483648 | bytes 4194304 | tf_op jit(solution)/shard_map/attention_back/pallas_call | solution.py:1715
  472.6 0.7 reduce_sum.42
  473.3 0.1 reshape.581
  473.4 0.1 stack.59
  473.5 0.6 gather_fusion.1
  474.1 0.1 reshape.582
  474.2 10.5 %projection_back.1 = (bf16[512,2048]{1,0:T(8,128)(2,1)}, bf16[512,2048]{1,0:T(8,128)(2,1)}) custom-call(s32[9]{0:T(128)} %concatenate.33.scalars, bf16[1024,512]{1,0:T(8,128)(2,1)} %get-tuple-element.109.refs_0_.refs_6_, bf16[1024,256]{1,0:T(8,128)(2,1)} %get-tuple-element.110.refs_1_.refs_7_, bf16[1024,256]{1,0:T(8,128)(2,1)} %get-tuple-element.111.refs_2_.refs_8_, ...), custom_call_target="tpu_custom_call" | custom-call | flops 4294967296 | bytes 17179868 | tf_op jit(solution)/shard_map/projection_back/pallas_call | solution.py:616
  484.7 1.2 copy-done.1
  486.0 1.0 copy-done.3
  487.0 105.2 %tail_ring.1 = (bf16[1024,2048]{1,0:T(8,128)(2,1)}, bf16[1024,2048]{1,0:T(8,128)(2,1)}, f32[2,256,768]{2,1,0:T(8,128)S(1)}) custom-call(bf16[512,2048]{1,0:T(8,128)(2,1)} %get-tuple-element.112.refs_0_, bf16[512,2048]{1,0:T(8,128)(2,1)} %get-tuple-element.113.refs_1_, bf16[1024,2048]{1,0:T(8,128)(2,1)} %get-tuple-element.114.refs_2_, ...), custom_call_target="tpu_custom_call" | custom-call | tf_op jit(solution)/shard_map/tail_ring/pallas_call | solution.py:1557
  592.3 0.0 copy-start.5
  592.3 14.8 %first_back.1 = (f32[1024,2048]{1,0:T(8,128)}, f32[8,2048]{1,0:T(8,128)}) custom-call(s32[9]{0:T(128)} %concatenate.33.scalars, bf16[1024,2048]{1,0:T(8,128)(2,1)} %get-tuple-element.115.refs_3_.dx_ref, bf16[1024,2048]{1,0:T(8,128)(2,1)} %get-tuple-element.95.refs_2_.x_ref, bf16[1024,2048]{1,0:T(8,128)(2,1)} %get-tuple-element.120.came_ref, f32[1,2048]{1,0:T(1,128)} %bitcast.50), custom_call_target="tpu_custom_call" | custom-call | flops 16777216 | bytes 25165824 | tf_op jit(solution)/shard_map/first_back/pallas_call | solution.py:440
  607.1 0.9 reduce_sum.40
  608.0 0.6 fusion.4.pieces
  608.6 10.8 %gain_sums.1 = f32[1,640]{1,0:T(1,128)} custom-call(f32[8,1,640]{2,1,0:T(1,128)} %fusion.4.pieces), custom_call_target="tpu_custom_call" | custom-call | tf_op jit(solution)/shard_map/gain_sums/pallas_call | solution.py:1772
  619.4 0.7 slice_reduce_fusion
  620.2 0.6 slice_reduce_fusion.1
  620.8 0.1 reshape.584
  620.9 1.2 slice_bitcast_fusion.2
  622.1 3.4 adam_update.4
  625.5 3.3 adam_update.3
  628.8 0.0 copy-start.10
  628.9 10.2 %layer_out.1 = f32[1024,2048]{1,0:T(8,128)} custom-call(s32[9]{0:T(128)} %concatenate.33.scalars, bf16[1024,2048]{1,0:T(8,128)(2,1)} %get-tuple-element.100.mid_ref, bf16[1024,2048]{1,0:T(8,128)(2,1)} %get-tuple-element.119.came_ref), custom_call_target="tpu_custom_call" | custom-call | flops 16777216 | bytes 25165824 | tf_op jit(solution)/shard_map/layer_out/pallas_call | solution.py:440
  639.1 0.6 subtract_subtract_fusion.2
  639.7 0.6 subtract_subtract_fusion.1
  640.3 1.8 slice_bitcast_fusion
  642.2 15.6 %adam_update.5 = (f32[2,256,1536]{2,1,0:T(8,128)}, f32[2,256,1536]{2,1,0:T(8,128)}, f32[2,256,1536]{2,1,0:T(8,128)}, f32[2,256,1536]{2,1,0:T(8,128)}, f32[256,15...) custom-call(f32[256,1536]{1,0:T(8,128)} %get-tuple-element.159.refs_0_, ...), custom_call_target="tpu_custom_call" | custom-call | flops 23592960 | bytes 37748736 | tf_op jit(solution)/shard_map/adam_update/pallas_call | solution.py:687
  (37 shorter events, 0.2 us)
Async XLA Ops:
  7.2 635.0 %reduce-scatter.2.cloned.1.call-start = ((), (), s32[]{:S(2)}) async-start(), calls=%async_computation.1 | async-start | bytes 7077888 | tf_op jit(solution)/shard_map/reduce_scatter | solution.py:1892
  474.2 10.5 %copy-start = (bf16[1024,512]{1,0:T(8,128)(2,1)S(1)}, bf16[1024,512]{1,0:T(8,128)(2,1)}, u32[]{:S(2)}) copy-start(bf16[1024,512]{1,0:T(8,128)(2,1)} %get-tuple-element.118.refs_9_) | copy-start | bytes 3145732
  474.2 10.5 %copy-start.2 = (bf16[1024,256]{1,0:T(8,128)(2,1)S(1)}, bf16[1024,256]{1,0:T(8,128)(2,1)}, u32[]{:S(2)}) copy-start(bf16[1024,256]{1,0:T(8,128)(2,1)} %get-tuple-element.110.refs_1_.refs_7_) | copy-start | bytes 1572868
  484.7 1.2 copy-start.1
  486.0 1.0 copy-start.3
  592.3 15.7 %copy-start.5 = (f32[8,2048]{1,0:T(8,128)S(1)}, f32[8,2048]{1,0:T(8,128)}, u32[]{:S(2)}) copy-start(f32[8,2048]{1,0:T(8,128)} %get-tuple-element.132) | copy-start | bytes 196612
  620.2 19.5 %copy-start.7 = (f32[2,256]{1,0:T(2,128)}, f32[2,256]{1,0:T(2,128)S(1)}, u32[]{:S(2)}) copy-start(f32[2,256]{1,0:T(2,128)S(1)} %reshape.583) | copy-start | bytes 6148
  620.9 18.2 %copy-start.13 = (f32[2,16]{1,0:T(2,128)}, f32[2,16]{1,0:T(2,128)S(1)}, u32[]{:S(2)}) copy-start(f32[2,16]{1,0:T(2,128)S(1)} %reshape.584) | copy-start | bytes 388
  628.8 10.3 %copy-start.10 = (f32[2,16]{1,0:T(2,128)S(1)}, f32[2,16]{1,0:T(2,128)}, u32[]{:S(2)}) copy-start(f32[2,16]{1,0:T(2,128)} %param.37) | copy-start | bytes 388
  628.9 10.2 %copy-start.11 = (f32[2,16]{1,0:T(2,128)S(1)}, f32[2,16]{1,0:T(2,128)}, u32[]{:S(2)}) copy-start(f32[2,16]{1,0:T(2,128)} %param.45) | copy-start | bytes 388
  628.9 10.2 %copy-start.12 = (f32[2,16]{1,0:T(2,128)S(1)}, f32[2,16]{1,0:T(2,128)}, u32[]{:S(2)}) copy-start(f32[2,16]{1,0:T(2,128)} %param.53) | copy-start | bytes 388
  628.9 10.8 %copy-start.6 = (f32[2,256]{1,0:T(2,128)S(1)}, f32[2,256]{1,0:T(2,128)}, u32[]{:S(2)}) copy-start(f32[2,256]{1,0:T(2,128)} %param.36) | copy-start | bytes 6148
  628.9 10.8 %copy-start.8 = (f32[2,256]{1,0:T(2,128)S(1)}, f32[2,256]{1,0:T(2,128)}, u32[]{:S(2)}) copy-start(f32[2,256]{1,0:T(2,128)} %param.44) | copy-start | bytes 6148
  628.9 10.8 %copy-start.9 = (f32[2,256]{1,0:T(2,128)S(1)}, f32[2,256]{1,0:T(2,128)}, u32[]{:S(2)}) copy-start(f32[2,256]{1,0:T(2,128)} %param.52) | copy-start | bytes 6148
  628.9 11.4 %copy-start.4 = (f32[2,256,1536]{2,1,0:T(8,128)S(1)}, f32[2,256,1536]{2,1,0:T(8,128)}, u32[]{:S(2)}) copy-start(f32[2,256,1536]{2,1,0:T(8,128)} %get-tuple-element.127) | copy-start | bytes 9437188
Sparse Core Ops, SparseCore 0:
  432.5 146.8 reduce-scatter.1
